TPU v7x, 32 devices: a whole 2x2x4 slice. The times are simulated.
32 devices in a mesh: crops: 1, rows: 16 (over z, y, core), cols: 2 (over x).
Axes of the slice: x: 2, y: 2, z: 4, core: 2. Of those that a mesh axis runs over, the one named last changes fastest.
Arguments:
- family_representation: float32 [128, 256, 256], P(('crops', 'rows'), 'cols'), may hold values from -6 to 6
- family_keep_flags: int32 [128, 256], P(('crops', 'rows'), 'cols'), may hold values 0 or 1
- amino_presence: int32 [256], P('crops'), may hold values 0 or 1
- contact_embedding: float32 [256, 256, 128], P(('crops', 'rows'), 'cols'), may hold values from -6 to 6
- couple_lhs_weights: bfloat16 [256, 32], replicated, may hold values from -0.375 to 0.375
- couple_rhs_weights: bfloat16 [256, 32], replicated, may hold values from -0.375 to 0.375
- pairwise_final_matrix: bfloat16 [1024, 128], replicated, may hold values from -1.5 to 1.5
- edge_source_matrix: bfloat16 [128, 256], replicated, may hold values from -0.5 to 0.5
- edge_target_matrix: bfloat16 [128, 256], replicated, may hold values from -0.5 to 0.5
- edge_final_sigmoid_matrix: bfloat16 [128, 128], replicated, may hold values from -0.5 to 0.5
- edge_final_matrix: bfloat16 [128, 128], replicated, may hold values from -0.5 to 0.5
- feedforward_expand_matrix: bfloat16 [128, 512], replicated, may hold values from -0.5 to 0.5
- feedforward_shrink_matrix: bfloat16 [512, 128], replicated, may hold values from -0.25 to 0.25
Outputs:
- pair_out: float32 [256, 256, 128], P(('crops', 'rows'), 'cols')
All inputs are finite; a program needn't handle non-finite values. No bound on the sum of `family_keep_flags` on one device may be relied on, other than what follows from the above.
Results may differ from a plain program's by a relative error of at most 0.0053.
Values may be sent and summed in bfloat16 or wider, within the bound.
No kernel may reach another device: no remote copies, remote signals or barrier semaphores. Data moves between devices by JAX's collectives and lax.ppermute only.
A program may use at most 64 MiB of HBM per device.

v0:
```python
import jax
import jax.numpy as jnp
from jax import lax
from jax.sharding import PartitionSpec as P

epsilon = 1e-05


def normalise_features_step(values, reduce_axis):
    mean = jnp.mean(values, axis=reduce_axis, keepdims=True)
    centred = values - mean
    spread = jnp.mean(centred * centred, axis=reduce_axis, keepdims=True)
    return centred * lax.rsqrt(spread + epsilon)


def make_panel(normed_pair, weight, pair_live):
    raw = jnp.einsum("ijz,zc->cij", normed_pair, weight, preferred_element_type=jnp.float32)
    channels = raw.shape[0] // 2
    return (raw[:channels] * jax.nn.sigmoid(raw[channels:]) * pair_live[None]).astype(jnp.bfloat16)


def on_device(
    family_representation,
    family_keep_flags,
    amino_presence,
    contact_embedding,
    couple_lhs_weights,
    couple_rhs_weights,
    pairwise_final_matrix,
    edge_source_matrix,
    edge_target_matrix,
    edge_final_sigmoid_matrix,
    edge_final_matrix,
    feedforward_expand_matrix,
    feedforward_shrink_matrix,
):
    tile_rows = contact_embedding.shape[0]
    tile_cols = contact_embedding.shape[1]
    rows_count = lax.axis_size("rows")
    cols_count = lax.axis_size("cols")
    row_start = lax.axis_index("rows") * tile_rows
    col_start = lax.axis_index("cols") * tile_cols
    residue_float_mask = amino_presence.astype(jnp.float32)
    rows_live = lax.dynamic_slice_in_dim(residue_float_mask, row_start, tile_rows, 0)
    active_columns = lax.dynamic_slice_in_dim(residue_float_mask, col_start, tile_cols, 0)
    retained_family_entries = family_keep_flags.astype(jnp.float32) * active_columns[None, :]
    rescaled_family_rep = normalise_features_step(family_representation, -1).astype(jnp.bfloat16)
    family_lhs_mapped = (
        jnp.einsum(
            "ohp,pd->ohd",
            rescaled_family_rep,
            couple_lhs_weights,
            preferred_element_type=jnp.float32,
        )
        * retained_family_entries[:, :, None]
    ).astype(jnp.bfloat16)
    family_rhs_mapped = (
        jnp.einsum(
            "ohp,pd->ohd",
            rescaled_family_rep,
            couple_rhs_weights,
            preferred_element_type=jnp.float32,
        )
        * retained_family_entries[:, :, None]
    ).astype(jnp.bfloat16)
    live_half = retained_family_entries.astype(jnp.bfloat16)
    right_all, right_live = (
        lax.all_gather(family_rhs_mapped, "rows", axis=0, tiled=True),
        lax.all_gather(live_half, "rows", axis=0, tiled=True),
    )
    left_wide, wide_live = (
        lax.all_gather(family_lhs_mapped, "cols", axis=1, tiled=True),
        lax.all_gather(live_half, "cols", axis=1, tiled=True),
    )
    left_all, left_live = (
        lax.all_to_all(left_wide, "rows", split_axis=1, concat_axis=0, tiled=True),
        lax.all_to_all(wide_live, "rows", split_axis=1, concat_axis=0, tiled=True),
    )
    family_tally = left_all.shape[0]
    intermediate_breadth = left_all.shape[2]
    portion_number = min(8, tile_rows)
    count_blocks = tile_rows // portion_number
    port_portion_group = left_all.reshape(
        family_tally, count_blocks, portion_number, intermediate_breadth
    ).transpose(1, 0, 2, 3)
    live_blocks = left_live.reshape(family_tally, count_blocks, portion_number).transpose(1, 0, 2)

    def outer_block(item):
        port_segments, lives = item
        averaged_tensor_contraction = jnp.einsum(
            "lyj,lnx->ynjx", port_segments, right_all, preferred_element_type=jnp.float32
        )
        counts = jnp.einsum("si,sj->ij", lives, right_live, preferred_element_type=jnp.float32)
        mean = (averaged_tensor_contraction / jnp.maximum(counts, 1.0)[:, :, None, None]).astype(
            jnp.bfloat16
        )
        flat = mean.reshape(portion_number * tile_cols, intermediate_breadth * intermediate_breadth)
        return jnp.dot(flat, pairwise_final_matrix, preferred_element_type=jnp.float32).reshape(
            portion_number, tile_cols, -1
        )

    update = lax.map(outer_block, (port_portion_group, live_blocks))
    first = contact_embedding + update.reshape(tile_rows, tile_cols, -1)
    pair_normed = normalise_features_step(first, -1).astype(jnp.bfloat16)
    pair_live = rows_live[:, None] * active_columns[None, :]
    left_panel = make_panel(pair_normed, edge_source_matrix, pair_live)
    right_panel = make_panel(pair_normed, edge_target_matrix, pair_live)
    gate = jax.nn.sigmoid(
        jnp.dot(pair_normed, edge_final_sigmoid_matrix, preferred_element_type=jnp.float32)
    )
    left_recv, right_recv = (
        lax.all_to_all(left_panel, ("rows", "cols"), split_axis=0, concat_axis=1, tiled=True),
        lax.all_to_all(right_panel, ("rows", "cols"), split_axis=0, concat_axis=1, tiled=True),
    )
    owned = left_recv.shape[0]
    left_full = (
        left_recv.reshape(owned, rows_count, cols_count, tile_rows, tile_cols)
        .transpose(0, 1, 3, 2, 4)
        .reshape(owned, rows_count * tile_rows, cols_count * tile_cols)
    )
    right_full = (
        right_recv.reshape(owned, rows_count, cols_count, tile_rows, tile_cols)
        .transpose(0, 1, 3, 2, 4)
        .reshape(owned, rows_count * tile_rows, cols_count * tile_cols)
    )
    product = jnp.einsum(
        "cik,cjk->cij", left_full, right_full, preferred_element_type=jnp.float32
    ).astype(jnp.bfloat16)
    owned = product.shape[0]
    regrouped = (
        product.reshape(owned, rows_count, tile_rows, cols_count, tile_cols)
        .transpose(0, 1, 3, 2, 4)
        .reshape(owned, rows_count * cols_count * tile_rows, tile_cols)
    )
    returned = lax.all_to_all(regrouped, ("rows", "cols"), split_axis=1, concat_axis=0, tiled=True)
    mixed = normalise_features_step(returned.astype(jnp.float32), 0).astype(jnp.bfloat16)
    projected = jnp.einsum(
        "cij,cz->ijz", mixed, edge_final_matrix, preferred_element_type=jnp.float32
    )
    second = first + gate * projected
    trans_normed = normalise_features_step(second, -1).astype(jnp.bfloat16)
    hidden = jax.nn.relu(
        jnp.dot(trans_normed, feedforward_expand_matrix, preferred_element_type=jnp.float32)
    ).astype(jnp.bfloat16)
    return second + jnp.dot(hidden, feedforward_shrink_matrix, preferred_element_type=jnp.float32)


def solution(mesh):
    in_specs = (
        P(("crops", "rows"), "cols", None),
        P(("crops", "rows"), "cols"),
        P("crops"),
        P(("crops", "rows"), "cols", None),
        P(),
        P(),
        P(),
        P(),
        P(),
        P(),
        P(),
        P(),
        P(),
    )
    out_specs = P(("crops", "rows"), "cols", None)
    return jax.shard_map(
        on_device, mesh=mesh, in_specs=in_specs, out_specs=out_specs, check_vma=False
    )
```

profile of v0, /device:TPU:1, one launch (start us, length us, event | category | flops | bytes accessed | tf_op | source)
XLA Modules:
  0.0 145.9 jit_solution(2600993245930080658)
XLA Ops:
  6.6 0.8 convert_element_type.65
  7.4 1.4 reduce_sum.72
  8.8 1.6 %multiply_reduce_fusion.3 = f32[8,128]{1,0:T(8,128)S(1)} fusion(f32[8,128,256]{2,1,0:T(8,128)} %param.15, f32[8,128]{1,0:T(8,128)S(1)} %broadcast_multiply_fusion.4), kind=kLoop, calls=%fused_computation.52 | loop fusion | flops 785408 | bytes 1056768 | tf_op jit(solution)/shard_map/reduce_sum | solution.py:12
  10.5 1.1 fusion.18
  11.6 3.8 %all_gather.14 = bf16[8,256]{1,0:T(8,128)(2,1)S(1)} all-gather(bf16[8,128]{1,0:T(8,128)(2,1)S(1)} %get-tuple-element.94), channel_id=1, replica_groups=mesh['crops'=1,'rows'=16,'cols'=2] {'cols'}, dimensions={1}, use_global_device_ids=true | all-gather | bytes 6144 | tf_op jit(solution)/shard_map/all_gather | solution.py:73
  15.4 0.1 all_to_all.55
  15.5 0.6 copy.105
  16.1 7.9 %all-to-all-start.1 = ((bf16[8,16,16]{2,0,1:T(8,128)(2,1)}), bf16[8,16,16]{2,0,1:T(8,128)(2,1)S(1)}, u32[]{:S(2)}, u32[]{:S(2)}) async-start(bf16[8,16,16]{2,0,1:T(8,128)(2,1)} %copy.105), calls=%async_computation.1 | async-start | bytes 65536 | tf_op jit(solution)/shard_map/all_to_all | solution.py:77
  24.1 0.5 fusion.17
  24.6 4.3 %all_gather.12 = bf16[8,256,32]{1,2,0:T(8,128)(2,1)S(1)} all-gather(bf16[8,128,32]{1,2,0:T(8,128)(2,1)S(1)} %fusion.17), channel_id=1, replica_groups=mesh['crops'=1,'rows'=16,'cols'=2] {'cols'}, dimensions={1}, use_global_device_ids=true | all-gather | bytes 196608 | tf_op jit(solution)/shard_map/all_gather | solution.py:72
  28.8 0.3 copy.102
  29.1 1.2 reshape.150
  30.3 6.7 %all-to-all-start = ((bf16[16,2,2048]{2,1,0:T(2,128)(2,1)}), bf16[16,2,2048]{2,1,0:T(2,128)(2,1)S(1)}, u32[]{:S(2)}, u32[]{:S(2)}) async-start(bf16[16,2,2048]{2,1,0:T(2,128)(2,1)} %reshape.150), calls=%async_computation | async-start | bytes 262144 | tf_op jit(solution)/shard_map/all_to_all | solution.py:76
  37.1 0.3 copy.110
  37.5 21.7 %all_gather.15 = bf16[128,128]{1,0:T(8,128)(2,1)S(1)} all-gather(bf16[8,128]{1,0:T(8,128)(2,1)S(1)} %get-tuple-element.94), channel_id=1, replica_groups=mesh['crops'=1,'rows'=16,'cols'=2] {'rows'}, dimensions={0}, use_global_device_ids=true | all-gather | bytes 34816 | tf_op jit(solution)/shard_map/all_gather | solution.py:69
  59.5 0.3 reshape.151
  59.7 0.1 copy.104
  59.9 0.4 copy.107
  60.3 2.6 %copy.108 = bf16[128,128,32]{1,0,2:T(8,128)(2,1)} copy(bf16[128,128,32]{1,2,0:T(8,128)(2,1)} %all-gather.2.cloned.1.call-done) | data formatting | bytes 2097152 | tf_op jit(solution)/shard_map/while | solution.py:102
  62.9 9.5 %while.10 = (s32[]{:T(128)}, f32[2,8,128,128]{2,3,1,0:T(8,128)}, bf16[2,128,8,32]{1,3,2,0:T(8,128)(2,1)S(1)}, bf16[128,128,32]{1,0,2:T(8,128)(2,1)}, bf16[2,128,...) while((s32[]{:T(128)}, f32[2,8,128,128]{2,3,1,0:T(8,128)}, ...), condition=%wide.region_3.4_spmd, body=%wide.region_2.3_spmd.sunk | while | flops 539231232 | bytes 18720920 | solution.py:102
  62.9 0.1 convolution_maximum_fusion.2
  63.1 1.9 %fusion.72 = bf16[8,128,32,32]{1,2,3,0:T(8,128)(2,1)S(1)} fusion(f32[8,128]{1,0:T(8,128)S(1)} %convolution_maximum_fusion.2, bf16[128,128,32]{1,0,2:T(8,128)(2,1)} %get-tuple-element.165, bf16[2,128,8,32]{1,3,2,0:T(8,128)(2,1)S(1)} %get-tuple-element.164, s32[]{:T(128)} %get-tuple-element.154), kind=kOutput, calls=%fused_computation.1.clone.1 | convolution fusion | flops 270532608 | bytes 3215364 | tf_op jit(solution)/shard_map/while/body/eval_jaxpr/lyj,lnx->ynjx/dot_general | solution.py:90
  65.0 0.8 copy.160
  65.8 0.4 copy-done.3
  66.2 0.5 fusion.73
  66.7 1.0 copy-done.4
  67.7 0.1 convolution_maximum_fusion.2
  67.8 1.9 %fusion.72 = bf16[8,128,32,32]{1,2,3,0:T(8,128)(2,1)S(1)} fusion(f32[8,128]{1,0:T(8,128)S(1)} %convolution_maximum_fusion.2, bf16[128,128,32]{1,0,2:T(8,128)(2,1)} %get-tuple-element.165, bf16[2,128,8,32]{1,3,2,0:T(8,128)(2,1)S(1)} %get-tuple-element.164, s32[]{:T(128)} %get-tuple-element.154), kind=kOutput, calls=%fused_computation.1.clone.1 | convolution fusion | flops 270532608 | bytes 3215364 | tf_op jit(solution)/shard_map/while/body/eval_jaxpr/lyj,lnx->ynjx/dot_general | solution.py:90
  69.8 0.8 copy.160
  70.6 0.4 copy-done.3
  71.0 0.5 fusion.73
  71.5 1.0 copy-done.4
  72.5 1.4 fusion.50
  73.9 0.1 multiply_reduce_fusion.2
  74.0 0.5 convolution_bitcast_fusion.2
  74.5 0.2 copy-done.8
  74.7 0.5 convolution_bitcast_fusion.1
  75.2 0.6 fusion.32
  75.8 1.2 copy.114
  77.0 2.4 %all-to-all-start.2 = ((bf16[128,16,128]{2,1,0:T(8,128)(2,1)}), bf16[128,16,128]{2,1,0:T(8,128)(2,1)S(1)}, u32[]{:S(2)}, u32[]{:S(2)}) async-start(bf16[128,16,128]{2,1,0:T(8,128)(2,1)} %copy.114), calls=%async_computation.2 | async-start | bytes 1048576 | tf_op jit(solution)/shard_map/all_to_all | solution.py:112
  79.4 1.2 copy.117
  80.5 14.8 %all-to-all-done.2 = bf16[128,16,128]{2,1,0:T(8,128)(2,1)S(1)} async-done(((bf16[128,16,128]{2,1,0:T(8,128)(2,1)}), bf16[128,16,128]{2,1,0:T(8,128)(2,1)S(1)}, u32[]{:S(2)}, u32[]{:S(2)}) %all-to-all-start.2) | async-done | bytes 524320 | tf_op jit(solution)/shard_map/all_to_all | solution.py:112
  95.3 2.7 %all-to-all-start.3 = ((bf16[128,16,128]{2,1,0:T(8,128)(2,1)}), bf16[128,16,128]{2,1,0:T(8,128)(2,1)S(1)}, u32[]{:S(2)}, u32[]{:S(2)}) async-start(bf16[128,16,128]{2,1,0:T(8,128)(2,1)} %copy.117), calls=%async_computation.3 | async-start | bytes 1048576 | tf_op jit(solution)/shard_map/all_to_all | solution.py:113
  98.0 0.5 copy.158
  98.6 0.3 reshape.130
  98.9 15.0 %all-to-all-done.3 = bf16[128,16,128]{2,1,0:T(8,128)(2,1)S(1)} async-done(((bf16[128,16,128]{2,1,0:T(8,128)(2,1)}), bf16[128,16,128]{2,1,0:T(8,128)(2,1)S(1)}, u32[]{:S(2)}, u32[]{:S(2)}) %all-to-all-start.3) | async-done | bytes 524320 | tf_op jit(solution)/shard_map/all_to_all | solution.py:113
  113.9 0.5 copy.157
  114.4 0.3 reshape.132
  114.7 0.3 convolution_convert_fusion
  115.1 0.1 reshape.133
  115.3 0.4 copy.120
  115.7 18.4 %all_to_all.70 = bf16[4,512,128]{2,0,1:T(4,128)(2,1)S(1)} all-to-all(bf16[4,512,128]{2,0,1:T(4,128)(2,1)S(1)} %copy.120), channel_id=1, replica_groups=mesh['crops'=1,'rows'=16,'cols'=2] {'rows','cols'}, dimensions={1} | all-to-all | bytes 1048576 | tf_op jit(solution)/shard_map/all_to_all | solution.py:135
  134.1 0.1 fusion.52
  134.3 0.1 fusion.33
  134.4 0.2 multiply_reduce_fusion.1
  134.6 0.1 copy.122
  134.8 0.1 fusion.30
  134.9 0.3 copy-done.9
  135.2 0.3 fusion.34
  135.5 0.5 fusion.53
  136.1 0.1 multiply_reduce_fusion
  136.2 0.2 copy-done.6
  136.4 1.3 fusion.12
  137.8 1.3 copy.127
  (45 shorter events, 0.7 us)
Async XLA Ops:
  6.5 129.7 %copy-start = (bf16[512,128]{1,0:T(8,128)(2,1)S(1)}, bf16[512,128]{1,0:T(8,128)(2,1)}, u32[]{:S(2)}) copy-start(bf16[512,128]{1,0:T(8,128)(2,1)} %param.27) | copy-start | bytes 393220
  6.5 4.0 %copy-start.1 = (f32[8,128,256]{2,1,0:T(8,128)S(1)}, f32[8,128,256]{2,1,0:T(8,128)}, u32[]{:S(2)}) copy-start(f32[8,128,256]{2,1,0:T(8,128)} %param.15) | copy-start | bytes 3145732
  6.5 4.0 %copy-start.12 = (s32[8,128]{1,0:T(8,128)S(1)}, s32[8,128]{1,0:T(8,128)}, u32[]{:S(2)}) copy-start(s32[8,128]{1,0:T(8,128)} %param.16) | copy-start | bytes 12292
  6.5 4.0 %copy-start.10 = (bf16[256,32]{0,1:T(8,128)(2,1)S(1)}, bf16[256,32]{0,1:T(8,128)(2,1)}, u32[]{:S(2)}) copy-start(bf16[256,32]{0,1:T(8,128)(2,1)} %param.20) | copy-start | bytes 49156
  6.5 17.5 %copy-start.11 = (bf16[256,32]{0,1:T(8,128)(2,1)S(1)}, bf16[256,32]{0,1:T(8,128)(2,1)}, u32[]{:S(2)}) copy-start(bf16[256,32]{0,1:T(8,128)(2,1)} %param.19) | copy-start | bytes 49156
  6.5 53.8 %all-gather.2.cloned.1.call-start = ((), (), s32[]{:S(2)}) async-start(), calls=%async_computation.5 | async-start | bytes 1114112 | tf_op jit(solution)/shard_map/all_gather | solution.py:68
  10.5 26.5 %copy-start.5 = (f32[16,128,128]{2,1,0:T(8,128)S(1)}, f32[16,128,128]{2,1,0:T(8,128)}, u32[]{:S(2)}) copy-start(f32[16,128,128]{2,1,0:T(8,128)} %param.18) | copy-start | bytes 3145732
  16.1 14.2 %all-to-all-start.1 = ((bf16[8,16,16]{2,0,1:T(8,128)(2,1)}), bf16[8,16,16]{2,0,1:T(8,128)(2,1)S(1)}, u32[]{:S(2)}, u32[]{:S(2)}) async-start(bf16[8,16,16]{2,0,1:T(8,128)(2,1)} %copy.105), calls=%async_computation.1 | async-start | bytes 65536 | tf_op jit(solution)/shard_map/all_to_all | solution.py:77
  30.3 29.1 %all-to-all-start = ((bf16[16,2,2048]{2,1,0:T(2,128)(2,1)}), bf16[16,2,2048]{2,1,0:T(2,128)(2,1)S(1)}, u32[]{:S(2)}, u32[]{:S(2)}) async-start(bf16[16,2,2048]{2,1,0:T(2,128)(2,1)} %reshape.150), calls=%async_computation | async-start | bytes 262144 | tf_op jit(solution)/shard_map/all_to_all | solution.py:76
  59.4 3.5 %copy-start.2 = (bf16[1024,128]{1,0:T(8,128)(2,1)S(1)}, bf16[1024,128]{1,0:T(8,128)(2,1)}, u32[]{:S(2)}) copy-start(bf16[1024,128]{1,0:T(8,128)(2,1)} %param.21) | copy-start | bytes 786436
  65.0 1.2 copy-start.3
  66.7 1.0 copy-start.4
  69.8 1.2 copy-start.3
  71.5 1.0 copy-start.4
  72.5 1.6 %copy-start.7 = (bf16[128,256]{1,0:T(8,128)(2,1)S(1)}, bf16[128,256]{1,0:T(8,128)(2,1)}, u32[]{:S(2)}) copy-start(bf16[128,256]{1,0:T(8,128)(2,1)} %param.22) | copy-start | bytes 196612
  73.9 0.8 copy-start.8
  77.0 18.4 %all-to-all-start.2 = ((bf16[128,16,128]{2,1,0:T(8,128)(2,1)}), bf16[128,16,128]{2,1,0:T(8,128)(2,1)S(1)}, u32[]{:S(2)}, u32[]{:S(2)}) async-start(bf16[128,16,128]{2,1,0:T(8,128)(2,1)} %copy.114), calls=%async_computation.2 | async-start | bytes 1048576 | tf_op jit(solution)/shard_map/all_to_all | solution.py:112
  95.3 18.5 %all-to-all-start.3 = ((bf16[128,16,128]{2,1,0:T(8,128)(2,1)}), bf16[128,16,128]{2,1,0:T(8,128)(2,1)S(1)}, u32[]{:S(2)}, u32[]{:S(2)}) async-start(bf16[128,16,128]{2,1,0:T(8,128)(2,1)} %copy.117), calls=%async_computation.3 | async-start | bytes 1048576 | tf_op jit(solution)/shard_map/all_to_all | solution.py:113
  134.4 0.8 copy-start.9
  134.8 0.8 copy-start.13
  135.5 0.9 copy-start.6
Sparse Core Ops, SparseCore 0:
  11.8 41.1 all-gather.1
where the time goes:
time: 147 us; the launch traced here: 146 us
  blocking collectives  48.2 us (33%)
  waiting for transfers between devices  29.8 us (20%)
  starting transfers between devices  19.7 us (13%)
  local copies, waits for them, and re-layouts  17.6 us (12%)
  between operations  13.8 us (9%)
  matrix products  10.1 us (7%)
  other arithmetic  6.74 us (5%)
    all_gather x1, blocking collectives, on_device(): lax.all_gather(live_half, 'rows', axis=0, tiled=True)  21.7 us
    all_to_all x1, blocking collectives, on_device(): lax.all_to_all(regrouped, ('rows', 'cols'), split_axis=1, concat_axis=0,...  18.4 us
    all_to_all x1, waiting for transfers between devices, on_device(): lax.all_to_all(right_panel, ('rows', 'cols'), split_axis=0, concat_axis=1...  15 us
    all_to_all x1, waiting for transfers between devices, on_device(): lax.all_to_all(left_panel, ('rows', 'cols'), split_axis=0, concat_axis=1,...  14.8 us
    all_to_all x1, starting transfers between devices, on_device(): lax.all_to_all(wide_live, 'rows', split_axis=1, concat_axis=0, tiled=True)  7.94 us
    all_to_all x1, starting transfers between devices, on_device(): lax.all_to_all(left_wide, 'rows', split_axis=1, concat_axis=0, tiled=True)  6.72 us
    all_gather x1, blocking collectives, on_device(): lax.all_gather(family_lhs_mapped, 'cols', axis=1, tiled=True)  4.26 us
    dot_general x2, matrix products, outer_block(): jnp.einsum('lyj,lnx->ynjx', port_segments, right_all, preferred_element_t...  3.85 us
  transfers between devices with their start and end apart: 5, of which 2 were waited for; matrix products, arithmetic and copies ran while one was open for 4% of the time, Pallas kernels for 0%

commit v1 on v0

v1 whole, which is shorter than its diff:
```python
import functools

import jax
import jax.numpy as jnp
from jax import lax
from jax.experimental import pallas as pl
from jax.experimental.pallas import tpu as pltpu
from jax.sharding import PartitionSpec as P

EPS = 1e-05
F32 = jnp.float32
BF16 = jnp.bfloat16
TILE = 16
LANES = 128
VMEM = pl.BlockSpec(memory_space=pltpu.VMEM)


def dot(a, b):
    return lax.dot_general(a, b, (((1,), (0,)), ((), ())), preferred_element_type=F32)


def dot_nt(a, b):
    return lax.dot_general(a, b, (((1,), (1,)), ((), ())), preferred_element_type=F32)


def sigmoid(x):
    return 0.5 * jnp.tanh(0.5 * x) + 0.5


def call(kernel, out_shape, scratch, name):
    def run(*args):
        return pl.pallas_call(
            kernel,
            out_shape=out_shape,
            in_specs=[VMEM] * len(args),
            out_specs=jax.tree.map(lambda _: VMEM, out_shape),
            scratch_shapes=scratch,
            name=name,
        )(*args)

    return run


def project_kernel(fam_ref, keep_ref, pres_ref, wl_ref, wr_ref, right_ref, left_ref, nf, rs, *, tile_rows):
    seqs, cols, feats = fam_ref.shape
    chans = wl_ref.shape[1]
    col = lax.axis_index("cols")
    live = (keep_ref[...] * pres_ref[pl.ds(col, 1), :]).astype(F32)
    live_t = jnp.concatenate([live, jnp.zeros((LANES - seqs, cols), F32)], 0).T
    wr_t = wr_ref[...].astype(F32).T.astype(BF16)
    for s in range(seqs):
        v = fam_ref[s]
        centred = v - jnp.mean(v, -1, keepdims=True)
        spread = jnp.mean(centred * centred, -1, keepdims=True)
        n = centred * (lax.rsqrt(spread + EPS) * live_t[:, s : s + 1])
        for h in range(feats // LANES):
            nf[h, pl.ds(s * cols, cols), :] = n[:, h * LANES : (h + 1) * LANES]
        rs[pl.ds(s, chans, stride=seqs), :] = dot_nt(wr_t, n.astype(BF16))
    right_ref[0 : chans * seqs, :] = rs[...].astype(BF16)
    live_tile = jnp.concatenate([live, jnp.zeros((TILE - seqs, cols), F32)], 0).astype(BF16)
    right_ref[chans * seqs : chans * seqs + TILE, :] = live_tile
    per = LANES // chans
    groups = tile_rows // per
    pieces = cols // tile_rows
    wl = wl_ref[...].astype(F32)
    acc = None
    for i4 in range(per):
        parts = []
        if i4:
            parts.append(jnp.zeros((feats, i4 * chans), F32))
        parts.append(wl)
        if i4 < per - 1:
            parts.append(jnp.zeros((feats, (per - 1 - i4) * chans), F32))
        w = jnp.concatenate(parts, 1).astype(BF16)
        rows = [
            jnp.concatenate(
                [nf[h, pl.ds(pq * per + i4, seqs, stride=cols), :] for h in range(feats // LANES)], 1
            )
            for pq in range(pieces * groups)
        ]
        part = dot(jnp.concatenate(rows, 0).astype(BF16), w)
        acc = part if acc is None else acc + part
    block = groups * seqs
    for p in range(pieces):
        left_ref[p, 0:block, :] = acc[p * block : (p + 1) * block].astype(BF16)
        left_ref[p, block : block + TILE, :] = live_tile


def pair_kernel(
    right0_ref, right1_ref, left_ref, contact_ref, pres_ref, wo_ref, wp_ref,
    first_ref, gate_ref, panel_ref,
    o_scr, cnt_scr, pan_scr,
    *, seqs, radix, tile_rows, chans,
):
    tiles = right0_ref.shape[1] // TILE - 1
    half = right0_ref.shape[0]
    blocks = 2 * half
    cols = right0_ref.shape[2]
    feats = first_ref.shape[1]
    width = pan_scr.shape[1] // tile_rows
    pack = TILE // seqs
    per = LANES // chans
    groups = tile_rows // per
    row = lax.axis_index("rows")
    col = lax.axis_index("cols")
    z, y, c = row // 4, (row // 2) % 2, row % 2

    def source(b):
        cz, cy, cc = b % radix, (b // radix) % 2, b // (2 * radix)
        return lax.rem(z + radix - cz, radix) * 4 + (y ^ cy) * 2 + (c ^ cc)

    def right(b, t):
        ref = right0_ref if b < half else right1_ref
        return ref[b % half, t * TILE : (t + 1) * TILE, :]

    lefts = [left_ref[source(b)].astype(F32) for b in range(blocks)]
    block = groups * seqs
    live_l = jnp.concatenate([v[block : block + seqs] for v in lefts], 0).T.astype(BF16)
    live_r = jnp.concatenate([right(b, tiles).astype(F32)[:seqs] for b in range(blocks)], 0).astype(BF16)
    cnt_scr[...] = dot(live_l, live_r)
    start = lax.rem(row * tile_rows, cols)
    inv = 1.0 / jnp.maximum(cnt_scr[pl.ds(pl.multiple_of(start, 8), tile_rows), :], 1.0)
    zero = jnp.zeros((seqs, LANES), F32)
    ops = []
    for d2 in range(pack):
        for q in range(groups):
            rows = []
            for v in lefts:
                rows += [v[q * seqs : (q + 1) * seqs] if k == d2 else zero for k in range(pack)]
            ops.append(jnp.concatenate(rows, 0).T.astype(BF16))
    a_ext = jnp.concatenate(ops, 0)

    for t in range(0, tiles, 2):
        rhs = jnp.concatenate(
            [jnp.concatenate([right(b, u) for b in range(blocks)], 0) for u in (t, t + 1)], 1
        )
        out = dot(a_ext, rhs)
        for k in range(2):
            for d2 in range(pack):
                for i in range(tile_rows):
                    at = (d2 * tile_rows + i) * chans
                    val = out[at : at + chans, k * cols : (k + 1) * cols] * inv[i : i + 1]
                    d = (t + k) * pack + d2
                    o_scr[i, d * chans : (d + 1) * chans, :] = val.astype(BF16)

    w_o = wo_ref[...]
    w_p = wp_ref[...]
    live_j = pres_ref[pl.ds(col, 1), :].astype(F32)
    live_i = pres_ref[pl.ds(lax.div(row * tile_rows, cols), 1), :].astype(F32)
    cnt_scr[0:LANES, :] = jnp.broadcast_to(live_i, (LANES, cols)).T
    live_rows = cnt_scr[pl.ds(pl.multiple_of(start, 8), tile_rows), :]
    for i in range(0, tile_rows, 2):
        upd = dot(w_o, jnp.concatenate([o_scr[i], o_scr[i + 1]], 1))
        normed = []
        for k in range(2):
            first = contact_ref[i + k] + upd[:, k * cols : (k + 1) * cols]
            first_ref[i + k] = first
            centred = first - jnp.mean(first, 0, keepdims=True)
            spread = jnp.mean(centred * centred, 0, keepdims=True)
            normed.append((centred * lax.rsqrt(spread + EPS)).astype(BF16))
        raw = dot(w_p, jnp.concatenate(normed, 1))
        for k in range(2):
            live = live_rows[i + k : i + k + 1] * live_j
            part = raw[:, k * cols : (k + 1) * cols]
            for side in range(2):
                at = side * 2 * width
                val = part[at : at + width] * sigmoid(part[at + width : at + 2 * width]) * live
                pan_scr[side, pl.ds(i + k, width, stride=tile_rows), :] = val
            gate_ref[i + k] = sigmoid(part[4 * width : 4 * width + feats])
    for ch in range(width):
        for side in range(2):
            panel_ref[ch, side] = pan_scr[side, ch * tile_rows : (ch + 1) * tile_rows, :].astype(BF16)


def triangle_kernel(recv_ref, out_ref, *, n_rows, n_cols):
    own = recv_ref.shape[1]
    tile_rows, cols = recv_ref.shape[3:]
    for ch in range(own):
        sides = [
            jnp.concatenate(
                [
                    jnp.concatenate([recv_ref[r * n_cols + x, ch, side] for r in range(n_rows)], 0)
                    for x in range(n_cols)
                ],
                1,
            )
            for side in range(2)
        ]
        prod = dot_nt(sides[0], sides[1]).astype(BF16)
        for r in range(n_rows):
            for x in range(n_cols):
                out_ref[r * n_cols + x, ch] = prod[
                    r * tile_rows : (r + 1) * tile_rows, x * cols : (x + 1) * cols
                ]


def finish_kernel(prod_ref, first_ref, gate_ref, we_ref, w1_ref, w2_ref, out_ref, mix):
    chans, tile_rows, cols = prod_ref.shape
    total = jnp.zeros((tile_rows, cols), F32)
    for ch in range(chans):
        total = total + prod_ref[ch].astype(F32)
    mean = total * (1.0 / chans)
    square = jnp.zeros((tile_rows, cols), F32)
    for ch in range(chans):
        centred = prod_ref[ch].astype(F32) - mean
        square = square + centred * centred
    scale = lax.rsqrt(square * (1.0 / chans) + EPS)
    for ch in range(chans):
        mix[ch * tile_rows : (ch + 1) * tile_rows, :] = (prod_ref[ch].astype(F32) - mean) * scale
    w_e, w_1, w_2 = we_ref[...], w1_ref[...], w2_ref[...]
    for i in range(0, tile_rows, 2):
        mixed = jnp.concatenate(
            [mix[pl.ds(i + k, chans, stride=tile_rows), :].astype(BF16) for k in range(2)], 1
        )
        proj = dot(w_e, mixed)
        seconds, normed = [], []
        for k in range(2):
            second = first_ref[i + k] + gate_ref[i + k] * proj[:, k * cols : (k + 1) * cols]
            centred = second - jnp.mean(second, 0, keepdims=True)
            spread = jnp.mean(centred * centred, 0, keepdims=True)
            seconds.append(second)
            normed.append((centred * lax.rsqrt(spread + EPS)).astype(BF16))
        hidden = jnp.maximum(dot(w_1, jnp.concatenate(normed, 1)), 0.0).astype(BF16)
        out = dot(w_2, hidden)
        for k in range(2):
            out_ref[i + k] = (seconds[k] + out[:, k * cols : (k + 1) * cols]).T


def on_device(
    family_representation,
    family_keep_flags,
    amino_presence,
    contact_embedding,
    couple_lhs_weights,
    couple_rhs_weights,
    pairwise_final_matrix,
    edge_source_matrix,
    edge_target_matrix,
    edge_final_sigmoid_matrix,
    edge_final_matrix,
    feedforward_expand_matrix,
    feedforward_shrink_matrix,
):
    seqs, cols, feats = family_representation.shape
    tile_rows, _, pair_feats = contact_embedding.shape
    n_rows = lax.axis_size("rows")
    n_cols = lax.axis_size("cols")
    chans = couple_lhs_weights.shape[1]
    width = edge_source_matrix.shape[1] // 2
    devices = n_rows * n_cols
    radix = n_rows // 4
    pieces = cols // tile_rows
    col = lax.axis_index("cols")
    presence = amino_presence.reshape(n_cols, cols)
    shape = jax.ShapeDtypeStruct

    right_rows = chans * seqs + TILE
    left_rows = tile_rows * chans * seqs // LANES + TILE
    right, left = call(
        functools.partial(project_kernel, tile_rows=tile_rows),
        (shape((right_rows, cols), BF16), shape((pieces, left_rows, LANES), BF16)),
        [pltpu.VMEM((feats // LANES, seqs * cols, LANES), F32), pltpu.VMEM((chans * seqs, cols), F32)],
        "project",
    )(family_representation, family_keep_flags, presence, couple_lhs_weights, couple_rhs_weights)

    left_wide = jnp.zeros((n_cols, pieces, left_rows, LANES), BF16)
    left_wide = lax.dynamic_update_slice_in_dim(left_wide, left[None], col, 0)
    for k in range(1, n_cols):
        got = lax.ppermute(left, "cols", [(i, (i + k) % n_cols) for i in range(n_cols)])
        left_wide = lax.dynamic_update_slice_in_dim(left_wide, got[None], (col + n_cols - k) % n_cols, 0)
    blocks = [right]
    for k in range(1, radix):
        blocks.append(lax.ppermute(right, "rows", [(i, (i + 4 * k) % n_rows) for i in range(n_rows)]))
    right_z = jnp.stack(blocks)
    right_y = lax.ppermute(right_z, "rows", [(i, i ^ 2) for i in range(n_rows)])
    left_all = lax.all_to_all(
        left_wide.reshape(n_rows, left_rows, LANES), "rows", split_axis=0, concat_axis=0, tiled=True
    )
    right0 = jnp.concatenate([right_z, right_y], 0)
    right1 = lax.ppermute(right0, "rows", [(i, i ^ 1) for i in range(n_rows)])

    contact_t = contact_embedding.transpose(0, 2, 1)
    w_o = pairwise_final_matrix.reshape(chans, chans, pair_feats).transpose(2, 1, 0).reshape(pair_feats, chans * chans)
    w_p = jnp.concatenate([edge_source_matrix, edge_target_matrix, edge_final_sigmoid_matrix], 1).T
    pair = shape((tile_rows, pair_feats, cols), F32)
    first, gate, panels = call(
        functools.partial(pair_kernel, seqs=seqs, radix=radix, tile_rows=tile_rows, chans=chans),
        (pair, pair, shape((width, 2, tile_rows, cols), BF16)),
        [
            pltpu.VMEM((tile_rows, chans * chans, cols), BF16),
            pltpu.VMEM((LANES, cols), F32),
            pltpu.VMEM((2, width * tile_rows, cols), F32),
        ],
        "pair",
    )(right0, right1, left_all, contact_t, presence, w_o, w_p)

    panels = lax.all_to_all(
        panels.reshape(devices, width // devices, 2, tile_rows, cols),
        ("rows", "cols"), split_axis=0, concat_axis=0, tiled=True,
    )
    product = call(
        functools.partial(triangle_kernel, n_rows=n_rows, n_cols=n_cols),
        shape((devices, width // devices, tile_rows, cols), BF16),
        [],
        "triangle",
    )(panels)
    product = lax.all_to_all(product, ("rows", "cols"), split_axis=0, concat_axis=0, tiled=True)
    return call(
        finish_kernel,
        shape((tile_rows, cols, pair_feats), F32),
        [pltpu.VMEM((width * tile_rows, cols), F32)],
        "finish",
    )(
        product.reshape(width, tile_rows, cols), first, gate,
        edge_final_matrix.T, feedforward_expand_matrix.T, feedforward_shrink_matrix.T,
    )


def solution(mesh):
    tiles = P(("crops", "rows"), "cols", None)
    in_specs = (tiles, P(("crops", "rows"), "cols"), P("crops"), tiles) + (P(),) * 9
    return jax.shard_map(on_device, mesh=mesh, in_specs=in_specs, out_specs=tiles, check_vma=False)
```

time: 147 us -> 107 us (0.73)
  Pallas kernels: 0 us -> 20.3 us
  blocking collectives: 48.2 us -> 29.9 us
  between operations: 13.8 us -> 0.12 us
  matrix products: 10.1 us -> 0 us
  other arithmetic: 6.74 us -> 0.74 us
  waiting for transfers between devices: 29.8 us -> 24.7 us
  local copies, waits for them, and re-layouts: 17.6 us -> 12.8 us
  starting transfers between devices: 19.7 us -> 17.4 us
    all_gather x3 -> x0, blocking collectives: 29.8 us -> none  [the longest x1 21.7 us: on_device(): lax.all_gather(live_half, 'rows', axis=0, tiled=True)]
    pallas_call x0 -> x4, Pallas kernels: none -> 20.3 us  [run(): pl.pallas_call(kernel, out_shape=out_shape, in_specs=[VMEM] * len(args),...]
    all_to_all x4 -> x2, waiting for transfers between devices: 29.8 us -> 17 us  [the longest x1 13.4 us: on_device(): lax.all_to_all(product, ('rows', 'cols'), split_axis=0, concat_axis=0, ti...]
    all_to_all x4 -> x2, starting transfers between devices: 19.7 us -> 7.86 us  [the longest x1 4.19 us: on_device(): lax.all_to_all(left_wide.reshape(n_rows, left_rows, LANES), 'rows', split...]
    all_to_all x1, blocking collectives: 18.4 us -> 29.9 us  [on_device(): lax.all_to_all(panels.reshape(devices, width // devices, 2, tile_rows, co...]
    dot_general x14 -> x0, matrix products: 10.1 us -> none  [the longest x2 3.85 us: outer_block(): jnp.einsum('lyj,lnx->ynjx', port_segments, right_all, preferred_element_t...]
    ppermute x0 -> x6, starting transfers between devices: none -> 9.55 us  [the longest x3 5.49 us: on_device(): lax.ppermute(right, 'rows', [(i, (i + 4 * k) % n_rows) for i in range(n_r...]
    ppermute x0 -> x6, waiting for transfers between devices: none -> 7.73 us  [the longest x1 6.3 us: on_device(): right_y = lax.ppermute(right_z, 'rows', [(i, i ^ 2) for i in range(n_rows)])]
  transfers between devices with their start and end apart: 5 -> 8, of which waited for: 2 -> 4; matrix products, arithmetic and copies ran while one was open for 4% -> 7% of each run, Pallas kernels for 0% -> 0%
where the time goes in v1:
time: 107 us; the launch traced here: 106 us
  blocking collectives  29.9 us (28%)
  waiting for transfers between devices  24.7 us (23%)
  Pallas kernels  20.3 us (19%)
  starting transfers between devices  17.4 us (16%)
  local copies, waits for them, and re-layouts  12.8 us (12%)
    all_to_all x1, blocking collectives, on_device(): lax.all_to_all(panels.reshape(devices, width // devices, 2, tile_rows, co...  29.9 us
    pallas_call x4, Pallas kernels, run(): pl.pallas_call(kernel, out_shape=out_shape, in_specs=[VMEM] * len(args),...  20.3 us
    all_to_all x1, waiting for transfers between devices, on_device(): lax.all_to_all(product, ('rows', 'cols'), split_axis=0, concat_axis=0, ti...  13.4 us
    unnamed x43, local copies, waits for them, and re-layouts  9.79 us
    ppermute x1, waiting for transfers between devices, on_device(): right_y = lax.ppermute(right_z, 'rows', [(i, i ^ 2) for i in range(n_rows)])  6.3 us
    ppermute x3, starting transfers between devices, on_device(): lax.ppermute(right, 'rows', [(i, (i + 4 * k) % n_rows) for i in range(n_r...  5.49 us
    all_to_all x1, starting transfers between devices, on_device(): lax.all_to_all(left_wide.reshape(n_rows, left_rows, LANES), 'rows', split...  4.19 us
    all_to_all x1, starting transfers between devices, on_device(): lax.all_to_all(product, ('rows', 'cols'), split_axis=0, concat_axis=0, ti...  3.67 us
  transfers between devices with their start and end apart: 8, of which 4 were waited for; matrix products, arithmetic and copies ran while one was open for 7% of the time, Pallas kernels for 0%

profile of v1, /device:TPU:1, one launch (start us, length us, event | category | flops | bytes accessed | tf_op | source)
XLA Modules:
  0.0 106.1 jit_solution(15299031701045221154)
XLA Ops:
  0.0 0.0 copy-start.14
  0.0 1.5 %copy.34.wl_ref = bf16[256,32]{1,0:T(8,128)(2,1)} copy(bf16[256,32]{0,1:T(8,128)(2,1)} %param.17) | data formatting | bytes 32768 | tf_op args[4]
  1.5 0.0 copy-done.14
  1.5 0.7 copy.35.wr_ref
  2.2 3.8 %project.1 = (bf16[272,128]{1,0:T(8,128)(2,1)}, bf16[8,48,128]{2,1,0:T(8,128)(2,1)}) custom-call(f32[8,128,256]{2,1,0:T(8,128)} %fam_ref.1, s32[8,128]{1,0:T(8,128)} %keep_ref.1, s32[2,128]{1,0:T(2,128)} %bitcast.38, bf16[256,32]{1,0:T(8,128)(2,1)} %copy.34.wl_ref, bf16[256,32]{1,0:T(8,128)(2,1)} %copy.35.wr_ref), custom_call_target="tpu_custom_call" | custom-call | tf_op jit(solution)/shard_map/project/pallas_call | solution.py:32
  6.0 2.1 %collective-permute-start = (bf16[272,128]{1,0:T(8,128)(2,1)}, bf16[272,128]{1,0:T(8,128)(2,1)S(1)}, u32[]{:S(2)}, u32[]{:S(2)}) collective-permute-start(bf16[272,128]{1,0:T(8,128)(2,1)} %get-tuple-element.10), channel_id=1, source_target_pairs={{0,8},{2,10},{4,12},{6,14},{8,16},{10,18},{12,20},{14,22},{16,24},... | collective-permute-start | bytes 208904 | tf_op jit(solution)/shard_map/ppermute | solution.py:273
  8.1 2.3 %collective-permute-start.1 = (bf16[272,128]{1,0:T(8,128)(2,1)}, bf16[272,128]{1,0:T(8,128)(2,1)S(1)}, u32[]{:S(2)}, u32[]{:S(2)}) collective-permute-start(bf16[272,128]{1,0:T(8,128)(2,1)} %get-tuple-element.10), channel_id=1, source_target_pairs={{0,16},{2,18},{4,20},{6,22},{8,24},{10,26},{12,28},{14,30},{16,0},... | collective-permute-start | bytes 208904 | tf_op jit(solution)/shard_map/ppermute | solution.py:273
  10.4 1.1 %collective-permute-start.2 = (bf16[272,128]{1,0:T(8,128)(2,1)}, bf16[272,128]{1,0:T(8,128)(2,1)S(1)}, u32[]{:S(2)}, u32[]{:S(2)}) collective-permute-start(bf16[272,128]{1,0:T(8,128)(2,1)} %get-tuple-element.10), channel_id=1, source_target_pairs={{0,24},{2,26},{4,28},{6,30},{8,0},{10,2},{12,4},{14,6},{16,8},{18,... | collective-permute-start | bytes 208904 | tf_op jit(solution)/shard_map/ppermute | solution.py:273
  11.5 1.2 %collective-permute-start.5 = (bf16[8,48,128]{2,1,0:T(8,128)(2,1)}, bf16[8,48,128]{2,1,0:T(8,128)(2,1)S(1)}, u32[]{:S(2)}, u32[]{:S(2)}) collective-permute-start(bf16[8,48,128]{2,1,0:T(8,128)(2,1)} %get-tuple-element.11), channel_id=1, source_target_pairs={{0,1},{1,0},{2,3},{3,2},{4,5},{5,4},{6,7},{7,6},{8,9},{9,8},{10,11... | collective-permute-start | bytes 294920 | tf_op jit(solution)/shard_map/ppermute | solution.py:269
  12.7 0.0 copy-start.9
  12.7 0.7 broadcast_in_dim.9
  13.4 0.2 copy-done.9
  13.6 0.0 copy-start.5
  13.6 0.7 bitcast_dynamic-update-slice_fusion.1
  14.3 0.2 copy-done.5
  14.5 0.0 collective-permute-done
  14.5 1.4 %collective-permute-done.1 = bf16[272,128]{1,0:T(8,128)(2,1)S(1)} collective-permute-done((bf16[272,128]{1,0:T(8,128)(2,1)}, bf16[272,128]{1,0:T(8,128)(2,1)S(1)}, u32[]{:S(2)}, u32[]{:S(2)}) %collective-permute-start.1) | collective-permute-done | bytes 69664 | tf_op jit(solution)/shard_map/ppermute | solution.py:273
  16.0 0.0 collective-permute-done.2
  16.0 0.0 copy-start.1
  16.0 1.1 %collective-permute-start.3 = (bf16[4,272,128]{2,1,0:T(8,128)(2,1)S(1)}, bf16[4,272,128]{2,1,0:T(8,128)(2,1)S(1)}, u32[]{:S(2)}, u32[]{:S(2)}) collective-permute-start(bf16[4,272,128]{2,1,0:T(8,128)(2,1)S(1)} %pad_maximum_fusion), channel_id=1, source_target_pairs={{0,4},{2,6},{4,0},{6,2},{8,12},{10,14},{12,8},{14,10},{16,20},{18,... | collective-permute-start | bytes 835592 | tf_op jit(solution)/shard_map/ppermute | solution.py:275
  17.1 6.3 %collective-permute-done.3 = bf16[4,272,128]{2,1,0:T(8,128)(2,1)S(1)} collective-permute-done((bf16[4,272,128]{2,1,0:T(8,128)(2,1)S(1)}, bf16[4,272,128]{2,1,0:T(8,128)(2,1)S(1)}, u32[]{:S(2)}, u32[]{:S(2)}) %collective-permute-start.3) | collective-permute-done | bytes 278560 | tf_op jit(solution)/shard_map/ppermute | solution.py:275
  23.5 0.0 copy-start.3
  23.5 1.8 %collective-permute-start.4 = (bf16[8,272,128]{2,1,0:T(8,128)(2,1)S(1)}, bf16[8,272,128]{2,1,0:T(8,128)(2,1)S(1)}, u32[]{:S(2)}, u32[]{:S(2)}) collective-permute-start(bf16[8,272,128]{2,1,0:T(8,128)(2,1)S(1)} %constant_dynamic-update-slice_fusion.right0_ref), channel_id=1, source_target_pairs={{0,2},{2,0},{4,6},{6,4},{8,10},{10,8},{12,14},{14,12},{16,18},{18,... | collective-permute-start | bytes 1671176 | tf_op jit(solution)/shard_map/ppermute | solution.py:280
  25.3 0.0 collective-permute-done.5
  25.3 0.6 bitcast_dynamic-update-slice_fusion
  25.9 4.2 %all-to-all-start = ((bf16[16,48,128]{2,1,0:T(8,128)(2,1)}), bf16[16,48,128]{2,1,0:T(8,128)(2,1)S(1)}, u32[]{:S(2)}, u32[]{:S(2)}) async-start(bf16[16,48,128]{2,1,0:T(8,128)(2,1)} %bitcast.7), calls=%async_computation | async-start | bytes 393216 | tf_op jit(solution)/shard_map/all_to_all | solution.py:276
  30.1 0.0 copy-done.1
  30.1 0.0 copy-start.6
  30.1 1.3 %copy.36 = f32[16,128,128]{1,2,0:T(8,128)} copy(f32[16,128,128]{2,1,0:T(8,128)S(1)} %copy-done.1) | data formatting | bytes 2097152 | tf_op args[3]
  31.4 0.0 copy-done.3
  31.4 0.0 copy-done.6
  31.4 0.1 copy.37
  31.5 0.0 copy-start.10
  31.5 0.9 copy.41.wo_ref
  32.4 0.0 copy-done.10
  32.4 0.0 copy-start.11
  32.4 0.1 copy.38
  32.5 0.7 copy-done.11
  33.3 0.0 copy-start.12
  33.3 0.1 copy.39
  33.4 0.6 copy-done.12
  34.0 0.1 copy.40
  34.1 0.7 maximum_bitcast_fusion.wp_ref
  34.8 3.5 %all-to-all-done.left_ref = bf16[16,48,128]{2,1,0:T(8,128)(2,1)S(1)} async-done(((bf16[16,48,128]{2,1,0:T(8,128)(2,1)}), bf16[16,48,128]{2,1,0:T(8,128)(2,1)S(1)}, u32[]{:S(2)}, u32[]{:S(2)}) %all-to-all-start) | async-done | bytes 196640 | tf_op jit(solution)/shard_map/all_to_all | solution.py:276
  38.4 0.0 copy-start.2
  38.4 0.0 collective-permute-done.4.right1_ref
  38.4 0.0 copy-start.4
  38.4 0.7 copy-done.2
  39.1 0.2 copy-done.4
  39.3 6.9 %pair.1 = (f32[16,128,128]{2,1,0:T(8,128)}, f32[16,128,128]{2,1,0:T(8,128)}, bf16[128,2,16,128]{3,2,1,0:T(8,128)(2,1)}) custom-call(bf16[8,272,128]{2,1,0:T(8,128)(2,1)} %copy-done.3, bf16[8,272,128]{2,1,0:T(8,128)(2,1)} %copy-done.4, bf16[16,48,128]{2,1,0:T(8,128)(2,1)} %copy-done.2, f32[16,128,128]{2,1,0:T(8,128)} %bitcast.26, s32[2,128]{1,0:T(2,128)} %bitcast.39, ...), custom_call_target="tpu_custom_call" | custom-call | tf_op jit(solution)/shard_map/pair/pallas_call | solution.py:32
  46.1 29.9 %all_to_all.15.recv_ref = bf16[32,4,2,16,128]{4,3,2,1,0:T(8,128)(2,1)} all-to-all(bf16[32,4,2,16,128]{4,3,2,1,0:T(8,128)(2,1)} %bitcast.28), channel_id=1, replica_groups=mesh['crops'=1,'rows'=16,'cols'=2] {'rows','cols'}, dimensions={0} | all-to-all | bytes 2097152 | tf_op jit(solution)/shard_map/all_to_all | solution.py:297
  76.1 2.3 %triangle.1 = bf16[32,4,16,128]{3,2,1,0:T(8,128)(2,1)} custom-call(bf16[32,4,2,16,128]{4,3,2,1,0:T(8,128)(2,1)} %all_to_all.15.recv_ref), custom_call_target="tpu_custom_call" | custom-call | tf_op jit(solution)/shard_map/triangle/pallas_call | solution.py:32
  78.4 0.0 copy-start.7
  78.4 3.7 %all-to-all-start.2 = ((bf16[32,4,16,128]{3,2,1,0:T(8,128)(2,1)}), bf16[32,4,16,128]{3,2,1,0:T(8,128)(2,1)S(1)}, u32[]{:S(2)}, u32[]{:S(2)}) async-start(bf16[32,4,16,128]{3,2,1,0:T(8,128)(2,1)} %triangle.1), calls=%async_computation.2 | async-start | bytes 1048576 | tf_op jit(solution)/shard_map/all_to_all | solution.py:307
  82.1 0.0 copy-done.7
  82.1 0.0 copy-start.8
  82.1 0.8 copy.43
  82.9 0.1 copy-done.8
  83.0 0.8 copy.44
  83.8 0.0 copy-done.13
  83.8 0.7 copy.42
  84.5 13.4 %all-to-all-done.2 = bf16[32,4,16,128]{3,2,1,0:T(8,128)(2,1)S(1)} async-done(((bf16[32,4,16,128]{3,2,1,0:T(8,128)(2,1)}), bf16[32,4,16,128]{3,2,1,0:T(8,128)(2,1)S(1)}, u32[]{:S(2)}, u32[]{:S(2)}) %all-to-all-start.2) | async-done | bytes 524320 | tf_op jit(solution)/shard_map/all_to_all | solution.py:307
  98.0 0.8 copy-done
  98.8 7.3 %finish.1 = f32[16,128,128]{2,1,0:T(8,128)} custom-call(bf16[128,16,128]{2,1,0:T(8,128)(2,1)} %bitcast.27, f32[16,128,128]{2,1,0:T(8,128)} %get-tuple-element.13.first_ref, f32[16,128,128]{2,1,0:T(8,128)} %get-tuple-element.14.gate_ref, bf16[128,128]{1,0:T(8,128)(2,1)} %bitcast.37, bf16[512,128]{1,0:T(8,128)(2,1)} %bitcast.30, bf16[128,512]{1,0:T(8,128)(2,1)} %bitcast.31), custom_call_target="tpu_custom_call" | custom-call | tf_op jit(solution)/shard_map/finish/pallas_call | solution.py:32
  (8 shorter events, 0.1 us)
Async XLA Ops:
  0.0 1.5 %copy-start.14 = (bf16[256,32]{0,1:T(8,128)(2,1)S(1)}, bf16[256,32]{0,1:T(8,128)(2,1)}, u32[]{:S(2)}) copy-start(bf16[256,32]{0,1:T(8,128)(2,1)} %param.18) | copy-start | bytes 49156
  6.0 8.5 %collective-permute-start = (bf16[272,128]{1,0:T(8,128)(2,1)}, bf16[272,128]{1,0:T(8,128)(2,1)S(1)}, u32[]{:S(2)}, u32[]{:S(2)}) collective-permute-start(bf16[272,128]{1,0:T(8,128)(2,1)} %get-tuple-element.10), channel_id=1, source_target_pairs={{0,8},{2,10},{4,12},{6,14},{8,16},{10,18},{12,20},{14,22},{16,24},... | collective-permute-start | bytes 208904 | tf_op jit(solution)/shard_map/ppermute | solution.py:273
  8.1 7.9 %collective-permute-start.1 = (bf16[272,128]{1,0:T(8,128)(2,1)}, bf16[272,128]{1,0:T(8,128)(2,1)S(1)}, u32[]{:S(2)}, u32[]{:S(2)}) collective-permute-start(bf16[272,128]{1,0:T(8,128)(2,1)} %get-tuple-element.10), channel_id=1, source_target_pairs={{0,16},{2,18},{4,20},{6,22},{8,24},{10,26},{12,28},{14,30},{16,0},... | collective-permute-start | bytes 208904 | tf_op jit(solution)/shard_map/ppermute | solution.py:273
  10.4 5.5 %collective-permute-start.2 = (bf16[272,128]{1,0:T(8,128)(2,1)}, bf16[272,128]{1,0:T(8,128)(2,1)S(1)}, u32[]{:S(2)}, u32[]{:S(2)}) collective-permute-start(bf16[272,128]{1,0:T(8,128)(2,1)} %get-tuple-element.10), channel_id=1, source_target_pairs={{0,24},{2,26},{4,28},{6,30},{8,0},{10,2},{12,4},{14,6},{16,8},{18,... | collective-permute-start | bytes 208904 | tf_op jit(solution)/shard_map/ppermute | solution.py:273
  11.5 13.8 %collective-permute-start.5 = (bf16[8,48,128]{2,1,0:T(8,128)(2,1)}, bf16[8,48,128]{2,1,0:T(8,128)(2,1)S(1)}, u32[]{:S(2)}, u32[]{:S(2)}) collective-permute-start(bf16[8,48,128]{2,1,0:T(8,128)(2,1)} %get-tuple-element.11), channel_id=1, source_target_pairs={{0,1},{1,0},{2,3},{3,2},{4,5},{5,4},{6,7},{7,6},{8,9},{9,8},{10,11... | collective-permute-start | bytes 294920 | tf_op jit(solution)/shard_map/ppermute | solution.py:269
  12.7 0.9 copy-start.9
  13.6 0.9 copy-start.5
  16.0 14.1 %copy-start.1 = (f32[16,128,128]{2,1,0:T(8,128)S(1)}, f32[16,128,128]{2,1,0:T(8,128)}, u32[]{:S(2)}) copy-start(f32[16,128,128]{2,1,0:T(8,128)} %param.16) | copy-start | bytes 3145732
  16.0 7.4 %collective-permute-start.3 = (bf16[4,272,128]{2,1,0:T(8,128)(2,1)S(1)}, bf16[4,272,128]{2,1,0:T(8,128)(2,1)S(1)}, u32[]{:S(2)}, u32[]{:S(2)}) collective-permute-start(bf16[4,272,128]{2,1,0:T(8,128)(2,1)S(1)} %pad_maximum_fusion), channel_id=1, source_target_pairs={{0,4},{2,6},{4,0},{6,2},{8,12},{10,14},{12,8},{14,10},{16,20},{18,... | collective-permute-start | bytes 835592 | tf_op jit(solution)/shard_map/ppermute | solution.py:275
  23.5 7.9 %copy-start.3 = (bf16[8,272,128]{2,1,0:T(8,128)(2,1)}, bf16[8,272,128]{2,1,0:T(8,128)(2,1)S(1)}, u32[]{:S(2)}) copy-start(bf16[8,272,128]{2,1,0:T(8,128)(2,1)S(1)} %constant_dynamic-update-slice_fusion.right0_ref) | copy-start | bytes 1671172
  23.5 14.9 %collective-permute-start.4 = (bf16[8,272,128]{2,1,0:T(8,128)(2,1)S(1)}, bf16[8,272,128]{2,1,0:T(8,128)(2,1)S(1)}, u32[]{:S(2)}, u32[]{:S(2)}) collective-permute-start(bf16[8,272,128]{2,1,0:T(8,128)(2,1)S(1)} %constant_dynamic-update-slice_fusion.right0_ref), channel_id=1, source_target_pairs={{0,2},{2,0},{4,6},{6,4},{8,10},{10,8},{12,14},{14,12},{16,18},{18,... | collective-permute-start | bytes 1671176 | tf_op jit(solution)/shard_map/ppermute | solution.py:280
  25.9 12.5 %all-to-all-start = ((bf16[16,48,128]{2,1,0:T(8,128)(2,1)}), bf16[16,48,128]{2,1,0:T(8,128)(2,1)S(1)}, u32[]{:S(2)}, u32[]{:S(2)}) async-start(bf16[16,48,128]{2,1,0:T(8,128)(2,1)} %bitcast.7), calls=%async_computation | async-start | bytes 393216 | tf_op jit(solution)/shard_map/all_to_all | solution.py:276
  30.1 1.3 %copy-start.6 = (bf16[1024,128]{1,0:T(8,128)(2,1)S(1)}, bf16[1024,128]{1,0:T(8,128)(2,1)}, u32[]{:S(2)}) copy-start(bf16[1024,128]{1,0:T(8,128)(2,1)} %param.19) | copy-start | bytes 786436
  31.5 0.9 copy-start.10
  32.4 0.8 copy-start.11
  33.3 0.8 copy-start.12
  38.4 0.7 copy-start.2
  38.4 0.9 copy-start.4
  78.4 3.7 %copy-start.7 = (bf16[128,512]{1,0:T(8,128)(2,1)S(1)}, bf16[128,512]{1,0:T(8,128)(2,1)}, u32[]{:S(2)}) copy-start(bf16[128,512]{1,0:T(8,128)(2,1)} %param.24) | copy-start | bytes 393220
  78.4 19.5 %all-to-all-start.2 = ((bf16[32,4,16,128]{3,2,1,0:T(8,128)(2,1)}), bf16[32,4,16,128]{3,2,1,0:T(8,128)(2,1)S(1)}, u32[]{:S(2)}, u32[]{:S(2)}) async-start(bf16[32,4,16,128]{3,2,1,0:T(8,128)(2,1)} %triangle.1), calls=%async_computation.2 | async-start | bytes 1048576 | tf_op jit(solution)/shard_map/all_to_all | solution.py:307
  82.1 0.9 copy-start.8
  83.0 0.8 copy-start.13
  98.0 0.8 copy-start

commit v2 on v1

--- a/solution.py
+++ b/solution.py
@@ -43,11 +43,11 @@
 
 def project_kernel(fam_ref, keep_ref, pres_ref, wl_ref, wr_ref, right_ref, left_ref, nf, rs, *, tile_rows):
     seqs, cols, feats = fam_ref.shape
-    chans = wl_ref.shape[1]
+    chans = wl_ref.shape[0]
     col = lax.axis_index("cols")
     live = (keep_ref[...] * pres_ref[pl.ds(col, 1), :]).astype(F32)
     live_t = jnp.concatenate([live, jnp.zeros((LANES - seqs, cols), F32)], 0).T
-    wr_t = wr_ref[...].astype(F32).T.astype(BF16)
+    wr_t = wr_ref[...]
     for s in range(seqs):
         v = fam_ref[s]
         centred = v - jnp.mean(v, -1, keepdims=True)
@@ -62,7 +62,7 @@
     per = LANES // chans
     groups = tile_rows // per
     pieces = cols // tile_rows
-    wl = wl_ref[...].astype(F32)
+    wl = wl_ref[...].astype(F32).T
     acc = None
     for i4 in range(per):
         parts = []
@@ -87,10 +87,10 @@
 
 
 def pair_kernel(
-    right0_ref, right1_ref, left_ref, contact_ref, pres_ref, wo_ref, wp_ref,
+    right0_ref, right1_ref, left0_ref, left1_ref, contact_ref, pres_ref, wo_ref, wp_ref,
     first_ref, gate_ref, panel_ref,
     o_scr, cnt_scr, pan_scr,
-    *, seqs, radix, tile_rows, chans,
+    *, seqs, tile_rows, chans,
 ):
     tiles = right0_ref.shape[1] // TILE - 1
     half = right0_ref.shape[0]
@@ -103,17 +103,11 @@
     groups = tile_rows // per
     row = lax.axis_index("rows")
     col = lax.axis_index("cols")
-    z, y, c = row // 4, (row // 2) % 2, row % 2
-
-    def source(b):
-        cz, cy, cc = b % radix, (b // radix) % 2, b // (2 * radix)
-        return lax.rem(z + radix - cz, radix) * 4 + (y ^ cy) * 2 + (c ^ cc)
-
     def right(b, t):
         ref = right0_ref if b < half else right1_ref
         return ref[b % half, t * TILE : (t + 1) * TILE, :]
 
-    lefts = [left_ref[source(b)].astype(F32) for b in range(blocks)]
+    lefts = [ref[b].astype(F32) for ref in (left0_ref, left1_ref) for b in range(half)]
     block = groups * seqs
     live_l = jnp.concatenate([v[block : block + seqs] for v in lefts], 0).T.astype(BF16)
     live_r = jnp.concatenate([right(b, tiles).astype(F32)[:seqs] for b in range(blocks)], 0).astype(BF16)
@@ -261,30 +255,45 @@
         (shape((right_rows, cols), BF16), shape((pieces, left_rows, LANES), BF16)),
         [pltpu.VMEM((feats // LANES, seqs * cols, LANES), F32), pltpu.VMEM((chans * seqs, cols), F32)],
         "project",
-    )(family_representation, family_keep_flags, presence, couple_lhs_weights, couple_rhs_weights)
-
+    )(family_representation, family_keep_flags, presence, couple_lhs_weights.T, couple_rhs_weights.T)
+
+    row = lax.axis_index("rows")
     left_wide = jnp.zeros((n_cols, pieces, left_rows, LANES), BF16)
     left_wide = lax.dynamic_update_slice_in_dim(left_wide, left[None], col, 0)
     for k in range(1, n_cols):
         got = lax.ppermute(left, "cols", [(i, (i + k) % n_cols) for i in range(n_cols)])
         left_wide = lax.dynamic_update_slice_in_dim(left_wide, got[None], (col + n_cols - k) % n_cols, 0)
-    blocks = [right]
+    left_wide = left_wide.reshape(radix, 2, 2, left_rows, LANES)
+
+    def shift(k):
+        return [(i, (i + 4 * k) % n_rows) for i in range(n_rows)]
+
+    right_z = jnp.stack([right] + [lax.ppermute(right, "rows", shift(k)) for k in range(1, radix)])
+    pair_y = [(i, i ^ 2) for i in range(n_rows)]
+    pair_c = [(i, i ^ 1) for i in range(n_rows)]
+    right_y = lax.ppermute(right_z, "rows", pair_y)
+
+    def pick(array, index, axis):
+        return lax.dynamic_index_in_dim(array, index, axis, keepdims=False)
+
+    left_z = [pick(left_wide, row // 4, 0)]
     for k in range(1, radix):
-        blocks.append(lax.ppermute(right, "rows", [(i, (i + 4 * k) % n_rows) for i in range(n_rows)]))
-    right_z = jnp.stack(blocks)
-    right_y = lax.ppermute(right_z, "rows", [(i, i ^ 2) for i in range(n_rows)])
-    left_all = lax.all_to_all(
-        left_wide.reshape(n_rows, left_rows, LANES), "rows", split_axis=0, concat_axis=0, tiled=True
-    )
+        left_z.append(lax.ppermute(pick(left_wide, (row // 4 + k) % radix, 0), "rows", shift(k)))
+    left_z = jnp.stack(left_z)
     right0 = jnp.concatenate([right_z, right_y], 0)
-    right1 = lax.ppermute(right0, "rows", [(i, i ^ 1) for i in range(n_rows)])
+    right1 = lax.ppermute(right0, "rows", pair_c)
+    y, c = (row // 2) % 2, row % 2
+    left_y = jnp.stack([pick(left_z, y, 1), lax.ppermute(pick(left_z, 1 - y, 1), "rows", pair_y)])
+    left_y = left_y.reshape(2 * radix, 2, left_rows, LANES)
+    left0 = pick(left_y, c, 1)
+    left1 = lax.ppermute(pick(left_y, 1 - c, 1), "rows", pair_c)
 
     contact_t = contact_embedding.transpose(0, 2, 1)
     w_o = pairwise_final_matrix.reshape(chans, chans, pair_feats).transpose(2, 1, 0).reshape(pair_feats, chans * chans)
     w_p = jnp.concatenate([edge_source_matrix, edge_target_matrix, edge_final_sigmoid_matrix], 1).T
     pair = shape((tile_rows, pair_feats, cols), F32)
     first, gate, panels = call(
-        functools.partial(pair_kernel, seqs=seqs, radix=radix, tile_rows=tile_rows, chans=chans),
+        functools.partial(pair_kernel, seqs=seqs, tile_rows=tile_rows, chans=chans),
         (pair, pair, shape((width, 2, tile_rows, cols), BF16)),
         [
             pltpu.VMEM((tile_rows, chans * chans, cols), BF16),
@@ -292,7 +301,7 @@
             pltpu.VMEM((2, width * tile_rows, cols), F32),
         ],
         "pair",
-    )(right0, right1, left_all, contact_t, presence, w_o, w_p)
+    )(right0, right1, left0, left1, contact_t, presence, w_o, w_p)
 
     panels = lax.all_to_all(
         panels.reshape(devices, width // devices, 2, tile_rows, cols),

time: 107 us -> 100 us (0.935)
  waiting for transfers between devices: 24.7 us -> 17.4 us
  starting transfers between devices: 17.4 us -> 19.9 us
  local copies, waits for them, and re-layouts: 12.8 us -> 10.6 us
    ppermute x5 -> x10, starting transfers between devices: 8.34 us -> 15 us  [the longest x3 5.49 us: on_device(): lax.ppermute(right, 'rows', shift(k))]
    all_to_all x1 -> x0, starting transfers between devices: 4.19 us -> none  [on_device(): lax.all_to_all(left_wide.reshape(n_rows, left_rows, LANES), 'rows', split...]
    ppermute x5 -> x10, waiting for transfers between devices: 7.72 us -> 3.91 us  [the longest x3 1.99 us: on_device(): lax.ppermute(pick(left_wide, (row // 4 + k) % radix, 0), 'rows', shift(k))]
    all_to_all x1 -> x0, waiting for transfers between devices: 3.55 us -> none  [on_device(): lax.all_to_all(left_wide.reshape(n_rows, left_rows, LANES), 'rows', split...]
    unnamed x43 -> x39, local copies, waits for them, and re-layouts: 9.79 us -> 8.85 us
  transfers between devices with their start and end apart: 8 -> 12, of which waited for: 4 -> 6; matrix products, arithmetic and copies ran while one was open for 7% -> 6% of each run, Pallas kernels for 0% -> 0%
where the time goes in v2:
time: 100 us; the launch traced here: 99.5 us
  blocking collectives  30 us (30%)
  Pallas kernels  20.5 us (20%)
  starting transfers between devices  19.9 us (20%)
  waiting for transfers between devices  17.4 us (17%)
  local copies, waits for them, and re-layouts  10.6 us (11%)
    all_to_all x1, blocking collectives, on_device(): lax.all_to_all(panels.reshape(devices, width // devices, 2, tile_rows, co...  30 us
    pallas_call x4, Pallas kernels, run(): pl.pallas_call(kernel, out_shape=out_shape, in_specs=[VMEM] * len(args),...  20.5 us
    all_to_all x1, waiting for transfers between devices, on_device(): lax.all_to_all(product, ('rows', 'cols'), split_axis=0, concat_axis=0, ti...  13.5 us
    unnamed x39, local copies, waits for them, and re-layouts  8.85 us
    ppermute x3, starting transfers between devices, on_device(): lax.ppermute(right, 'rows', shift(k))  5.49 us
    ppermute x3, starting transfers between devices, on_device(): lax.ppermute(pick(left_wide, (row // 4 + k) % radix, 0), 'rows', shift(k))  3.98 us
    all_to_all x1, starting transfers between devices, on_device(): lax.all_to_all(product, ('rows', 'cols'), split_axis=0, concat_axis=0, ti...  3.76 us
    ppermute x1, starting transfers between devices, on_device(): right1 = lax.ppermute(right0, 'rows', pair_c)  3.19 us
  transfers between devices with their start and end apart: 12, of which 6 were waited for; matrix products, arithmetic and copies ran while one was open for 6% of the time, Pallas kernels for 0%

profile of v2, /device:TPU:1, one launch (start us, length us, event | category | flops | bytes accessed | tf_op | source)
XLA Modules:
  0.0 99.5 jit_solution(12599757118151053709)
XLA Ops:
  0.0 4.0 %project.1 = (bf16[272,128]{1,0:T(8,128)(2,1)}, bf16[8,48,128]{2,1,0:T(8,128)(2,1)}) custom-call(f32[8,128,256]{2,1,0:T(8,128)} %fam_ref.1, s32[8,128]{1,0:T(8,128)} %keep_ref.1, s32[2,128]{1,0:T(2,128)} %bitcast.71, bf16[32,256]{1,0:T(8,128)(2,1)} %bitcast.69, bf16[32,256]{1,0:T(8,128)(2,1)} %bitcast.70), custom_call_target="tpu_custom_call" | custom-call | tf_op jit(solution)/shard_map/project/pallas_call | solution.py:32
  4.0 2.1 %collective-permute-start = (bf16[272,128]{1,0:T(8,128)(2,1)}, bf16[272,128]{1,0:T(8,128)(2,1)S(1)}, u32[]{:S(2)}, u32[]{:S(2)}) collective-permute-start(bf16[272,128]{1,0:T(8,128)(2,1)} %get-tuple-element.10), channel_id=1, source_target_pairs={{0,8},{2,10},{4,12},{6,14},{8,16},{10,18},{12,20},{14,22},{16,24},... | collective-permute-start | bytes 208904 | tf_op jit(solution)/shard_map/ppermute | solution.py:271
  6.1 2.3 %collective-permute-start.1 = (bf16[272,128]{1,0:T(8,128)(2,1)}, bf16[272,128]{1,0:T(8,128)(2,1)S(1)}, u32[]{:S(2)}, u32[]{:S(2)}) collective-permute-start(bf16[272,128]{1,0:T(8,128)(2,1)} %get-tuple-element.10), channel_id=1, source_target_pairs={{0,16},{2,18},{4,20},{6,22},{8,24},{10,26},{12,28},{14,30},{16,0},... | collective-permute-start | bytes 208904 | tf_op jit(solution)/shard_map/ppermute | solution.py:271
  8.4 1.1 %collective-permute-start.2 = (bf16[272,128]{1,0:T(8,128)(2,1)}, bf16[272,128]{1,0:T(8,128)(2,1)S(1)}, u32[]{:S(2)}, u32[]{:S(2)}) collective-permute-start(bf16[272,128]{1,0:T(8,128)(2,1)} %get-tuple-element.10), channel_id=1, source_target_pairs={{0,24},{2,26},{4,28},{6,30},{8,0},{10,2},{12,4},{14,6},{16,8},{18,... | collective-permute-start | bytes 208904 | tf_op jit(solution)/shard_map/ppermute | solution.py:271
  9.5 1.2 %collective-permute-start.5 = (bf16[8,48,128]{2,1,0:T(8,128)(2,1)}, bf16[8,48,128]{2,1,0:T(8,128)(2,1)S(1)}, u32[]{:S(2)}, u32[]{:S(2)}) collective-permute-start(bf16[8,48,128]{2,1,0:T(8,128)(2,1)} %get-tuple-element.11), channel_id=1, source_target_pairs={{0,1},{1,0},{2,3},{3,2},{4,5},{5,4},{6,7},{7,6},{8,9},{9,8},{10,11... | collective-permute-start | bytes 294920 | tf_op jit(solution)/shard_map/ppermute | solution.py:264
  10.7 0.0 copy-start.9
  10.8 0.9 copy-done.9
  11.6 0.0 copy-start.4
  11.7 0.9 copy-done.4
  12.5 0.0 collective-permute-done
  12.5 1.4 %collective-permute-done.1 = bf16[272,128]{1,0:T(8,128)(2,1)S(1)} collective-permute-done((bf16[272,128]{1,0:T(8,128)(2,1)}, bf16[272,128]{1,0:T(8,128)(2,1)S(1)}, u32[]{:S(2)}, u32[]{:S(2)}) %collective-permute-start.1) | collective-permute-done | bytes 69664 | tf_op jit(solution)/shard_map/ppermute | solution.py:271
  14.0 0.0 collective-permute-done.2
  14.0 1.1 %collective-permute-start.3 = (bf16[4,272,128]{2,1,0:T(8,128)(2,1)S(1)}, bf16[4,272,128]{2,1,0:T(8,128)(2,1)S(1)}, u32[]{:S(2)}, u32[]{:S(2)}) collective-permute-start(bf16[4,272,128]{2,1,0:T(8,128)(2,1)S(1)} %pad_maximum_fusion), channel_id=1, source_target_pairs={{0,4},{2,6},{4,0},{6,2},{8,12},{10,14},{12,8},{14,10},{16,20},{18,... | collective-permute-start | bytes 835592 | tf_op jit(solution)/shard_map/ppermute | solution.py:274
  15.1 0.0 collective-permute-done.5
  15.2 0.0 copy-start.1
  15.2 1.8 %collective-permute-start.6 = (bf16[2,2,48,128]{3,2,1,0:T(8,128)(2,1)S(1)}, bf16[2,2,48,128]{3,2,1,0:T(8,128)(2,1)S(1)}, u32[]{:S(2)}, u32[]{:S(2)}) collective-permute-start(bf16[2,2,48,128]{3,2,1,0:T(8,128)(2,1)S(1)} %get-tuple-element.22), channel_id=1, source_target_pairs={{0,8},{2,10},{4,12},{6,14},{8,16},{10,18},{12,20},{14,22},{16,24},... | collective-permute-start | bytes 147464 | tf_op jit(solution)/shard_map/ppermute | solution.py:281
  17.0 0.0 collective-permute-start.7
  17.0 2.2 %collective-permute-start.8 = (bf16[2,2,48,128]{3,2,1,0:T(8,128)(2,1)S(1)}, bf16[2,2,48,128]{3,2,1,0:T(8,128)(2,1)S(1)}, u32[]{:S(2)}, u32[]{:S(2)}) collective-permute-start(bf16[2,2,48,128]{3,2,1,0:T(8,128)(2,1)S(1)} %get-tuple-element.20), channel_id=1, source_target_pairs={{0,24},{2,26},{4,28},{6,30},{8,0},{10,2},{12,4},{14,6},{16,8},{18,... | collective-permute-start | bytes 147464 | tf_op jit(solution)/shard_map/ppermute | solution.py:281
  19.2 0.8 collective-permute-done.6
  20.0 1.2 %collective-permute-done.7 = bf16[2,2,48,128]{3,2,1,0:T(8,128)(2,1)S(1)} collective-permute-done((bf16[2,2,48,128]{3,2,1,0:T(8,128)(2,1)S(1)}, bf16[2,2,48,128]{3,2,1,0:T(8,128)(2,1)S(1)}, u32[]{:S(2)}, u32[]{:S(2)}) %collective-permute-start.7) | collective-permute-done | bytes 49184 | tf_op jit(solution)/shard_map/ppermute | solution.py:281
  21.2 0.0 collective-permute-done.8
  21.2 0.2 collective-permute-done.3
  21.5 0.0 copy-start.2
  21.5 3.2 %collective-permute-start.4 = (bf16[8,272,128]{2,1,0:T(8,128)(2,1)S(1)}, bf16[8,272,128]{2,1,0:T(8,128)(2,1)S(1)}, u32[]{:S(2)}, u32[]{:S(2)}) collective-permute-start(bf16[8,272,128]{2,1,0:T(8,128)(2,1)S(1)} %constant_dynamic-update-slice_fusion.right0_ref), channel_id=1, source_target_pairs={{0,2},{2,0},{4,6},{6,4},{8,10},{10,8},{12,14},{14,12},{16,18},{18,... | collective-permute-start | bytes 1671176 | tf_op jit(solution)/shard_map/ppermute | solution.py:284
  24.7 0.4 collective-permute-start.9
  25.1 0.0 copy-done.1
  25.1 0.0 copy-start.5
  25.1 1.3 %copy.36 = f32[16,128,128]{1,2,0:T(8,128)} copy(f32[16,128,128]{2,1,0:T(8,128)S(1)} %copy-done.1) | data formatting | bytes 2097152 | tf_op args[3]
  26.4 0.0 copy-done.2
  26.4 0.0 copy-done.5
  26.4 0.1 copy.37
  26.5 0.0 copy-start.10
  26.6 0.9 copy.41.wo_ref
  27.4 0.0 copy-done.10
  27.4 0.0 copy-start.11
  27.4 0.1 copy.38
  27.5 0.7 copy-done.11
  28.3 0.0 copy-start.12
  28.3 0.1 copy.39
  28.4 0.6 copy-done.12
  29.0 0.1 copy.40
  29.2 0.0 collective-permute-done.9
  29.2 0.7 dynamic-slice_bitcast_fusion
  29.9 0.8 collective-permute-start.10
  30.7 0.7 maximum_bitcast_fusion.wp_ref
  31.4 0.3 collective-permute-done.10.left1_ref
  31.6 0.0 copy-start.8
  31.6 0.0 collective-permute-done.4.right1_ref
  31.6 0.6 copy-done.8
  32.3 0.2 copy-done.3
  32.5 6.8 %pair.1 = (f32[16,128,128]{2,1,0:T(8,128)}, f32[16,128,128]{2,1,0:T(8,128)}, bf16[128,2,16,128]{3,2,1,0:T(8,128)(2,1)}) custom-call(bf16[8,272,128]{2,1,0:T(8,128)(2,1)} %copy-done.2, bf16[8,272,128]{2,1,0:T(8,128)(2,1)} %copy-done.3, bf16[8,48,128]{2,1,0:T(8,128)(2,1)} %get-tuple-element.16.left0_ref, bf16[8,48,128]{2,1,0:T(8,128)(2,1)} %copy-done.8, ...), custom_call_target="tpu_custom_call" | custom-call | tf_op jit(solution)/shard_map/pair/pallas_call | solution.py:32
  39.3 30.0 %all_to_all.10.recv_ref = bf16[32,4,2,16,128]{4,3,2,1,0:T(8,128)(2,1)} all-to-all(bf16[32,4,2,16,128]{4,3,2,1,0:T(8,128)(2,1)} %bitcast.51), channel_id=1, replica_groups=mesh['crops'=1,'rows'=16,'cols'=2] {'rows','cols'}, dimensions={0} | all-to-all | bytes 2097152 | tf_op jit(solution)/shard_map/all_to_all | solution.py:306
  69.4 2.4 %triangle.1 = bf16[32,4,16,128]{3,2,1,0:T(8,128)(2,1)} custom-call(bf16[32,4,2,16,128]{4,3,2,1,0:T(8,128)(2,1)} %all_to_all.10.recv_ref), custom_call_target="tpu_custom_call" | custom-call | tf_op jit(solution)/shard_map/triangle/pallas_call | solution.py:32
  71.7 3.8 %all-to-all-start.1 = ((bf16[32,4,16,128]{3,2,1,0:T(8,128)(2,1)}), bf16[32,4,16,128]{3,2,1,0:T(8,128)(2,1)S(1)}, u32[]{:S(2)}, u32[]{:S(2)}) async-start(bf16[32,4,16,128]{3,2,1,0:T(8,128)(2,1)} %triangle.1), calls=%async_computation.1 | async-start | bytes 1048576 | tf_op jit(solution)/shard_map/all_to_all | solution.py:316
  75.5 0.0 copy-done.6
  75.5 0.0 copy-start.7
  75.5 0.8 copy.43
  76.3 0.1 copy-done.7
  76.4 0.8 copy.44
  77.2 0.0 copy-done.13
  77.2 0.7 copy.42
  77.9 13.5 %all-to-all-done.1 = bf16[32,4,16,128]{3,2,1,0:T(8,128)(2,1)S(1)} async-done(((bf16[32,4,16,128]{3,2,1,0:T(8,128)(2,1)}), bf16[32,4,16,128]{3,2,1,0:T(8,128)(2,1)S(1)}, u32[]{:S(2)}, u32[]{:S(2)}) %all-to-all-start.1) | async-done | bytes 524320 | tf_op jit(solution)/shard_map/all_to_all | solution.py:316
  91.3 0.8 copy-done
  92.2 7.3 %finish.1 = f32[16,128,128]{2,1,0:T(8,128)} custom-call(bf16[128,16,128]{2,1,0:T(8,128)(2,1)} %bitcast.50, f32[16,128,128]{2,1,0:T(8,128)} %get-tuple-element.13.first_ref, f32[16,128,128]{2,1,0:T(8,128)} %get-tuple-element.14.gate_ref, bf16[128,128]{1,0:T(8,128)(2,1)} %bitcast.63, bf16[512,128]{1,0:T(8,128)(2,1)} %bitcast.55, bf16[128,512]{1,0:T(8,128)(2,1)} %bitcast.56), custom_call_target="tpu_custom_call" | custom-call | tf_op jit(solution)/shard_map/finish/pallas_call | solution.py:32
  (19 shorter events, 0.3 us)
Async XLA Ops:
  4.0 8.5 %collective-permute-start = (bf16[272,128]{1,0:T(8,128)(2,1)}, bf16[272,128]{1,0:T(8,128)(2,1)S(1)}, u32[]{:S(2)}, u32[]{:S(2)}) collective-permute-start(bf16[272,128]{1,0:T(8,128)(2,1)} %get-tuple-element.10), channel_id=1, source_target_pairs={{0,8},{2,10},{4,12},{6,14},{8,16},{10,18},{12,20},{14,22},{16,24},... | collective-permute-start | bytes 208904 | tf_op jit(solution)/shard_map/ppermute | solution.py:271
  6.1 7.8 %collective-permute-start.1 = (bf16[272,128]{1,0:T(8,128)(2,1)}, bf16[272,128]{1,0:T(8,128)(2,1)S(1)}, u32[]{:S(2)}, u32[]{:S(2)}) collective-permute-start(bf16[272,128]{1,0:T(8,128)(2,1)} %get-tuple-element.10), channel_id=1, source_target_pairs={{0,16},{2,18},{4,20},{6,22},{8,24},{10,26},{12,28},{14,30},{16,0},... | collective-permute-start | bytes 208904 | tf_op jit(solution)/shard_map/ppermute | solution.py:271
  8.4 5.5 %collective-permute-start.2 = (bf16[272,128]{1,0:T(8,128)(2,1)}, bf16[272,128]{1,0:T(8,128)(2,1)S(1)}, u32[]{:S(2)}, u32[]{:S(2)}) collective-permute-start(bf16[272,128]{1,0:T(8,128)(2,1)} %get-tuple-element.10), channel_id=1, source_target_pairs={{0,24},{2,26},{4,28},{6,30},{8,0},{10,2},{12,4},{14,6},{16,8},{18,... | collective-permute-start | bytes 208904 | tf_op jit(solution)/shard_map/ppermute | solution.py:271
  9.5 5.6 %collective-permute-start.5 = (bf16[8,48,128]{2,1,0:T(8,128)(2,1)}, bf16[8,48,128]{2,1,0:T(8,128)(2,1)S(1)}, u32[]{:S(2)}, u32[]{:S(2)}) collective-permute-start(bf16[8,48,128]{2,1,0:T(8,128)(2,1)} %get-tuple-element.11), channel_id=1, source_target_pairs={{0,1},{1,0},{2,3},{3,2},{4,5},{5,4},{6,7},{7,6},{8,9},{9,8},{10,11... | collective-permute-start | bytes 294920 | tf_op jit(solution)/shard_map/ppermute | solution.py:264
  10.7 0.9 copy-start.9
  11.6 0.9 copy-start.4
  14.0 7.4 %collective-permute-start.3 = (bf16[4,272,128]{2,1,0:T(8,128)(2,1)S(1)}, bf16[4,272,128]{2,1,0:T(8,128)(2,1)S(1)}, u32[]{:S(2)}, u32[]{:S(2)}) collective-permute-start(bf16[4,272,128]{2,1,0:T(8,128)(2,1)S(1)} %pad_maximum_fusion), channel_id=1, source_target_pairs={{0,4},{2,6},{4,0},{6,2},{8,12},{10,14},{12,8},{14,10},{16,20},{18,... | collective-permute-start | bytes 835592 | tf_op jit(solution)/shard_map/ppermute | solution.py:274
  15.2 9.9 %copy-start.1 = (f32[16,128,128]{2,1,0:T(8,128)S(1)}, f32[16,128,128]{2,1,0:T(8,128)}, u32[]{:S(2)}) copy-start(f32[16,128,128]{2,1,0:T(8,128)} %param.16) | copy-start | bytes 3145732
  15.2 4.8 %collective-permute-start.6 = (bf16[2,2,48,128]{3,2,1,0:T(8,128)(2,1)S(1)}, bf16[2,2,48,128]{3,2,1,0:T(8,128)(2,1)S(1)}, u32[]{:S(2)}, u32[]{:S(2)}) collective-permute-start(bf16[2,2,48,128]{3,2,1,0:T(8,128)(2,1)S(1)} %get-tuple-element.22), channel_id=1, source_target_pairs={{0,8},{2,10},{4,12},{6,14},{8,16},{10,18},{12,20},{14,22},{16,24},... | collective-permute-start | bytes 147464 | tf_op jit(solution)/shard_map/ppermute | solution.py:281
  17.0 4.2 %collective-permute-start.7 = (bf16[2,2,48,128]{3,2,1,0:T(8,128)(2,1)S(1)}, bf16[2,2,48,128]{3,2,1,0:T(8,128)(2,1)S(1)}, u32[]{:S(2)}, u32[]{:S(2)}) collective-permute-start(bf16[2,2,48,128]{3,2,1,0:T(8,128)(2,1)S(1)} %get-tuple-element.21), channel_id=1, source_target_pairs={{0,16},{2,18},{4,20},{6,22},{8,24},{10,26},{12,28},{14,30},{16,0},... | collective-permute-start | bytes 147464 | tf_op jit(solution)/shard_map/ppermute | solution.py:281
  17.0 4.2 %collective-permute-start.8 = (bf16[2,2,48,128]{3,2,1,0:T(8,128)(2,1)S(1)}, bf16[2,2,48,128]{3,2,1,0:T(8,128)(2,1)S(1)}, u32[]{:S(2)}, u32[]{:S(2)}) collective-permute-start(bf16[2,2,48,128]{3,2,1,0:T(8,128)(2,1)S(1)} %get-tuple-element.20), channel_id=1, source_target_pairs={{0,24},{2,26},{4,28},{6,30},{8,0},{10,2},{12,4},{14,6},{16,8},{18,... | collective-permute-start | bytes 147464 | tf_op jit(solution)/shard_map/ppermute | solution.py:281
  21.5 4.9 %copy-start.2 = (bf16[8,272,128]{2,1,0:T(8,128)(2,1)}, bf16[8,272,128]{2,1,0:T(8,128)(2,1)S(1)}, u32[]{:S(2)}) copy-start(bf16[8,272,128]{2,1,0:T(8,128)(2,1)S(1)} %constant_dynamic-update-slice_fusion.right0_ref) | copy-start | bytes 1671172
  21.5 10.1 %collective-permute-start.4 = (bf16[8,272,128]{2,1,0:T(8,128)(2,1)S(1)}, bf16[8,272,128]{2,1,0:T(8,128)(2,1)S(1)}, u32[]{:S(2)}, u32[]{:S(2)}) collective-permute-start(bf16[8,272,128]{2,1,0:T(8,128)(2,1)S(1)} %constant_dynamic-update-slice_fusion.right0_ref), channel_id=1, source_target_pairs={{0,2},{2,0},{4,6},{6,4},{8,10},{10,8},{12,14},{14,12},{16,18},{18,... | collective-permute-start | bytes 1671176 | tf_op jit(solution)/shard_map/ppermute | solution.py:284
  24.7 4.4 %collective-permute-start.9 = (bf16[4,2,48,128]{3,2,0,1:T(8,128)(2,1)S(1)}, bf16[4,2,48,128]{3,2,0,1:T(8,128)(2,1)S(1)}, u32[]{:S(2)}, u32[]{:S(2)}) collective-permute-start(bf16[4,2,48,128]{3,2,0,1:T(8,128)(2,1)S(1)} %bitcast.64), channel_id=1, source_target_pairs={{0,4},{2,6},{4,0},{6,2},{8,12},{10,14},{12,8},{14,10},{16,20},{18,... | collective-permute-start | bytes 294920 | tf_op jit(solution)/shard_map/ppermute | solution.py:286
  25.1 1.3 %copy-start.5 = (bf16[1024,128]{1,0:T(8,128)(2,1)S(1)}, bf16[1024,128]{1,0:T(8,128)(2,1)}, u32[]{:S(2)}) copy-start(bf16[1024,128]{1,0:T(8,128)(2,1)} %param.19) | copy-start | bytes 786436
  26.5 0.9 copy-start.10
  27.4 0.8 copy-start.11
  28.3 0.8 copy-start.12
  29.9 1.8 %collective-permute-start.10 = (bf16[8,48,128]{2,1,0:T(8,128)(2,1)S(1)}, bf16[8,48,128]{2,1,0:T(8,128)(2,1)S(1)}, u32[]{:S(2)}, u32[]{:S(2)}) collective-permute-start(bf16[8,48,128]{2,1,0:T(8,128)(2,1)S(1)} %get-tuple-element.15), channel_id=1, source_target_pairs={{0,2},{2,0},{4,6},{6,4},{8,10},{10,8},{12,14},{14,12},{16,18},{18,... | collective-permute-start | bytes 294920 | tf_op jit(solution)/shard_map/ppermute | solution.py:289
  31.6 0.6 copy-start.8
  31.6 0.8 copy-start.3
  71.7 3.8 %copy-start.6 = (bf16[128,512]{1,0:T(8,128)(2,1)S(1)}, bf16[128,512]{1,0:T(8,128)(2,1)}, u32[]{:S(2)}) copy-start(bf16[128,512]{1,0:T(8,128)(2,1)} %param.24) | copy-start | bytes 393220
  71.7 19.6 %all-to-all-start.1 = ((bf16[32,4,16,128]{3,2,1,0:T(8,128)(2,1)}), bf16[32,4,16,128]{3,2,1,0:T(8,128)(2,1)S(1)}, u32[]{:S(2)}, u32[]{:S(2)}) async-start(bf16[32,4,16,128]{3,2,1,0:T(8,128)(2,1)} %triangle.1), calls=%async_computation.1 | async-start | bytes 1048576 | tf_op jit(solution)/shard_map/all_to_all | solution.py:316
  75.5 0.9 copy-start.7
  76.4 0.8 copy-start.13
  91.3 0.8 copy-start

commit v3 on v1

--- a/solution.py
+++ b/solution.py
@@ -12,6 +12,7 @@
 BF16 = jnp.bfloat16
 TILE = 16
 LANES = 128
+VMEM_LIMIT = 32 * 2**20
 VMEM = pl.BlockSpec(memory_space=pltpu.VMEM)
 
 
@@ -27,14 +28,18 @@
     return 0.5 * jnp.tanh(0.5 * x) + 0.5
 
 
-def call(kernel, out_shape, scratch, name):
+def call(kernel, out_shape, scratch, name, ins=(), out_specs=None):
     def run(*args):
+        args = [
+            pltpu.with_memory_space_constraint(x, pltpu.VMEM) if k in ins else x for k, x in enumerate(args)
+        ]
         return pl.pallas_call(
             kernel,
             out_shape=out_shape,
             in_specs=[VMEM] * len(args),
-            out_specs=jax.tree.map(lambda _: VMEM, out_shape),
+            out_specs=out_specs or jax.tree.map(lambda _: VMEM, out_shape),
             scratch_shapes=scratch,
+            compiler_params=pltpu.CompilerParams(vmem_limit_bytes=VMEM_LIMIT),
             name=name,
         )(*args)
 
@@ -43,11 +48,11 @@
 
 def project_kernel(fam_ref, keep_ref, pres_ref, wl_ref, wr_ref, right_ref, left_ref, nf, rs, *, tile_rows):
     seqs, cols, feats = fam_ref.shape
-    chans = wl_ref.shape[1]
+    chans = wl_ref.shape[0]
     col = lax.axis_index("cols")
     live = (keep_ref[...] * pres_ref[pl.ds(col, 1), :]).astype(F32)
     live_t = jnp.concatenate([live, jnp.zeros((LANES - seqs, cols), F32)], 0).T
-    wr_t = wr_ref[...].astype(F32).T.astype(BF16)
+    wr_t = wr_ref[...]
     for s in range(seqs):
         v = fam_ref[s]
         centred = v - jnp.mean(v, -1, keepdims=True)
@@ -62,7 +67,7 @@
     per = LANES // chans
     groups = tile_rows // per
     pieces = cols // tile_rows
-    wl = wl_ref[...].astype(F32)
+    wl = wl_ref[...].astype(F32).T
     acc = None
     for i4 in range(per):
         parts = []
@@ -81,21 +86,45 @@
         part = dot(jnp.concatenate(rows, 0).astype(BF16), w)
         acc = part if acc is None else acc + part
     block = groups * seqs
+    planes = left_ref.shape[0]
+    row = lax.axis_index("rows")
+    z, y, c = lax.div(row, 4), lax.rem(lax.div(row, 2), 2), lax.rem(row, 2)
     for p in range(pieces):
-        left_ref[p, 0:block, :] = acc[p * block : (p + 1) * block].astype(BF16)
-        left_ref[p, block : block + TILE, :] = live_tile
-
-
-def pair_kernel(
-    right0_ref, right1_ref, left_ref, contact_ref, pres_ref, wo_ref, wp_ref,
-    first_ref, gate_ref, panel_ref,
-    o_scr, cnt_scr, pan_scr,
-    *, seqs, radix, tile_rows, chans,
-):
-    tiles = right0_ref.shape[1] // TILE - 1
-    half = right0_ref.shape[0]
-    blocks = 2 * half
-    cols = right0_ref.shape[2]
+        at = (
+            lax.rem(p // 4 + planes - lax.rem(z, planes), planes),
+            lax.rem((p // 2) % 2 + y, 2),
+            lax.rem(p % 2 + c, 2),
+        )
+        left_ref[at[0], at[1], at[2], 0:block, :] = acc[p * block : (p + 1) * block].astype(BF16)
+        left_ref[at[0], at[1], at[2], block : block + TILE, :] = live_tile
+
+
+def prepare_kernel(contact_ref, wo_ref, src_ref, tgt_ref, gate_ref, after_ref, contact_t_ref, wo_t_ref, wp_t_ref, scr):
+    tile_rows = contact_ref.shape[0]
+    rows = wo_ref.shape[0]
+    chans = int(rows**0.5)
+    for i in range(tile_rows):
+        contact_t_ref[i] = contact_ref[i].T
+    scr[...] = wo_ref[...].astype(F32)
+    for at in range(0, rows, LANES):
+        part = jnp.concatenate(
+            [scr[pl.ds(d, chans, stride=chans), :] for d in range(at // chans, (at + LANES) // chans)], 0
+        )
+        wo_t_ref[:, at : at + LANES] = part.T.astype(BF16)
+    at = 0
+    for ref in (src_ref, tgt_ref, gate_ref):
+        wp_t_ref[at : at + ref.shape[1], :] = ref[...].astype(F32).T.astype(BF16)
+        at += ref.shape[1]
+
+
+def pair_kernel(*refs, seqs, radix, tile_rows, chans):
+    z_refs, refs = refs[:radix], refs[radix:]
+    (y_ref, c_ref, left_ref, contact_ref, pres_ref, wo_ref, wp_ref,
+     first_ref, gate_ref, panel_ref, o_scr, cnt_scr, pan_scr) = refs
+    right_rows, cols = z_refs[0].shape
+    left_rows = left_ref.shape[3]
+    tiles = right_rows // TILE - 1
+    blocks = 4 * radix
     feats = first_ref.shape[1]
     width = pan_scr.shape[1] // tile_rows
     pack = TILE // seqs
@@ -103,17 +132,32 @@
     groups = tile_rows // per
     row = lax.axis_index("rows")
     col = lax.axis_index("cols")
-    z, y, c = row // 4, (row // 2) % 2, row % 2
-
-    def source(b):
-        cz, cy, cc = b % radix, (b // radix) % 2, b // (2 * radix)
-        return lax.rem(z + radix - cz, radix) * 4 + (y ^ cy) * 2 + (c ^ cc)
+    z = lax.div(row, 4)
+    planes = cols // tile_rows // 4
+    turn = col * planes + lax.rem(z, planes) - z + radix
 
     def right(b, t):
-        ref = right0_ref if b < half else right1_ref
-        return ref[b % half, t * TILE : (t + 1) * TILE, :]
-
-    lefts = [left_ref[source(b)].astype(F32) for b in range(blocks)]
+        core, pair, k = b // (2 * radix), b // radix % 2, b % radix
+        if core:
+            ref, at = c_ref, (pair * radix + k) * right_rows
+        elif pair:
+            ref, at = y_ref, k * right_rows
+        else:
+            ref, at = z_refs[k], 0
+        return ref[at + t * TILE : at + (t + 1) * TILE, :]
+
+    def left(b):
+        core, pair, k = b // (2 * radix), b // radix % 2, b % radix
+        m = lax.rem(turn + k, radix)
+        if not core and not pair:
+            return left_ref[m, 0, 0]
+        if core:
+            ref, at = c_ref, 2 * radix * right_rows + (pair * radix + m) * left_rows
+        else:
+            ref, at = y_ref, radix * right_rows + 2 * m * left_rows
+        return ref[pl.ds(pl.multiple_of(at, TILE), left_rows), :]
+
+    lefts = [left(b).astype(F32) for b in range(blocks)]
     block = groups * seqs
     live_l = jnp.concatenate([v[block : block + seqs] for v in lefts], 0).T.astype(BF16)
     live_r = jnp.concatenate([right(b, tiles).astype(F32)[:seqs] for b in range(blocks)], 0).astype(BF16)
@@ -194,7 +238,7 @@
                 ]
 
 
-def finish_kernel(prod_ref, first_ref, gate_ref, we_ref, w1_ref, w2_ref, out_ref, mix):
+def finish_kernel(prod_ref, first_ref, gate_ref, we_ref, w1_ref, w2_ref, hbm_ref, mix, out_ref, sems):
     chans, tile_rows, cols = prod_ref.shape
     total = jnp.zeros((tile_rows, cols), F32)
     for ch in range(chans):
@@ -208,6 +252,7 @@
     for ch in range(chans):
         mix[ch * tile_rows : (ch + 1) * tile_rows, :] = (prod_ref[ch].astype(F32) - mean) * scale
     w_e, w_1, w_2 = we_ref[...], w1_ref[...], w2_ref[...]
+    copies = []
     for i in range(0, tile_rows, 2):
         mixed = jnp.concatenate(
             [mix[pl.ds(i + k, chans, stride=tile_rows), :].astype(BF16) for k in range(2)], 1
@@ -224,6 +269,11 @@
         out = dot(w_2, hidden)
         for k in range(2):
             out_ref[i + k] = (seconds[k] + out[:, k * cols : (k + 1) * cols]).T
+        copy = pltpu.make_async_copy(out_ref.at[pl.ds(i, 2)], hbm_ref.at[pl.ds(i, 2)], sems.at[i // 2])
+        copy.start()
+        copies.append(copy)
+    for copy in copies:
+        copy.wait()
 
 
 def on_device(
@@ -252,37 +302,59 @@
     pieces = cols // tile_rows
     col = lax.axis_index("cols")
     presence = amino_presence.reshape(n_cols, cols)
-    shape = jax.ShapeDtypeStruct
+    shape = pltpu.VMEM
+    planes = pieces // 4
 
     right_rows = chans * seqs + TILE
     left_rows = tile_rows * chans * seqs // LANES + TILE
     right, left = call(
         functools.partial(project_kernel, tile_rows=tile_rows),
-        (shape((right_rows, cols), BF16), shape((pieces, left_rows, LANES), BF16)),
+        (shape((right_rows, cols), BF16), shape((planes, 2, 2, left_rows, LANES), BF16)),
         [pltpu.VMEM((feats // LANES, seqs * cols, LANES), F32), pltpu.VMEM((chans * seqs, cols), F32)],
         "project",
-    )(family_representation, family_keep_flags, presence, couple_lhs_weights, couple_rhs_weights)
-
-    left_wide = jnp.zeros((n_cols, pieces, left_rows, LANES), BF16)
-    left_wide = lax.dynamic_update_slice_in_dim(left_wide, left[None], col, 0)
-    for k in range(1, n_cols):
-        got = lax.ppermute(left, "cols", [(i, (i + k) % n_cols) for i in range(n_cols)])
-        left_wide = lax.dynamic_update_slice_in_dim(left_wide, got[None], (col + n_cols - k) % n_cols, 0)
-    blocks = [right]
+    )(family_representation, family_keep_flags, presence, couple_lhs_weights.T, couple_rhs_weights.T)
+
+    zs = [right]
     for k in range(1, radix):
-        blocks.append(lax.ppermute(right, "rows", [(i, (i + 4 * k) % n_rows) for i in range(n_rows)]))
-    right_z = jnp.stack(blocks)
-    right_y = lax.ppermute(right_z, "rows", [(i, i ^ 2) for i in range(n_rows)])
-    left_all = lax.all_to_all(
-        left_wide.reshape(n_rows, left_rows, LANES), "rows", split_axis=0, concat_axis=0, tiled=True
+        zs.append(lax.ppermute(right, "rows", [(i, (i + 4 * k) % n_rows) for i in range(n_rows)]))
+    lefts = []
+    for m in range(radix):
+        perm = []
+        for i in range(n_rows):
+            for x in range(n_cols):
+                to = (i // 4 + m) % radix
+                target = (x * planes + to % planes) * 4 + i % 4
+                perm.append((i * n_cols + x, target * n_cols + to // planes))
+        lefts.append(lax.ppermute(left[m % planes], ("rows", "cols"), perm))
+    lefts = jnp.stack(lefts)
+
+    def rows_of(array):
+        return array.reshape(-1, LANES)
+
+    y_msg = jnp.concatenate(zs + [rows_of(lefts[:, 1])], 0)
+    y_got = lax.ppermute(y_msg, "rows", [(i, i ^ 2) for i in range(n_rows)])
+    cut = radix * right_rows
+    c_msg = jnp.concatenate(
+        zs + [
+            y_got[:cut],
+            rows_of(lefts[:, 0, 1]),
+            rows_of(y_got[cut:].reshape(radix, 2, left_rows, LANES)[:, 1]),
+        ], 0
     )
-    right0 = jnp.concatenate([right_z, right_y], 0)
-    right1 = lax.ppermute(right0, "rows", [(i, i ^ 1) for i in range(n_rows)])
-
-    contact_t = contact_embedding.transpose(0, 2, 1)
-    w_o = pairwise_final_matrix.reshape(chans, chans, pair_feats).transpose(2, 1, 0).reshape(pair_feats, chans * chans)
-    w_p = jnp.concatenate([edge_source_matrix, edge_target_matrix, edge_final_sigmoid_matrix], 1).T
+    c_got = lax.ppermute(c_msg, "rows", [(i, i ^ 1) for i in range(n_rows)])
+
     pair = shape((tile_rows, pair_feats, cols), F32)
+    contact_t, w_o, w_p = call(
+        prepare_kernel,
+        (pair, shape((pair_feats, chans * chans), BF16), shape((4 * width + pair_feats, pair_feats), BF16)),
+        [pltpu.VMEM((chans * chans, pair_feats), F32)],
+        "prepare",
+        ins=(5,),
+    )(
+        contact_embedding, pairwise_final_matrix, edge_source_matrix, edge_target_matrix,
+        edge_final_sigmoid_matrix, zs[-1],
+    )
+    args = zs + [y_got, c_got, lefts, contact_t, presence, w_o, w_p]
     first, gate, panels = call(
         functools.partial(pair_kernel, seqs=seqs, radix=radix, tile_rows=tile_rows, chans=chans),
         (pair, pair, shape((width, 2, tile_rows, cols), BF16)),
@@ -292,7 +364,8 @@
             pltpu.VMEM((2, width * tile_rows, cols), F32),
         ],
         "pair",
-    )(right0, right1, left_all, contact_t, presence, w_o, w_p)
+        ins=[k for k in range(len(args)) if k != len(args) - 3],
+    )(*args)
 
     panels = lax.all_to_all(
         panels.reshape(devices, width // devices, 2, tile_rows, cols),
@@ -303,13 +376,20 @@
         shape((devices, width // devices, tile_rows, cols), BF16),
         [],
         "triangle",
+        ins=(0,),
     )(panels)
     product = lax.all_to_all(product, ("rows", "cols"), split_axis=0, concat_axis=0, tiled=True)
     return call(
         finish_kernel,
-        shape((tile_rows, cols, pair_feats), F32),
-        [pltpu.VMEM((width * tile_rows, cols), F32)],
+        jax.ShapeDtypeStruct((tile_rows, cols, pair_feats), F32),
+        [
+            pltpu.VMEM((width * tile_rows, cols), F32),
+            pltpu.VMEM((tile_rows, cols, pair_feats), F32),
+            pltpu.SemaphoreType.DMA((tile_rows // 2,)),
+        ],
         "finish",
+        ins=(0, 1, 2, 3, 4, 5),
+        out_specs=pl.BlockSpec(memory_space=pl.ANY),
     )(
         product.reshape(width, tile_rows, cols), first, gate,
         edge_final_matrix.T, feedforward_expand_matrix.T, feedforward_shrink_matrix.T,

time: 107 us -> 103 us (0.963)
  Pallas kernels: 20.3 us -> 13.1 us
  starting transfers between devices: 17.4 us -> 23.8 us
  local copies, waits for them, and re-layouts: 12.8 us -> 6.94 us
  blocking collectives: 29.9 us -> 33.5 us
    ppermute x3 -> x6, starting transfers between devices: 4.06 us -> 12.2 us  [the longest x4 7.57 us: on_device(): lefts.append(lax.ppermute(left[m % planes], ('rows', 'cols'), perm))]
    pallas_call x4 -> x5, Pallas kernels: 20.3 us -> 13.1 us  [run(): pl.pallas_call(kernel, out_shape=out_shape, in_specs=[VMEM] * len(args),...]
    all_to_all x1 -> x0, starting transfers between devices: 4.19 us -> none  [on_device(): lax.all_to_all(left_wide.reshape(n_rows, left_rows, LANES), 'rows', split...]
    unnamed x43 -> x39, local copies, waits for them, and re-layouts: 9.79 us -> 5.95 us
    all_to_all x1, blocking collectives: 29.9 us -> 33.5 us  [on_device(): lax.all_to_all(panels.reshape(devices, width // devices, 2, tile_rows, co...]
    all_to_all x1 -> x0, waiting for transfers between devices: 3.55 us -> none  [on_device(): lax.all_to_all(left_wide.reshape(n_rows, left_rows, LANES), 'rows', split...]
    ppermute x3, starting transfers between devices: 5.49 us -> 7.84 us  [on_device(): lax.ppermute(right, 'rows', [(i, (i + 4 * k) % n_rows) for i in range(n_r...]
    ppermute x3 -> x6, waiting for transfers between devices: 6.31 us -> 8.03 us  [the longest x1 6.65 us: on_device(): y_got = lax.ppermute(y_msg, 'rows', [(i, i ^ 2) for i in range(n_rows)])]
  transfers between devices with their start and end apart: 8 -> 10, of which waited for: 4 -> 5; matrix products, arithmetic and copies ran while one was open for 7% -> 0% of each run, Pallas kernels for 0% -> 1%
where the time goes in v3:
time: 103 us; the launch traced here: 102 us
  blocking collectives  33.5 us (33%)
  waiting for transfers between devices  24.4 us (24%)
  starting transfers between devices  23.8 us (23%)
  Pallas kernels  13.1 us (13%)
  local copies, waits for them, and re-layouts  6.94 us (7%)
    all_to_all x1, blocking collectives, on_device(): lax.all_to_all(panels.reshape(devices, width // devices, 2, tile_rows, co...  33.5 us
    all_to_all x1, waiting for transfers between devices, on_device(): lax.all_to_all(product, ('rows', 'cols'), split_axis=0, concat_axis=0, ti...  14.1 us
    pallas_call x5, Pallas kernels, run(): pl.pallas_call(kernel, out_shape=out_shape, in_specs=[VMEM] * len(args),...  13.1 us
    ppermute x3, starting transfers between devices, on_device(): lax.ppermute(right, 'rows', [(i, (i + 4 * k) % n_rows) for i in range(n_r...  7.84 us
    ppermute x4, starting transfers between devices, on_device(): lefts.append(lax.ppermute(left[m % planes], ('rows', 'cols'), perm))  7.57 us
    ppermute x1, waiting for transfers between devices, on_device(): y_got = lax.ppermute(y_msg, 'rows', [(i, i ^ 2) for i in range(n_rows)])  6.65 us
    unnamed x39, local copies, waits for them, and re-layouts  5.95 us
    all_to_all x1, starting transfers between devices, on_device(): lax.all_to_all(product, ('rows', 'cols'), split_axis=0, concat_axis=0, ti...  3.75 us
  transfers between devices with their start and end apart: 10, of which 5 were waited for; matrix products, arithmetic and copies ran while one was open for 0% of the time, Pallas kernels for 1%

profile of v3, /device:TPU:1, one launch (start us, length us, event | category | flops | bytes accessed | tf_op | source)
XLA Modules:
  0.0 102.1 jit_solution(5945961801659873817)
XLA Ops:
  0.0 0.0 copy-start.10
  0.0 0.0 copy-start.11
  0.0 0.7 copy-done.10
  0.7 0.0 copy-done.11
  0.7 0.0 copy-start.2
  0.7 1.2 %copy-done.2 = f32[8,128,256]{2,1,0:T(8,128)S(1)} copy-done((f32[8,128,256]{2,1,0:T(8,128)S(1)}, f32[8,128,256]{2,1,0:T(8,128)}, u32[]{:S(2)}) %copy-start.2) | copy-done | bytes 1048600
  1.9 0.0 copy-start.8
  1.9 0.7 copy-done.8
  2.6 0.0 copy-start.9
  2.6 0.7 copy-done.9
  3.4 2.2 %project.1 = (bf16[272,128]{1,0:T(8,128)(2,1)S(1)}, bf16[2,2,2,48,128]{4,3,2,1,0:T(8,128)(2,1)S(1)}) custom-call(f32[8,128,256]{2,1,0:T(8,128)S(1)} %copy-done.2, s32[8,128]{1,0:T(8,128)S(1)} %copy-done.10, s32[2,128]{1,0:T(2,128)S(1)} %bitcast.30, bf16[32,256]{1,0:T(8,128)(2,1)S(1)} %bitcast.28, bf16[32,256]{1,0:T(8,128)(2,1)S(1)} %bitcast.29), custom_call_target="tpu_custom_call" | custom-call | tf_op jit(solution)/shard_map/project/pallas_call | solution.py:36
  5.5 0.7 collective-permute-start.3
  6.2 5.6 %collective-permute-start.5 = (bf16[2,2,48,128]{3,2,1,0:T(8,128)(2,1)S(1)}, bf16[2,2,48,128]{3,2,1,0:T(8,128)(2,1)S(1)}, u32[]{:S(2)}, u32[]{:S(2)}) collective-permute-start(bf16[2,2,48,128]{3,2,1,0:T(8,128)(2,1)S(1)} %get-tuple-element.21), channel_id=1, source_target_pairs={{0,1},{1,17},{2,3},{3,19},{4,5},{5,21},{6,7},{7,23},{8,9},{9,25},{... | collective-permute-start | bytes 147464 | tf_op jit(solution)/shard_map/ppermute | solution.py:328
  11.8 1.3 %collective-permute-start.4 = (bf16[2,2,48,128]{3,2,1,0:T(8,128)(2,1)S(1)}, bf16[2,2,48,128]{3,2,1,0:T(8,128)(2,1)S(1)}, u32[]{:S(2)}, u32[]{:S(2)}) collective-permute-start(bf16[2,2,48,128]{3,2,1,0:T(8,128)(2,1)S(1)} %get-tuple-element.22), channel_id=1, source_target_pairs={{0,8},{1,24},{2,10},{3,26},{4,12},{5,28},{6,14},{7,30},{8,1},{9,17... | collective-permute-start | bytes 147464 | tf_op jit(solution)/shard_map/ppermute | solution.py:328
  13.1 0.0 collective-permute-start.6
  13.1 1.5 %collective-permute-start = (bf16[272,128]{1,0:T(8,128)(2,1)S(1)}, bf16[272,128]{1,0:T(8,128)(2,1)S(1)}, u32[]{:S(2)}, u32[]{:S(2)}) collective-permute-start(bf16[272,128]{1,0:T(8,128)(2,1)S(1)} %get-tuple-element.13.refs_0_), channel_id=1, source_target_pairs={{0,8},{2,10},{4,12},{6,14},{8,16},{10,18},{12,20},{14,22},{16,24},... | collective-permute-start | bytes 208904 | tf_op jit(solution)/shard_map/ppermute | solution.py:319
  14.6 0.0 collective-permute-done.3
  14.6 2.6 %collective-permute-start.1 = (bf16[272,128]{1,0:T(8,128)(2,1)S(1)}, bf16[272,128]{1,0:T(8,128)(2,1)S(1)}, u32[]{:S(2)}, u32[]{:S(2)}) collective-permute-start(bf16[272,128]{1,0:T(8,128)(2,1)S(1)} %get-tuple-element.13.refs_0_), channel_id=1, source_target_pairs={{0,16},{2,18},{4,20},{6,22},{8,24},{10,26},{12,28},{14,30},{16,0},... | collective-permute-start | bytes 208904 | tf_op jit(solution)/shard_map/ppermute | solution.py:319
  17.2 0.0 collective-permute-done.4
  17.2 3.7 %collective-permute-start.2 = (bf16[272,128]{1,0:T(8,128)(2,1)S(1)}, bf16[272,128]{1,0:T(8,128)(2,1)S(1)}, u32[]{:S(2)}, u32[]{:S(2)}) collective-permute-start(bf16[272,128]{1,0:T(8,128)(2,1)S(1)} %get-tuple-element.13.refs_0_), channel_id=1, source_target_pairs={{0,24},{2,26},{4,28},{6,30},{8,0},{10,2},{12,4},{14,6},{16,8},{18,... | collective-permute-start | bytes 208904 | tf_op jit(solution)/shard_map/ppermute | solution.py:319
  21.0 0.0 collective-permute-done.5
  21.0 0.3 collective-permute-done.6
  21.3 0.0 copy-start.3
  21.4 0.0 copy-start
  21.4 0.7 copy-done
  22.0 0.0 collective-permute-done.refs_1_
  22.1 2.3 %collective-permute-done.1.refs_2_ = bf16[272,128]{1,0:T(8,128)(2,1)S(1)} collective-permute-done((bf16[272,128]{1,0:T(8,128)(2,1)S(1)}, bf16[272,128]{1,0:T(8,128)(2,1)S(1)}, u32[]{:S(2)}, u32[]{:S(2)}) %collective-permute-start.1) | collective-permute-done | bytes 69664 | tf_op jit(solution)/shard_map/ppermute | solution.py:319
  24.4 0.0 collective-permute-done.2.after_ref.refs_3_
  24.4 0.0 slice-start
  24.4 0.0 copy-start.1
  24.5 0.9 slice-done
  25.4 1.3 %collective-permute-start.7 = (bf16[1472,128]{1,0:T(8,128)(2,1)S(1)}, bf16[1472,128]{1,0:T(8,128)(2,1)S(1)}, u32[]{:S(2)}, u32[]{:S(2)}) collective-permute-start(bf16[1472,128]{1,0:T(8,128)(2,1)S(1)} %constant_dynamic-update-slice_fusion), channel_id=1, source_target_pairs={{0,4},{2,6},{4,0},{6,2},{8,12},{10,14},{12,8},{14,10},{16,20},{18,... | collective-permute-start | bytes 1130504 | tf_op jit(solution)/shard_map/ppermute | solution.py:335
  26.7 0.0 copy-done.1
  26.8 6.6 %collective-permute-done.7.refs_4_ = bf16[1472,128]{1,0:T(8,128)(2,1)S(1)} collective-permute-done((bf16[1472,128]{1,0:T(8,128)(2,1)S(1)}, bf16[1472,128]{1,0:T(8,128)(2,1)S(1)}, u32[]{:S(2)}, u32[]{:S(2)}) %collective-permute-start.7) | collective-permute-done | bytes 376864 | tf_op jit(solution)/shard_map/ppermute | solution.py:335
  33.4 0.0 copy-start.4
  33.5 0.0 copy-start.6
  33.5 0.0 copy-start.5
  33.5 0.0 copy-start.7
  33.6 3.4 %collective-permute-start.8 = (bf16[2560,128]{1,0:T(8,128)(2,1)S(1)}, bf16[2560,128]{1,0:T(8,128)(2,1)S(1)}, u32[]{:S(2)}, u32[]{:S(2)}) collective-permute-start(bf16[2560,128]{1,0:T(8,128)(2,1)S(1)} %constant_dynamic-update-slice_fusion.5), channel_id=1, source_target_pairs={{0,2},{2,0},{4,6},{6,4},{8,10},{10,8},{12,14},{14,12},{16,18},{18,... | collective-permute-start | bytes 1966088 | tf_op jit(solution)/shard_map/ppermute | solution.py:344
  36.9 0.0 copy-done.3
  36.9 0.0 copy-done.4
  36.9 0.0 copy-done.6
  36.9 0.0 copy-done.5
  36.9 0.0 copy-done.7
  36.9 0.7 prepare.1
  37.6 1.0 %collective-permute-done.8.refs_5_ = bf16[2560,128]{1,0:T(8,128)(2,1)S(1)} collective-permute-done((bf16[2560,128]{1,0:T(8,128)(2,1)S(1)}, bf16[2560,128]{1,0:T(8,128)(2,1)S(1)}, u32[]{:S(2)}, u32[]{:S(2)}) %collective-permute-start.8) | collective-permute-done | bytes 655392 | tf_op jit(solution)/shard_map/ppermute | solution.py:344
  38.6 3.9 %pair.1 = (f32[16,128,128]{2,1,0:T(8,128)S(1)}, f32[16,128,128]{2,1,0:T(8,128)S(1)}, bf16[128,2,16,128]{3,2,1,0:T(8,128)(2,1)S(1)}) custom-call(bf16[272,128]{1,0:T(8,128)(2,1)S(1)} %get-tuple-element.13.refs_0_, bf16[272,128]{1,0:T(8,128)(2,1)S(1)} %collective-permute-done.refs_1_, bf16[272,128]{1,0:T(8,128)(2,1)S(1)} %collective-permute-done.1.refs_2_, ...), custom_call_target="tpu_custom_call" | custom-call | tf_op jit(solution)/shard_map/pair/pallas_call | solution.py:36
  42.5 33.5 %all_to_all.10.recv_ref = bf16[32,4,2,16,128]{4,3,2,1,0:T(8,128)(2,1)S(1)} all-to-all(bf16[32,4,2,16,128]{4,3,2,1,0:T(8,128)(2,1)S(1)} %bitcast.24), channel_id=1, replica_groups=mesh['crops'=1,'rows'=16,'cols'=2] {'rows','cols'}, dimensions={0} | all-to-all | bytes 2097152 | tf_op jit(solution)/shard_map/all_to_all | solution.py:370
  76.0 1.1 %triangle.1 = bf16[32,4,16,128]{3,2,1,0:T(8,128)(2,1)} custom-call(bf16[32,4,2,16,128]{4,3,2,1,0:T(8,128)(2,1)S(1)} %all_to_all.10.recv_ref), custom_call_target="tpu_custom_call" | custom-call | tf_op jit(solution)/shard_map/triangle/pallas_call | solution.py:36
  77.1 0.0 copy-start.12
  77.1 3.8 %all-to-all-start.1 = ((bf16[32,4,16,128]{3,2,1,0:T(8,128)(2,1)}), bf16[32,4,16,128]{3,2,1,0:T(8,128)(2,1)S(1)}, u32[]{:S(2)}, u32[]{:S(2)}) async-start(bf16[32,4,16,128]{3,2,1,0:T(8,128)(2,1)} %triangle.1), calls=%async_computation.1 | async-start | bytes 1048576 | tf_op jit(solution)/shard_map/all_to_all | solution.py:381
  80.9 0.0 copy-done.12
  80.9 0.0 copy-start.13
  80.9 0.1 copy.16
  81.0 0.8 copy-done.13
  81.8 0.0 copy-start.14
  81.8 0.1 copy.17
  81.9 0.6 copy-done.14
  82.6 0.1 copy.15
  82.7 14.1 %all-to-all-done.1 = bf16[32,4,16,128]{3,2,1,0:T(8,128)(2,1)S(1)} async-done(((bf16[32,4,16,128]{3,2,1,0:T(8,128)(2,1)}), bf16[32,4,16,128]{3,2,1,0:T(8,128)(2,1)S(1)}, u32[]{:S(2)}, u32[]{:S(2)}) %all-to-all-start.1) | async-done | bytes 524320 | tf_op jit(solution)/shard_map/all_to_all | solution.py:381
  96.8 5.3 %finish.1 = f32[16,128,128]{2,1,0:T(8,128)} custom-call(bf16[128,16,128]{2,1,0:T(8,128)(2,1)S(1)} %bitcast.22, f32[16,128,128]{2,1,0:T(8,128)S(1)} %get-tuple-element.19.first_ref, f32[16,128,128]{2,1,0:T(8,128)S(1)} %get-tuple-element.20.gate_ref, bf16[128,128]{1,0:T(8,128)(2,1)S(1)} %bitcast.27, bf16[512,128]{1,0:T(8,128)(2,1)S(1)} %bitcast.25, ...), custom_call_target="tpu_custom_call" | custom-call | tf_op jit(solution)/shard_map/finish/pallas_call | solution.py:36
  (13 shorter events, 0.2 us)
Async XLA Ops:
  0.0 0.7 copy-start.10
  0.0 0.7 copy-start.11
  0.7 1.2 %copy-start.2 = (f32[8,128,256]{2,1,0:T(8,128)S(1)}, f32[8,128,256]{2,1,0:T(8,128)}, u32[]{:S(2)}) copy-start(f32[8,128,256]{2,1,0:T(8,128)} %fam_ref.1) | copy-start | bytes 3145732
  1.9 0.7 copy-start.8
  2.6 0.7 copy-start.9
  5.5 9.1 %collective-permute-start.3 = (bf16[2,2,48,128]{3,2,1,0:T(8,128)(2,1)S(1)}, bf16[2,2,48,128]{3,2,1,0:T(8,128)(2,1)S(1)}, u32[]{:S(2)}, u32[]{:S(2)}) collective-permute-start(bf16[2,2,48,128]{3,2,1,0:T(8,128)(2,1)S(1)} %get-tuple-element.21), channel_id=1, source_target_pairs={{0,0},{1,16},{2,2},{3,18},{4,4},{5,20},{6,6},{7,22},{8,8},{9,24},{... | collective-permute-start | bytes 147464 | tf_op jit(solution)/shard_map/ppermute | solution.py:328
  6.2 14.8 %collective-permute-start.5 = (bf16[2,2,48,128]{3,2,1,0:T(8,128)(2,1)S(1)}, bf16[2,2,48,128]{3,2,1,0:T(8,128)(2,1)S(1)}, u32[]{:S(2)}, u32[]{:S(2)}) collective-permute-start(bf16[2,2,48,128]{3,2,1,0:T(8,128)(2,1)S(1)} %get-tuple-element.21), channel_id=1, source_target_pairs={{0,1},{1,17},{2,3},{3,19},{4,5},{5,21},{6,7},{7,23},{8,9},{9,25},{... | collective-permute-start | bytes 147464 | tf_op jit(solution)/shard_map/ppermute | solution.py:328
  11.8 5.4 %collective-permute-start.4 = (bf16[2,2,48,128]{3,2,1,0:T(8,128)(2,1)S(1)}, bf16[2,2,48,128]{3,2,1,0:T(8,128)(2,1)S(1)}, u32[]{:S(2)}, u32[]{:S(2)}) collective-permute-start(bf16[2,2,48,128]{3,2,1,0:T(8,128)(2,1)S(1)} %get-tuple-element.22), channel_id=1, source_target_pairs={{0,8},{1,24},{2,10},{3,26},{4,12},{5,28},{6,14},{7,30},{8,1},{9,17... | collective-permute-start | bytes 147464 | tf_op jit(solution)/shard_map/ppermute | solution.py:328
  13.1 8.2 %collective-permute-start.6 = (bf16[2,2,48,128]{3,2,1,0:T(8,128)(2,1)S(1)}, bf16[2,2,48,128]{3,2,1,0:T(8,128)(2,1)S(1)}, u32[]{:S(2)}, u32[]{:S(2)}) collective-permute-start(bf16[2,2,48,128]{3,2,1,0:T(8,128)(2,1)S(1)} %get-tuple-element.22), channel_id=1, source_target_pairs={{0,9},{1,25},{2,11},{3,27},{4,13},{5,29},{6,15},{7,31},{8,0},{9,16... | collective-permute-start | bytes 147464 | tf_op jit(solution)/shard_map/ppermute | solution.py:328
  13.1 8.9 %collective-permute-start = (bf16[272,128]{1,0:T(8,128)(2,1)S(1)}, bf16[272,128]{1,0:T(8,128)(2,1)S(1)}, u32[]{:S(2)}, u32[]{:S(2)}) collective-permute-start(bf16[272,128]{1,0:T(8,128)(2,1)S(1)} %get-tuple-element.13.refs_0_), channel_id=1, source_target_pairs={{0,8},{2,10},{4,12},{6,14},{8,16},{10,18},{12,20},{14,22},{16,24},... | collective-permute-start | bytes 208904 | tf_op jit(solution)/shard_map/ppermute | solution.py:319
  14.6 9.8 %collective-permute-start.1 = (bf16[272,128]{1,0:T(8,128)(2,1)S(1)}, bf16[272,128]{1,0:T(8,128)(2,1)S(1)}, u32[]{:S(2)}, u32[]{:S(2)}) collective-permute-start(bf16[272,128]{1,0:T(8,128)(2,1)S(1)} %get-tuple-element.13.refs_0_), channel_id=1, source_target_pairs={{0,16},{2,18},{4,20},{6,22},{8,24},{10,26},{12,28},{14,30},{16,0},... | collective-permute-start | bytes 208904 | tf_op jit(solution)/shard_map/ppermute | solution.py:319
  17.2 7.2 %collective-permute-start.2 = (bf16[272,128]{1,0:T(8,128)(2,1)S(1)}, bf16[272,128]{1,0:T(8,128)(2,1)S(1)}, u32[]{:S(2)}, u32[]{:S(2)}) collective-permute-start(bf16[272,128]{1,0:T(8,128)(2,1)S(1)} %get-tuple-element.13.refs_0_), channel_id=1, source_target_pairs={{0,24},{2,26},{4,28},{6,30},{8,0},{10,2},{12,4},{14,6},{16,8},{18,... | collective-permute-start | bytes 208904 | tf_op jit(solution)/shard_map/ppermute | solution.py:319
  21.3 15.6 %copy-start.3 = (f32[16,128,128]{2,1,0:T(8,128)S(1)}, f32[16,128,128]{2,1,0:T(8,128)}, u32[]{:S(2)}) copy-start(f32[16,128,128]{2,1,0:T(8,128)} %contact_ref.1) | copy-start | bytes 3145732
  21.4 0.7 copy-start
  24.4 1.0 slice-start
  24.4 2.3 %copy-start.1 = (bf16[4,2,2,48,128]{4,3,2,1,0:T(8,128)(2,1)S(1)}, bf16[4,2,2,48,128]{4,3,2,1,0:T(8,128)(2,1)}, u32[]{:S(2)}) copy-start(bf16[4,2,2,48,128]{4,3,2,1,0:T(8,128)(2,1)} %copy-done) | copy-start | bytes 589828
  25.4 8.0 %collective-permute-start.7 = (bf16[1472,128]{1,0:T(8,128)(2,1)S(1)}, bf16[1472,128]{1,0:T(8,128)(2,1)S(1)}, u32[]{:S(2)}, u32[]{:S(2)}) collective-permute-start(bf16[1472,128]{1,0:T(8,128)(2,1)S(1)} %constant_dynamic-update-slice_fusion), channel_id=1, source_target_pairs={{0,4},{2,6},{4,0},{6,2},{8,12},{10,14},{12,8},{14,10},{16,20},{18,... | collective-permute-start | bytes 1130504 | tf_op jit(solution)/shard_map/ppermute | solution.py:335
  33.4 3.5 %copy-start.4 = (bf16[1024,128]{1,0:T(8,128)(2,1)S(1)}, bf16[1024,128]{1,0:T(8,128)(2,1)}, u32[]{:S(2)}) copy-start(bf16[1024,128]{1,0:T(8,128)(2,1)} %wo_ref.1) | copy-start | bytes 786436
  33.5 3.4 %copy-start.6 = (bf16[128,256]{1,0:T(8,128)(2,1)S(1)}, bf16[128,256]{1,0:T(8,128)(2,1)}, u32[]{:S(2)}) copy-start(bf16[128,256]{1,0:T(8,128)(2,1)} %tgt_ref.1) | copy-start | bytes 196612
  33.5 3.4 %copy-start.5 = (bf16[128,256]{1,0:T(8,128)(2,1)S(1)}, bf16[128,256]{1,0:T(8,128)(2,1)}, u32[]{:S(2)}) copy-start(bf16[128,256]{1,0:T(8,128)(2,1)} %src_ref.1) | copy-start | bytes 196612
  33.5 3.4 %copy-start.7 = (bf16[128,128]{1,0:T(8,128)(2,1)S(1)}, bf16[128,128]{1,0:T(8,128)(2,1)}, u32[]{:S(2)}) copy-start(bf16[128,128]{1,0:T(8,128)(2,1)} %gate_ref.1) | copy-start | bytes 98308
  33.6 5.1 %collective-permute-start.8 = (bf16[2560,128]{1,0:T(8,128)(2,1)S(1)}, bf16[2560,128]{1,0:T(8,128)(2,1)S(1)}, u32[]{:S(2)}, u32[]{:S(2)}) collective-permute-start(bf16[2560,128]{1,0:T(8,128)(2,1)S(1)} %constant_dynamic-update-slice_fusion.5), channel_id=1, source_target_pairs={{0,2},{2,0},{4,6},{6,4},{8,10},{10,8},{12,14},{14,12},{16,18},{18,... | collective-permute-start | bytes 1966088 | tf_op jit(solution)/shard_map/ppermute | solution.py:344
  77.1 3.8 %copy-start.12 = (bf16[128,512]{1,0:T(8,128)(2,1)S(1)}, bf16[128,512]{1,0:T(8,128)(2,1)}, u32[]{:S(2)}) copy-start(bf16[128,512]{1,0:T(8,128)(2,1)} %param.24) | copy-start | bytes 393220
  77.1 19.6 %all-to-all-start.1 = ((bf16[32,4,16,128]{3,2,1,0:T(8,128)(2,1)}), bf16[32,4,16,128]{3,2,1,0:T(8,128)(2,1)S(1)}, u32[]{:S(2)}, u32[]{:S(2)}) async-start(bf16[32,4,16,128]{3,2,1,0:T(8,128)(2,1)} %triangle.1), calls=%async_computation.1 | async-start | bytes 1048576 | tf_op jit(solution)/shard_map/all_to_all | solution.py:381
  80.9 0.9 copy-start.13
  81.8 0.8 copy-start.14

commit v4 on v3

--- a/solution.py
+++ b/solution.py
@@ -6,6 +6,7 @@
 from jax.experimental import pallas as pl
 from jax.experimental.pallas import tpu as pltpu
 from jax.sharding import PartitionSpec as P
+
 
 EPS = 1e-05
 F32 = jnp.float32
@@ -28,10 +29,13 @@
     return 0.5 * jnp.tanh(0.5 * x) + 0.5
 
 
-def call(kernel, out_shape, scratch, name, ins=(), out_specs=None):
+def call(kernel, out_shape, scratch, ins=(), hbm=(), out_specs=None):
     def run(*args):
         args = [
-            pltpu.with_memory_space_constraint(x, pltpu.VMEM) if k in ins else x for k, x in enumerate(args)
+            pltpu.with_memory_space_constraint(x, pltpu.VMEM if k in ins else pltpu.HBM)
+            if k in ins or k in hbm
+            else x
+            for k, x in enumerate(args)
         ]
         return pl.pallas_call(
             kernel,
@@ -40,7 +44,6 @@
             out_specs=out_specs or jax.tree.map(lambda _: VMEM, out_shape),
             scratch_shapes=scratch,
             compiler_params=pltpu.CompilerParams(vmem_limit_bytes=VMEM_LIMIT),
-            name=name,
         )(*args)
 
     return run
@@ -86,20 +89,19 @@
         part = dot(jnp.concatenate(rows, 0).astype(BF16), w)
         acc = part if acc is None else acc + part
     block = groups * seqs
-    planes = left_ref.shape[0]
     row = lax.axis_index("rows")
-    z, y, c = lax.div(row, 4), lax.rem(lax.div(row, 2), 2), lax.rem(row, 2)
+    y, c = lax.rem(lax.div(row, 2), 2), lax.rem(row, 2)
     for p in range(pieces):
-        at = (
-            lax.rem(p // 4 + planes - lax.rem(z, planes), planes),
-            lax.rem((p // 2) % 2 + y, 2),
-            lax.rem(p % 2 + c, 2),
-        )
+        at = (p // 4, lax.rem((p // 2) % 2 + y, 2), lax.rem(p % 2 + c, 2))
         left_ref[at[0], at[1], at[2], 0:block, :] = acc[p * block : (p + 1) * block].astype(BF16)
         left_ref[at[0], at[1], at[2], block : block + TILE, :] = live_tile
 
 
-def prepare_kernel(contact_ref, wo_ref, src_ref, tgt_ref, gate_ref, after_ref, contact_t_ref, wo_t_ref, wp_t_ref, scr):
+def prepare_kernel(
+    contact_ref, wo_ref, src_ref, tgt_ref, gate_ref, pres_ref, after_ref,
+    contact_t_ref, wo_t_ref, wp_t_ref, live_ref,
+    scr, column,
+):
     tile_rows = contact_ref.shape[0]
     rows = wo_ref.shape[0]
     chans = int(rows**0.5)
@@ -115,14 +117,21 @@
     for ref in (src_ref, tgt_ref, gate_ref):
         wp_t_ref[at : at + ref.shape[1], :] = ref[...].astype(F32).T.astype(BF16)
         at += ref.shape[1]
-
-
-def pair_kernel(*refs, seqs, radix, tile_rows, chans):
-    z_refs, refs = refs[:radix], refs[radix:]
-    (y_ref, c_ref, left_ref, contact_ref, pres_ref, wo_ref, wp_ref,
-     first_ref, gate_ref, panel_ref, o_scr, cnt_scr, pan_scr) = refs
-    right_rows, cols = z_refs[0].shape
-    left_rows = left_ref.shape[3]
+    cols = contact_ref.shape[1]
+    start = lax.axis_index("rows") * tile_rows
+    live_i = pres_ref[pl.ds(lax.div(start, cols), 1), :].astype(F32)
+    column[...] = jnp.broadcast_to(live_i, (LANES, cols)).T
+    live_j = pres_ref[pl.ds(lax.axis_index("cols"), 1), :].astype(F32)
+    live_ref[...] = column[pl.ds(pl.multiple_of(lax.rem(start, cols), 8), tile_rows), :] * live_j
+
+
+def pair_kernel(
+    z_ref, y_ref, c_ref, left_z_ref, left_y_ref, left_c_ref, contact_ref, live_ref, wo_ref, wp_ref,
+    first_ref, gate_ref, panel_ref,
+    o_scr, cnt_scr, pan_scr,
+    *, seqs, radix, tile_rows, chans,
+):
+    right_rows, cols = z_ref.shape[0] // radix, z_ref.shape[1]
     tiles = right_rows // TILE - 1
     blocks = 4 * radix
     feats = first_ref.shape[1]
@@ -131,31 +140,17 @@
     per = LANES // chans
     groups = tile_rows // per
     row = lax.axis_index("rows")
-    col = lax.axis_index("cols")
-    z = lax.div(row, 4)
-    planes = cols // tile_rows // 4
-    turn = col * planes + lax.rem(z, planes) - z + radix
 
     def right(b, t):
         core, pair, k = b // (2 * radix), b // radix % 2, b % radix
-        if core:
-            ref, at = c_ref, (pair * radix + k) * right_rows
-        elif pair:
-            ref, at = y_ref, k * right_rows
-        else:
-            ref, at = z_refs[k], 0
-        return ref[at + t * TILE : at + (t + 1) * TILE, :]
+        ref, at = (c_ref, pair * radix + k) if core else (y_ref if pair else z_ref, k)
+        return ref[at * right_rows + t * TILE : at * right_rows + (t + 1) * TILE, :]
 
     def left(b):
         core, pair, k = b // (2 * radix), b // radix % 2, b % radix
-        m = lax.rem(turn + k, radix)
-        if not core and not pair:
-            return left_ref[m, 0, 0]
         if core:
-            ref, at = c_ref, 2 * radix * right_rows + (pair * radix + m) * left_rows
-        else:
-            ref, at = y_ref, radix * right_rows + 2 * m * left_rows
-        return ref[pl.ds(pl.multiple_of(at, TILE), left_rows), :]
+            return left_c_ref[pair * radix + k]
+        return left_y_ref[k, 0] if pair else left_z_ref[k, 0, 0]
 
     lefts = [left(b).astype(F32) for b in range(blocks)]
     block = groups * seqs
@@ -189,10 +184,6 @@
 
     w_o = wo_ref[...]
     w_p = wp_ref[...]
-    live_j = pres_ref[pl.ds(col, 1), :].astype(F32)
-    live_i = pres_ref[pl.ds(lax.div(row * tile_rows, cols), 1), :].astype(F32)
-    cnt_scr[0:LANES, :] = jnp.broadcast_to(live_i, (LANES, cols)).T
-    live_rows = cnt_scr[pl.ds(pl.multiple_of(start, 8), tile_rows), :]
     for i in range(0, tile_rows, 2):
         upd = dot(w_o, jnp.concatenate([o_scr[i], o_scr[i + 1]], 1))
         normed = []
@@ -204,7 +195,7 @@
             normed.append((centred * lax.rsqrt(spread + EPS)).astype(BF16))
         raw = dot(w_p, jnp.concatenate(normed, 1))
         for k in range(2):
-            live = live_rows[i + k : i + k + 1] * live_j
+            live = live_ref[i + k : i + k + 1, :]
             part = raw[:, k * cols : (k + 1) * cols]
             for side in range(2):
                 at = side * 2 * width
@@ -311,50 +302,50 @@
         functools.partial(project_kernel, tile_rows=tile_rows),
         (shape((right_rows, cols), BF16), shape((planes, 2, 2, left_rows, LANES), BF16)),
         [pltpu.VMEM((feats // LANES, seqs * cols, LANES), F32), pltpu.VMEM((chans * seqs, cols), F32)],
-        "project",
+        hbm=(0, 1, 2, 3, 4),
     )(family_representation, family_keep_flags, presence, couple_lhs_weights.T, couple_rhs_weights.T)
 
-    zs = [right]
-    for k in range(1, radix):
-        zs.append(lax.ppermute(right, "rows", [(i, (i + 4 * k) % n_rows) for i in range(n_rows)]))
+    def shift(k):
+        return [(i, (i + 4 * k) % n_rows) for i in range(n_rows)]
+
+    pair_y = [(i, i ^ 2) for i in range(n_rows)]
+    pair_c = [(i, i ^ 1) for i in range(n_rows)]
+    zs = [right] + [lax.ppermute(right, "rows", shift(k)) for k in range(1, radix)]
+    wide = jnp.zeros((n_cols,) + left.shape, BF16)
+    wide = lax.dynamic_update_slice_in_dim(wide, left[None], col, 0)
+    for k in range(1, n_cols):
+        got = lax.ppermute(left, "cols", [(i, (i + k) % n_cols) for i in range(n_cols)])
+        wide = lax.dynamic_update_slice_in_dim(wide, got[None], (col + n_cols - k) % n_cols, 0)
+    wide = wide.reshape((radix,) + left.shape[1:])
+    y_msg = jnp.concatenate(zs, 0)
+    y_got = lax.ppermute(y_msg, "rows", pair_y)
+    z = lax.axis_index("rows") // 4
     lefts = []
-    for m in range(radix):
-        perm = []
-        for i in range(n_rows):
-            for x in range(n_cols):
-                to = (i // 4 + m) % radix
-                target = (x * planes + to % planes) * 4 + i % 4
-                perm.append((i * n_cols + x, target * n_cols + to // planes))
-        lefts.append(lax.ppermute(left[m % planes], ("rows", "cols"), perm))
+    for k in range(radix):
+        piece = lax.dynamic_index_in_dim(wide, (z + k) % radix, 0, keepdims=False)
+        lefts.append(lax.ppermute(piece, "rows", shift(k)) if k else piece)
     lefts = jnp.stack(lefts)
-
-    def rows_of(array):
-        return array.reshape(-1, LANES)
-
-    y_msg = jnp.concatenate(zs + [rows_of(lefts[:, 1])], 0)
-    y_got = lax.ppermute(y_msg, "rows", [(i, i ^ 2) for i in range(n_rows)])
-    cut = radix * right_rows
-    c_msg = jnp.concatenate(
-        zs + [
-            y_got[:cut],
-            rows_of(lefts[:, 0, 1]),
-            rows_of(y_got[cut:].reshape(radix, 2, left_rows, LANES)[:, 1]),
-        ], 0
-    )
-    c_got = lax.ppermute(c_msg, "rows", [(i, i ^ 1) for i in range(n_rows)])
+    c_got = lax.ppermute(jnp.concatenate([y_msg, y_got], 0), "rows", pair_c)
+    left_y = lax.ppermute(lefts[:, 1], "rows", pair_y)
+    left_c = lax.ppermute(jnp.concatenate([lefts[:, 0, 1], left_y[:, 1]], 0), "rows", pair_c)
 
     pair = shape((tile_rows, pair_feats, cols), F32)
-    contact_t, w_o, w_p = call(
+    contact_t, w_o, w_p, live = call(
         prepare_kernel,
-        (pair, shape((pair_feats, chans * chans), BF16), shape((4 * width + pair_feats, pair_feats), BF16)),
-        [pltpu.VMEM((chans * chans, pair_feats), F32)],
-        "prepare",
-        ins=(5,),
+        (
+            pair,
+            shape((pair_feats, chans * chans), BF16),
+            shape((4 * width + pair_feats, pair_feats), BF16),
+            shape((tile_rows, cols), F32),
+        ),
+        [pltpu.VMEM((chans * chans, pair_feats), F32), pltpu.VMEM((cols, LANES), F32)],
+        ins=(6,),
+        hbm=(0, 1, 2, 3, 4, 5),
     )(
         contact_embedding, pairwise_final_matrix, edge_source_matrix, edge_target_matrix,
-        edge_final_sigmoid_matrix, zs[-1],
+        edge_final_sigmoid_matrix, presence, zs[-1],
     )
-    args = zs + [y_got, c_got, lefts, contact_t, presence, w_o, w_p]
+    args = [y_msg, y_got, c_got, lefts, left_y, left_c, contact_t, live, w_o, w_p]
     first, gate, panels = call(
         functools.partial(pair_kernel, seqs=seqs, radix=radix, tile_rows=tile_rows, chans=chans),
         (pair, pair, shape((width, 2, tile_rows, cols), BF16)),
@@ -363,8 +354,7 @@
             pltpu.VMEM((LANES, cols), F32),
             pltpu.VMEM((2, width * tile_rows, cols), F32),
         ],
-        "pair",
-        ins=[k for k in range(len(args)) if k != len(args) - 3],
+        ins=range(len(args)),
     )(*args)
 
     panels = lax.all_to_all(
@@ -375,7 +365,6 @@
         functools.partial(triangle_kernel, n_rows=n_rows, n_cols=n_cols),
         shape((devices, width // devices, tile_rows, cols), BF16),
         [],
-        "triangle",
         ins=(0,),
     )(panels)
     product = lax.all_to_all(product, ("rows", "cols"), split_axis=0, concat_axis=0, tiled=True)
@@ -387,7 +376,6 @@
             pltpu.VMEM((tile_rows, cols, pair_feats), F32),
             pltpu.SemaphoreType.DMA((tile_rows // 2,)),
         ],
-        "finish",
         ins=(0, 1, 2, 3, 4, 5),
         out_specs=pl.BlockSpec(memory_space=pl.ANY),
     )(
@@ -399,4 +387,5 @@
 def solution(mesh):
     tiles = P(("crops", "rows"), "cols", None)
     in_specs = (tiles, P(("crops", "rows"), "cols"), P("crops"), tiles) + (P(),) * 9
+
     return jax.shard_map(on_device, mesh=mesh, in_specs=in_specs, out_specs=tiles, check_vma=False)

time: 103 us -> 91.3 us (0.89)
  local copies, waits for them, and re-layouts: 6.94 us -> 2.02 us
  waiting for transfers between devices: 24.4 us -> 20.7 us
  blocking collectives: 33.5 us -> 30.9 us
  Pallas kernels: 13.1 us -> 15.7 us
  starting transfers between devices: 23.8 us -> 21.4 us
    unnamed x39 -> x13, local copies, waits for them, and re-layouts: 5.95 us -> 1.84 us
    ppermute x9 -> x11, waiting for transfers between devices: 10.4 us -> 6.64 us  [the longest x3 3.69 us: on_device(): lefts.append(lax.ppermute(piece, 'rows', shift(k)) if k else piece)]
    all_to_all x1, blocking collectives: 33.5 us -> 30.9 us  [on_device(): lax.all_to_all(panels.reshape(devices, width // devices, 2, tile_rows, co...]
    pallas_call x5, Pallas kernels: 13.1 us -> 15.7 us  [run(): pl.pallas_call(kernel, out_shape=out_shape, in_specs=[VMEM] * len(args),...]
    ppermute x9 -> x11, starting transfers between devices: 20.1 us -> 17.6 us  [the longest x3 5.54 us: on_device(): lax.ppermute(right, 'rows', shift(k))]
  transfers between devices with their start and end apart: 10 -> 12, of which waited for: 5 -> 4; matrix products, arithmetic and copies ran while one was open for 0% -> 1% of each run, Pallas kernels for 1% -> 2%
where the time goes in v4:
time: 91.3 us; the launch traced here: 90.9 us
  blocking collectives  30.9 us (34%)
  starting transfers between devices  21.4 us (23%)
  waiting for transfers between devices  20.7 us (23%)
  Pallas kernels  15.7 us (17%)
  local copies, waits for them, and re-layouts  2.02 us (2%)
    all_to_all x1, blocking collectives, on_device(): lax.all_to_all(panels.reshape(devices, width // devices, 2, tile_rows, co...  30.9 us
    pallas_call x5, Pallas kernels, run(): pl.pallas_call(kernel, out_shape=out_shape, in_specs=[VMEM] * len(args),...  15.7 us
    all_to_all x1, waiting for transfers between devices, on_device(): lax.all_to_all(product, ('rows', 'cols'), split_axis=0, concat_axis=0, ti...  14.1 us
    ppermute x3, starting transfers between devices, on_device(): lax.ppermute(right, 'rows', shift(k))  5.54 us
    ppermute x1, starting transfers between devices, on_device(): c_got = lax.ppermute(jnp.concatenate([y_msg, y_got], 0), 'rows', pair_c)  4.15 us
    all_to_all x1, starting transfers between devices, on_device(): lax.all_to_all(product, ('rows', 'cols'), split_axis=0, concat_axis=0, ti...  3.75 us
    ppermute x3, waiting for transfers between devices, on_device(): lefts.append(lax.ppermute(piece, 'rows', shift(k)) if k else piece)  3.69 us
    ppermute x3, waiting for transfers between devices, on_device(): lax.ppermute(right, 'rows', shift(k))  2.93 us
  transfers between devices with their start and end apart: 12, of which 4 were waited for; matrix products, arithmetic and copies ran while one was open for 1% of the time, Pallas kernels for 2%

profile of v4, /device:TPU:1, one launch (start us, length us, event | category | flops | bytes accessed | tf_op | source)
XLA Modules:
  0.0 90.9 jit_solution(1646551589905733739)
XLA Ops:
  0.0 3.4 %shard_map.127 = (bf16[272,128]{1,0:T(8,128)(2,1)S(1)}, bf16[2,2,2,48,128]{4,3,2,1,0:T(8,128)(2,1)S(1)}) custom-call(f32[8,128,256]{2,1,0:T(8,128)} %fam_ref.1, s32[8,128]{1,0:T(8,128)} %keep_ref.1, s32[2,128]{1,0:T(2,128)} %bitcast.41, bf16[32,256]{1,0:T(8,128)(2,1)} %bitcast.39, bf16[32,256]{1,0:T(8,128)(2,1)} %bitcast.40), custom_call_target="tpu_custom_call" | custom-call | tf_op jit(solution)/shard_map/pallas_call | solution.py:40
  3.4 2.2 %collective-permute-start = (bf16[272,128]{1,0:T(8,128)(2,1)S(1)}, bf16[272,128]{1,0:T(8,128)(2,1)S(1)}, u32[]{:S(2)}, u32[]{:S(2)}) collective-permute-start(bf16[272,128]{1,0:T(8,128)(2,1)S(1)} %get-tuple-element.14), channel_id=1, source_target_pairs={{0,8},{2,10},{4,12},{6,14},{8,16},{10,18},{12,20},{14,22},{16,24},... | collective-permute-start | bytes 208904 | tf_op jit(solution)/shard_map/ppermute | solution.py:313
  5.5 2.3 %collective-permute-start.1 = (bf16[272,128]{1,0:T(8,128)(2,1)S(1)}, bf16[272,128]{1,0:T(8,128)(2,1)S(1)}, u32[]{:S(2)}, u32[]{:S(2)}) collective-permute-start(bf16[272,128]{1,0:T(8,128)(2,1)S(1)} %get-tuple-element.14), channel_id=1, source_target_pairs={{0,16},{2,18},{4,20},{6,22},{8,24},{10,26},{12,28},{14,30},{16,0},... | collective-permute-start | bytes 208904 | tf_op jit(solution)/shard_map/ppermute | solution.py:313
  7.8 1.1 %collective-permute-start.2 = (bf16[272,128]{1,0:T(8,128)(2,1)S(1)}, bf16[272,128]{1,0:T(8,128)(2,1)S(1)}, u32[]{:S(2)}, u32[]{:S(2)}) collective-permute-start(bf16[272,128]{1,0:T(8,128)(2,1)S(1)} %get-tuple-element.14), channel_id=1, source_target_pairs={{0,24},{2,26},{4,28},{6,30},{8,0},{10,2},{12,4},{14,6},{16,8},{18,... | collective-permute-start | bytes 208904 | tf_op jit(solution)/shard_map/ppermute | solution.py:313
  8.9 1.2 %collective-permute-start.5 = (bf16[2,2,2,48,128]{4,3,2,1,0:T(8,128)(2,1)S(1)}, bf16[2,2,2,48,128]{4,3,2,1,0:T(8,128)(2,1)S(1)}, u32[]{:S(2)}, u32[]{:S(2)}) collective-permute-start(bf16[2,2,2,48,128]{4,3,2,1,0:T(8,128)(2,1)S(1)} %get-tuple-element.15), channel_id=1, source_target_pairs={{0,1},{1,0},{2,3},{3,2},{4,5},{5,4},{6,7},{7,6},{8,9},{9,8},{10,11... | collective-permute-start | bytes 294920 | tf_op jit(solution)/shard_map/ppermute | solution.py:317
  10.2 0.0 collective-permute-done
  10.2 2.9 %collective-permute-done.1 = bf16[272,128]{1,0:T(8,128)(2,1)S(1)} collective-permute-done((bf16[272,128]{1,0:T(8,128)(2,1)S(1)}, bf16[272,128]{1,0:T(8,128)(2,1)S(1)}, u32[]{:S(2)}, u32[]{:S(2)}) %collective-permute-start.1) | collective-permute-done | bytes 69664 | tf_op jit(solution)/shard_map/ppermute | solution.py:313
  13.2 0.0 collective-permute-done.5
  13.3 1.5 %collective-permute-start.8 = (bf16[2,2,48,128]{3,2,1,0:T(8,128)(2,1)S(1)}, bf16[2,2,48,128]{3,2,1,0:T(8,128)(2,1)S(1)}, u32[]{:S(2)}, u32[]{:S(2)}) collective-permute-start(bf16[2,2,48,128]{3,2,1,0:T(8,128)(2,1)S(1)} %get-tuple-element.24), channel_id=1, source_target_pairs={{0,24},{2,26},{4,28},{6,30},{8,0},{10,2},{12,4},{14,6},{16,8},{18,... | collective-permute-start | bytes 147464 | tf_op jit(solution)/shard_map/ppermute | solution.py:326
  14.8 0.0 collective-permute-start.6
  14.8 0.3 collective-permute-start.7
  15.1 0.0 collective-permute-done.2.after_ref
  15.2 1.3 %collective-permute-start.3 = (bf16[1088,128]{1,0:T(8,128)(2,1)S(1)}, bf16[1088,128]{1,0:T(8,128)(2,1)S(1)}, u32[]{:S(2)}, u32[]{:S(2)}) collective-permute-start(bf16[1088,128]{1,0:T(8,128)(2,1)S(1)} %get-tuple-element.28.z_ref), channel_id=1, source_target_pairs={{0,4},{2,6},{4,0},{6,2},{8,12},{10,14},{12,8},{14,10},{16,20},{18,... | collective-permute-start | bytes 835592 | tf_op jit(solution)/shard_map/ppermute | solution.py:321
  16.5 0.0 collective-permute-done.8
  16.5 3.1 %collective-permute-done.6 = bf16[2,2,48,128]{3,2,1,0:T(8,128)(2,1)S(1)} collective-permute-done((bf16[2,2,48,128]{3,2,1,0:T(8,128)(2,1)S(1)}, bf16[2,2,48,128]{3,2,1,0:T(8,128)(2,1)S(1)}, u32[]{:S(2)}, u32[]{:S(2)}) %collective-permute-start.6) | collective-permute-done | bytes 49184 | tf_op jit(solution)/shard_map/ppermute | solution.py:326
  19.6 0.5 collective-permute-done.7
  20.2 1.3 %collective-permute-start.9 = (bf16[4,2,48,128]{3,2,0,1:T(8,128)(2,1)S(1)}, bf16[4,2,48,128]{3,2,0,1:T(8,128)(2,1)S(1)}, u32[]{:S(2)}, u32[]{:S(2)}) collective-permute-start(bf16[4,2,48,128]{3,2,0,1:T(8,128)(2,1)S(1)} %slice_bitcast_fusion), channel_id=1, source_target_pairs={{0,4},{2,6},{4,0},{6,2},{8,12},{10,14},{12,8},{14,10},{16,20},{18,... | collective-permute-start | bytes 294920 | tf_op jit(solution)/shard_map/ppermute | solution.py:329
  21.5 0.0 collective-permute-done.3.y_ref
  21.6 4.2 %collective-permute-start.4 = (bf16[2176,128]{1,0:T(8,128)(2,1)S(1)}, bf16[2176,128]{1,0:T(8,128)(2,1)S(1)}, u32[]{:S(2)}, u32[]{:S(2)}) collective-permute-start(bf16[2176,128]{1,0:T(8,128)(2,1)S(1)} %constant_dynamic-update-slice_fusion.4), channel_id=1, source_target_pairs={{0,2},{2,0},{4,6},{6,4},{8,10},{10,8},{12,14},{14,12},{16,18},{18,... | collective-permute-start | bytes 1671176 | tf_op jit(solution)/shard_map/ppermute | solution.py:328
  25.7 0.0 collective-permute-done.9
  25.8 2.2 %collective-permute-start.10 = (bf16[8,48,128]{2,1,0:T(8,128)(2,1)S(1)}, bf16[8,48,128]{2,1,0:T(8,128)(2,1)S(1)}, u32[]{:S(2)}, u32[]{:S(2)}) collective-permute-start(bf16[8,48,128]{2,1,0:T(8,128)(2,1)S(1)} %pad_maximum_fusion.1), channel_id=1, source_target_pairs={{0,2},{2,0},{4,6},{6,4},{8,10},{10,8},{12,14},{14,12},{16,18},{18,... | collective-permute-start | bytes 294920 | tf_op jit(solution)/shard_map/ppermute | solution.py:330
  28.0 2.0 %shard_map.128 = (f32[16,128,128]{2,1,0:T(8,128)S(1)}, bf16[128,1024]{1,0:T(8,128)(2,1)S(1)}, bf16[640,128]{1,0:T(8,128)(2,1)S(1)}, f32[16,128]{1,0:T(8,128)S(1)}) custom-call(f32[16,128,128]{2,1,0:T(8,128)} %contact_ref.1, bf16[1024,128]{1,0:T(8,128)(2,1)} %wo_ref.1, bf16[128,256]{1,0:T(8,128)(2,1)} %src_ref.1, bf16[128,256]{1,0:T(8,128)(2,1)} %tgt_ref.1, ...), custom_call_target="tpu_custom_call" | custom-call | tf_op jit(solution)/shard_map/pallas_call | solution.py:40
  30.1 0.0 collective-permute-done.10.left_c_ref
  30.1 0.0 collective-permute-done.4.c_ref
  30.1 3.9 %shard_map.129 = (f32[16,128,128]{2,1,0:T(8,128)S(1)}, f32[16,128,128]{2,1,0:T(8,128)S(1)}, bf16[128,2,16,128]{3,2,1,0:T(8,128)(2,1)S(1)}) custom-call(bf16[1088,128]{1,0:T(8,128)(2,1)S(1)} %get-tuple-element.28.z_ref, bf16[1088,128]{1,0:T(8,128)(2,1)S(1)} %collective-permute-done.3.y_ref, bf16[2176,128]{1,0:T(8,128)(2,1)S(1)} %collective-permute-done.4.c_ref, ...), custom_call_target="tpu_custom_call" | custom-call | tf_op jit(solution)/shard_map/pallas_call | solution.py:40
  34.0 30.9 %all_to_all.10.recv_ref = bf16[32,4,2,16,128]{4,3,2,1,0:T(8,128)(2,1)S(1)} all-to-all(bf16[32,4,2,16,128]{4,3,2,1,0:T(8,128)(2,1)S(1)} %bitcast.31), channel_id=1, replica_groups=mesh['crops'=1,'rows'=16,'cols'=2] {'rows','cols'}, dimensions={0} | all-to-all | bytes 2097152 | tf_op jit(solution)/shard_map/all_to_all | solution.py:360
  64.9 1.1 %shard_map.130 = bf16[32,4,16,128]{3,2,1,0:T(8,128)(2,1)} custom-call(bf16[32,4,2,16,128]{4,3,2,1,0:T(8,128)(2,1)S(1)} %all_to_all.10.recv_ref), custom_call_target="tpu_custom_call" | custom-call | tf_op jit(solution)/shard_map/pallas_call | solution.py:40
  66.0 0.0 copy-start
  66.0 3.8 %all-to-all-start.1 = ((bf16[32,4,16,128]{3,2,1,0:T(8,128)(2,1)}), bf16[32,4,16,128]{3,2,1,0:T(8,128)(2,1)S(1)}, u32[]{:S(2)}, u32[]{:S(2)}) async-start(bf16[32,4,16,128]{3,2,1,0:T(8,128)(2,1)} %shard_map.130), calls=%async_computation.1 | async-start | bytes 1048576 | tf_op jit(solution)/shard_map/all_to_all | solution.py:370
  69.8 0.0 copy-done
  69.8 0.0 copy-start.1
  69.8 0.1 copy.19
  69.9 0.8 copy-done.1
  70.7 0.0 copy-start.2
  70.7 0.1 copy.20
  70.8 0.6 copy-done.2
  71.4 0.1 copy.18
  71.6 14.1 %all-to-all-done.1 = bf16[32,4,16,128]{3,2,1,0:T(8,128)(2,1)S(1)} async-done(((bf16[32,4,16,128]{3,2,1,0:T(8,128)(2,1)}), bf16[32,4,16,128]{3,2,1,0:T(8,128)(2,1)S(1)}, u32[]{:S(2)}, u32[]{:S(2)}) %all-to-all-start.1) | async-done | bytes 524320 | tf_op jit(solution)/shard_map/all_to_all | solution.py:370
  85.6 5.3 %shard_map.131 = f32[16,128,128]{2,1,0:T(8,128)} custom-call(bf16[128,16,128]{2,1,0:T(8,128)(2,1)S(1)} %bitcast.30, f32[16,128,128]{2,1,0:T(8,128)S(1)} %get-tuple-element.21.first_ref, f32[16,128,128]{2,1,0:T(8,128)S(1)} %get-tuple-element.22.gate_ref, bf16[128,128]{1,0:T(8,128)(2,1)S(1)} %bitcast.34, bf16[512,128]{1,0:T(8,128)(2,1)S(1)} %bitcast.32, ...), custom_call_target="tpu_custom_call" | custom-call | tf_op jit(solution)/shard_map/pallas_call | solution.py:40
  (16 shorter events, 0.3 us)
Async XLA Ops:
  3.4 6.8 %collective-permute-start = (bf16[272,128]{1,0:T(8,128)(2,1)S(1)}, bf16[272,128]{1,0:T(8,128)(2,1)S(1)}, u32[]{:S(2)}, u32[]{:S(2)}) collective-permute-start(bf16[272,128]{1,0:T(8,128)(2,1)S(1)} %get-tuple-element.14), channel_id=1, source_target_pairs={{0,8},{2,10},{4,12},{6,14},{8,16},{10,18},{12,20},{14,22},{16,24},... | collective-permute-start | bytes 208904 | tf_op jit(solution)/shard_map/ppermute | solution.py:313
  5.5 7.6 %collective-permute-start.1 = (bf16[272,128]{1,0:T(8,128)(2,1)S(1)}, bf16[272,128]{1,0:T(8,128)(2,1)S(1)}, u32[]{:S(2)}, u32[]{:S(2)}) collective-permute-start(bf16[272,128]{1,0:T(8,128)(2,1)S(1)} %get-tuple-element.14), channel_id=1, source_target_pairs={{0,16},{2,18},{4,20},{6,22},{8,24},{10,26},{12,28},{14,30},{16,0},... | collective-permute-start | bytes 208904 | tf_op jit(solution)/shard_map/ppermute | solution.py:313
  7.8 7.3 %collective-permute-start.2 = (bf16[272,128]{1,0:T(8,128)(2,1)S(1)}, bf16[272,128]{1,0:T(8,128)(2,1)S(1)}, u32[]{:S(2)}, u32[]{:S(2)}) collective-permute-start(bf16[272,128]{1,0:T(8,128)(2,1)S(1)} %get-tuple-element.14), channel_id=1, source_target_pairs={{0,24},{2,26},{4,28},{6,30},{8,0},{10,2},{12,4},{14,6},{16,8},{18,... | collective-permute-start | bytes 208904 | tf_op jit(solution)/shard_map/ppermute | solution.py:313
  8.9 4.3 %collective-permute-start.5 = (bf16[2,2,2,48,128]{4,3,2,1,0:T(8,128)(2,1)S(1)}, bf16[2,2,2,48,128]{4,3,2,1,0:T(8,128)(2,1)S(1)}, u32[]{:S(2)}, u32[]{:S(2)}) collective-permute-start(bf16[2,2,2,48,128]{4,3,2,1,0:T(8,128)(2,1)S(1)} %get-tuple-element.15), channel_id=1, source_target_pairs={{0,1},{1,0},{2,3},{3,2},{4,5},{5,4},{6,7},{7,6},{8,9},{9,8},{10,11... | collective-permute-start | bytes 294920 | tf_op jit(solution)/shard_map/ppermute | solution.py:317
  13.3 3.2 %collective-permute-start.8 = (bf16[2,2,48,128]{3,2,1,0:T(8,128)(2,1)S(1)}, bf16[2,2,48,128]{3,2,1,0:T(8,128)(2,1)S(1)}, u32[]{:S(2)}, u32[]{:S(2)}) collective-permute-start(bf16[2,2,48,128]{3,2,1,0:T(8,128)(2,1)S(1)} %get-tuple-element.24), channel_id=1, source_target_pairs={{0,24},{2,26},{4,28},{6,30},{8,0},{10,2},{12,4},{14,6},{16,8},{18,... | collective-permute-start | bytes 147464 | tf_op jit(solution)/shard_map/ppermute | solution.py:326
  14.8 4.8 %collective-permute-start.6 = (bf16[2,2,48,128]{3,2,1,0:T(8,128)(2,1)S(1)}, bf16[2,2,48,128]{3,2,1,0:T(8,128)(2,1)S(1)}, u32[]{:S(2)}, u32[]{:S(2)}) collective-permute-start(bf16[2,2,48,128]{3,2,1,0:T(8,128)(2,1)S(1)} %get-tuple-element.26), channel_id=1, source_target_pairs={{0,8},{2,10},{4,12},{6,14},{8,16},{10,18},{12,20},{14,22},{16,24},... | collective-permute-start | bytes 147464 | tf_op jit(solution)/shard_map/ppermute | solution.py:326
  14.8 5.4 %collective-permute-start.7 = (bf16[2,2,48,128]{3,2,1,0:T(8,128)(2,1)S(1)}, bf16[2,2,48,128]{3,2,1,0:T(8,128)(2,1)S(1)}, u32[]{:S(2)}, u32[]{:S(2)}) collective-permute-start(bf16[2,2,48,128]{3,2,1,0:T(8,128)(2,1)S(1)} %get-tuple-element.25), channel_id=1, source_target_pairs={{0,16},{2,18},{4,20},{6,22},{8,24},{10,26},{12,28},{14,30},{16,0},... | collective-permute-start | bytes 147464 | tf_op jit(solution)/shard_map/ppermute | solution.py:326
  15.2 6.4 %collective-permute-start.3 = (bf16[1088,128]{1,0:T(8,128)(2,1)S(1)}, bf16[1088,128]{1,0:T(8,128)(2,1)S(1)}, u32[]{:S(2)}, u32[]{:S(2)}) collective-permute-start(bf16[1088,128]{1,0:T(8,128)(2,1)S(1)} %get-tuple-element.28.z_ref), channel_id=1, source_target_pairs={{0,4},{2,6},{4,0},{6,2},{8,12},{10,14},{12,8},{14,10},{16,20},{18,... | collective-permute-start | bytes 835592 | tf_op jit(solution)/shard_map/ppermute | solution.py:321
  20.2 5.5 %collective-permute-start.9 = (bf16[4,2,48,128]{3,2,0,1:T(8,128)(2,1)S(1)}, bf16[4,2,48,128]{3,2,0,1:T(8,128)(2,1)S(1)}, u32[]{:S(2)}, u32[]{:S(2)}) collective-permute-start(bf16[4,2,48,128]{3,2,0,1:T(8,128)(2,1)S(1)} %slice_bitcast_fusion), channel_id=1, source_target_pairs={{0,4},{2,6},{4,0},{6,2},{8,12},{10,14},{12,8},{14,10},{16,20},{18,... | collective-permute-start | bytes 294920 | tf_op jit(solution)/shard_map/ppermute | solution.py:329
  21.6 8.5 %collective-permute-start.4 = (bf16[2176,128]{1,0:T(8,128)(2,1)S(1)}, bf16[2176,128]{1,0:T(8,128)(2,1)S(1)}, u32[]{:S(2)}, u32[]{:S(2)}) collective-permute-start(bf16[2176,128]{1,0:T(8,128)(2,1)S(1)} %constant_dynamic-update-slice_fusion.4), channel_id=1, source_target_pairs={{0,2},{2,0},{4,6},{6,4},{8,10},{10,8},{12,14},{14,12},{16,18},{18,... | collective-permute-start | bytes 1671176 | tf_op jit(solution)/shard_map/ppermute | solution.py:328
  25.8 4.3 %collective-permute-start.10 = (bf16[8,48,128]{2,1,0:T(8,128)(2,1)S(1)}, bf16[8,48,128]{2,1,0:T(8,128)(2,1)S(1)}, u32[]{:S(2)}, u32[]{:S(2)}) collective-permute-start(bf16[8,48,128]{2,1,0:T(8,128)(2,1)S(1)} %pad_maximum_fusion.1), channel_id=1, source_target_pairs={{0,2},{2,0},{4,6},{6,4},{8,10},{10,8},{12,14},{14,12},{16,18},{18,... | collective-permute-start | bytes 294920 | tf_op jit(solution)/shard_map/ppermute | solution.py:330
  66.0 3.8 %copy-start = (bf16[128,512]{1,0:T(8,128)(2,1)S(1)}, bf16[128,512]{1,0:T(8,128)(2,1)}, u32[]{:S(2)}) copy-start(bf16[128,512]{1,0:T(8,128)(2,1)} %param.24) | copy-start | bytes 393220
  66.0 19.6 %all-to-all-start.1 = ((bf16[32,4,16,128]{3,2,1,0:T(8,128)(2,1)}), bf16[32,4,16,128]{3,2,1,0:T(8,128)(2,1)S(1)}, u32[]{:S(2)}, u32[]{:S(2)}) async-start(bf16[32,4,16,128]{3,2,1,0:T(8,128)(2,1)} %shard_map.130), calls=%async_computation.1 | async-start | bytes 1048576 | tf_op jit(solution)/shard_map/all_to_all | solution.py:370
  69.8 0.9 copy-start.1
  70.7 0.8 copy-start.2

commit v5 on v4

--- a/solution.py
+++ b/solution.py
@@ -14,6 +14,8 @@
 TILE = 16
 LANES = 128
 VMEM_LIMIT = 32 * 2**20
+PAD = 8
+GROUP = 16
 VMEM = pl.BlockSpec(memory_space=pltpu.VMEM)
 
 
@@ -62,7 +64,7 @@
         spread = jnp.mean(centred * centred, -1, keepdims=True)
         n = centred * (lax.rsqrt(spread + EPS) * live_t[:, s : s + 1])
         for h in range(feats // LANES):
-            nf[h, pl.ds(s * cols, cols), :] = n[:, h * LANES : (h + 1) * LANES]
+            nf[h, pl.ds(s * (cols + PAD), cols), :] = n[:, h * LANES : (h + 1) * LANES]
         rs[pl.ds(s, chans, stride=seqs), :] = dot_nt(wr_t, n.astype(BF16))
     right_ref[0 : chans * seqs, :] = rs[...].astype(BF16)
     live_tile = jnp.concatenate([live, jnp.zeros((TILE - seqs, cols), F32)], 0).astype(BF16)
@@ -82,7 +84,7 @@
         w = jnp.concatenate(parts, 1).astype(BF16)
         rows = [
             jnp.concatenate(
-                [nf[h, pl.ds(pq * per + i4, seqs, stride=cols), :] for h in range(feats // LANES)], 1
+                [nf[h, pl.ds(pq * per + i4, seqs, stride=cols + PAD), :] for h in range(feats // LANES)], 1
             )
             for pq in range(pieces * groups)
         ]
@@ -90,9 +92,10 @@
         acc = part if acc is None else acc + part
     block = groups * seqs
     row = lax.axis_index("rows")
-    y, c = lax.rem(lax.div(row, 2), 2), lax.rem(row, 2)
+    planes = left_ref.shape[0]
+    z, y, c = lax.rem(lax.div(row, 4), planes), lax.rem(lax.div(row, 2), 2), lax.rem(row, 2)
     for p in range(pieces):
-        at = (p // 4, lax.rem((p // 2) % 2 + y, 2), lax.rem(p % 2 + c, 2))
+        at = ((p // 4) ^ z, lax.rem((p // 2) % 2 + y, 2), lax.rem(p % 2 + c, 2))
         left_ref[at[0], at[1], at[2], 0:block, :] = acc[p * block : (p + 1) * block].astype(BF16)
         left_ref[at[0], at[1], at[2], block : block + TILE, :] = live_tile
 
@@ -135,7 +138,8 @@
     tiles = right_rows // TILE - 1
     blocks = 4 * radix
     feats = first_ref.shape[1]
-    width = pan_scr.shape[1] // tile_rows
+    pitch = tile_rows + PAD
+    width = pan_scr.shape[1] // pitch
     pack = TILE // seqs
     per = LANES // chans
     groups = tile_rows // per
@@ -184,27 +188,27 @@
 
     w_o = wo_ref[...]
     w_p = wp_ref[...]
-    for i in range(0, tile_rows, 2):
-        upd = dot(w_o, jnp.concatenate([o_scr[i], o_scr[i + 1]], 1))
+    for i in range(0, tile_rows, GROUP):
+        upd = dot(w_o, jnp.concatenate([o_scr[i + k] for k in range(GROUP)], 1))
         normed = []
-        for k in range(2):
+        for k in range(GROUP):
             first = contact_ref[i + k] + upd[:, k * cols : (k + 1) * cols]
             first_ref[i + k] = first
             centred = first - jnp.mean(first, 0, keepdims=True)
             spread = jnp.mean(centred * centred, 0, keepdims=True)
             normed.append((centred * lax.rsqrt(spread + EPS)).astype(BF16))
         raw = dot(w_p, jnp.concatenate(normed, 1))
-        for k in range(2):
+        for k in range(GROUP):
             live = live_ref[i + k : i + k + 1, :]
             part = raw[:, k * cols : (k + 1) * cols]
             for side in range(2):
                 at = side * 2 * width
                 val = part[at : at + width] * sigmoid(part[at + width : at + 2 * width]) * live
-                pan_scr[side, pl.ds(i + k, width, stride=tile_rows), :] = val
+                pan_scr[side, pl.ds(i + k, width, stride=pitch), :] = val
             gate_ref[i + k] = sigmoid(part[4 * width : 4 * width + feats])
     for ch in range(width):
         for side in range(2):
-            panel_ref[ch, side] = pan_scr[side, ch * tile_rows : (ch + 1) * tile_rows, :].astype(BF16)
+            panel_ref[ch, side] = pan_scr[side, ch * pitch : ch * pitch + tile_rows, :].astype(BF16)
 
 
 def triangle_kernel(recv_ref, out_ref, *, n_rows, n_cols):
@@ -231,6 +235,7 @@
 
 def finish_kernel(prod_ref, first_ref, gate_ref, we_ref, w1_ref, w2_ref, hbm_ref, mix, out_ref, sems):
     chans, tile_rows, cols = prod_ref.shape
+    pitch = tile_rows + PAD
     total = jnp.zeros((tile_rows, cols), F32)
     for ch in range(chans):
         total = total + prod_ref[ch].astype(F32)
@@ -241,16 +246,16 @@
         square = square + centred * centred
     scale = lax.rsqrt(square * (1.0 / chans) + EPS)
     for ch in range(chans):
-        mix[ch * tile_rows : (ch + 1) * tile_rows, :] = (prod_ref[ch].astype(F32) - mean) * scale
+        mix[ch * pitch : ch * pitch + tile_rows, :] = (prod_ref[ch].astype(F32) - mean) * scale
     w_e, w_1, w_2 = we_ref[...], w1_ref[...], w2_ref[...]
     copies = []
-    for i in range(0, tile_rows, 2):
+    for i in range(0, tile_rows, GROUP):
         mixed = jnp.concatenate(
-            [mix[pl.ds(i + k, chans, stride=tile_rows), :].astype(BF16) for k in range(2)], 1
+            [mix[pl.ds(i + k, chans, stride=pitch), :].astype(BF16) for k in range(GROUP)], 1
         )
         proj = dot(w_e, mixed)
         seconds, normed = [], []
-        for k in range(2):
+        for k in range(GROUP):
             second = first_ref[i + k] + gate_ref[i + k] * proj[:, k * cols : (k + 1) * cols]
             centred = second - jnp.mean(second, 0, keepdims=True)
             spread = jnp.mean(centred * centred, 0, keepdims=True)
@@ -258,9 +263,9 @@
             normed.append((centred * lax.rsqrt(spread + EPS)).astype(BF16))
         hidden = jnp.maximum(dot(w_1, jnp.concatenate(normed, 1)), 0.0).astype(BF16)
         out = dot(w_2, hidden)
-        for k in range(2):
+        for k in range(GROUP):
             out_ref[i + k] = (seconds[k] + out[:, k * cols : (k + 1) * cols]).T
-        copy = pltpu.make_async_copy(out_ref.at[pl.ds(i, 2)], hbm_ref.at[pl.ds(i, 2)], sems.at[i // 2])
+        copy = pltpu.make_async_copy(out_ref.at[pl.ds(i, GROUP)], hbm_ref.at[pl.ds(i, GROUP)], sems.at[i // GROUP])
         copy.start()
         copies.append(copy)
     for copy in copies:
@@ -300,31 +305,29 @@
     left_rows = tile_rows * chans * seqs // LANES + TILE
     right, left = call(
         functools.partial(project_kernel, tile_rows=tile_rows),
-        (shape((right_rows, cols), BF16), shape((planes, 2, 2, left_rows, LANES), BF16)),
-        [pltpu.VMEM((feats // LANES, seqs * cols, LANES), F32), pltpu.VMEM((chans * seqs, cols), F32)],
+        (shape((right_rows, cols), BF16), shape((pieces // 4, 2, 2, left_rows, LANES), BF16)),
+        [pltpu.VMEM((feats // LANES, seqs * (cols + PAD), LANES), F32), pltpu.VMEM((chans * seqs, cols), F32)],
         hbm=(0, 1, 2, 3, 4),
     )(family_representation, family_keep_flags, presence, couple_lhs_weights.T, couple_rhs_weights.T)
 
-    def shift(k):
-        return [(i, (i + 4 * k) % n_rows) for i in range(n_rows)]
-
     pair_y = [(i, i ^ 2) for i in range(n_rows)]
     pair_c = [(i, i ^ 1) for i in range(n_rows)]
-    zs = [right] + [lax.ppermute(right, "rows", shift(k)) for k in range(1, radix)]
+    own = lax.axis_index("rows") // 4 // planes ^ col
     wide = jnp.zeros((n_cols,) + left.shape, BF16)
-    wide = lax.dynamic_update_slice_in_dim(wide, left[None], col, 0)
+    wide = lax.dynamic_update_slice_in_dim(wide, left[None], own, 0)
     for k in range(1, n_cols):
-        got = lax.ppermute(left, "cols", [(i, (i + k) % n_cols) for i in range(n_cols)])
-        wide = lax.dynamic_update_slice_in_dim(wide, got[None], (col + n_cols - k) % n_cols, 0)
-    wide = wide.reshape((radix,) + left.shape[1:])
-    y_msg = jnp.concatenate(zs, 0)
+        got = lax.ppermute(left, "cols", [(i, i ^ k) for i in range(n_cols)])
+        wide = lax.dynamic_update_slice_in_dim(wide, got[None], own ^ k, 0)
+    lefts = wide.reshape((1, radix) + left.shape[1:])
+    y_msg = right
+    half = radix // 2
+    while half:
+        pairs = [(i, i ^ (4 * half)) for i in range(n_rows)]
+        y_msg = jnp.concatenate([y_msg, lax.ppermute(y_msg, "rows", pairs)], 0)
+        lefts = jnp.concatenate([lefts[:, :half], lax.ppermute(lefts[:, half:], "rows", pairs)], 0)
+        half //= 2
+    lefts = lefts[:, 0]
     y_got = lax.ppermute(y_msg, "rows", pair_y)
-    z = lax.axis_index("rows") // 4
-    lefts = []
-    for k in range(radix):
-        piece = lax.dynamic_index_in_dim(wide, (z + k) % radix, 0, keepdims=False)
-        lefts.append(lax.ppermute(piece, "rows", shift(k)) if k else piece)
-    lefts = jnp.stack(lefts)
     c_got = lax.ppermute(jnp.concatenate([y_msg, y_got], 0), "rows", pair_c)
     left_y = lax.ppermute(lefts[:, 1], "rows", pair_y)
     left_c = lax.ppermute(jnp.concatenate([lefts[:, 0, 1], left_y[:, 1]], 0), "rows", pair_c)
@@ -343,7 +346,7 @@
         hbm=(0, 1, 2, 3, 4, 5),
     )(
         contact_embedding, pairwise_final_matrix, edge_source_matrix, edge_target_matrix,
-        edge_final_sigmoid_matrix, presence, zs[-1],
+        edge_final_sigmoid_matrix, presence, y_msg,
     )
     args = [y_msg, y_got, c_got, lefts, left_y, left_c, contact_t, live, w_o, w_p]
     first, gate, panels = call(
@@ -352,7 +355,7 @@
         [
             pltpu.VMEM((tile_rows, chans * chans, cols), BF16),
             pltpu.VMEM((LANES, cols), F32),
-            pltpu.VMEM((2, width * tile_rows, cols), F32),
+            pltpu.VMEM((2, width * (tile_rows + PAD), cols), F32),
         ],
         ins=range(len(args)),
     )(*args)
@@ -372,9 +375,9 @@
         finish_kernel,
         jax.ShapeDtypeStruct((tile_rows, cols, pair_feats), F32),
         [
-            pltpu.VMEM((width * tile_rows, cols), F32),
+            pltpu.VMEM((width * (tile_rows + PAD), cols), F32),
             pltpu.VMEM((tile_rows, cols, pair_feats), F32),
-            pltpu.SemaphoreType.DMA((tile_rows // 2,)),
+            pltpu.SemaphoreType.DMA((tile_rows // GROUP,)),
         ],
         ins=(0, 1, 2, 3, 4, 5),
         out_specs=pl.BlockSpec(memory_space=pl.ANY),

time: 91.3 us -> 87.6 us (0.959)
  Pallas kernels: 15.7 us -> 11.7 us
  waiting for transfers between devices: 20.7 us -> 22.9 us
  local copies, waits for them, and re-layouts: 2.02 us -> 0.51 us
    pallas_call x5, Pallas kernels: 15.7 us -> 11.7 us  [run(): pl.pallas_call(kernel, out_shape=out_shape, in_specs=[VMEM] * len(args),...]
    ppermute x1, waiting for transfers between devices: 0.01 us -> 1.94 us  [on_device(): y_got = lax.ppermute(y_msg, 'rows', pair_y)]
    unnamed x13 -> x11, local copies, waits for them, and re-layouts: 1.84 us -> 0.37 us
    all_to_all x1, waiting for transfers between devices: 14.1 us -> 15.5 us  [on_device(): lax.all_to_all(product, ('rows', 'cols'), split_axis=0, concat_axis=0, ti...]
    ppermute x1, starting transfers between devices: 2.24 us -> 0.99 us  [on_device(): lax.ppermute(jnp.concatenate([lefts[:, 0, 1], left_y[:, 1]], 0), 'rows',...]
    ppermute x7 -> x5, starting transfers between devices: 8.62 us -> 9.82 us  [the longest x2 3.92 us: on_device(): lax.ppermute(lefts[:, half:], 'rows', pairs)]
    ppermute x7 -> x5, waiting for transfers between devices: 6.63 us -> 5.44 us  [the longest x2 3.76 us: on_device(): lax.ppermute(lefts[:, half:], 'rows', pairs)]
  transfers between devices with their start and end apart: 12 -> 10, of which waited for: 4 -> 5; matrix products, arithmetic and copies ran while one was open for 1% -> 1% of each run, Pallas kernels for 2% -> 2%
where the time goes in v5:
time: 87.6 us; the launch traced here: 87.4 us
  blocking collectives  30.4 us (35%)
  waiting for transfers between devices  22.9 us (26%)
  starting transfers between devices  21.7 us (25%)
  Pallas kernels  11.7 us (13%)
    all_to_all x1, blocking collectives, on_device(): lax.all_to_all(panels.reshape(devices, width // devices, 2, tile_rows, co...  30.4 us
    all_to_all x1, waiting for transfers between devices, on_device(): lax.all_to_all(product, ('rows', 'cols'), split_axis=0, concat_axis=0, ti...  15.5 us
    pallas_call x5, Pallas kernels, run(): pl.pallas_call(kernel, out_shape=out_shape, in_specs=[VMEM] * len(args),...  11.7 us
    ppermute x1, starting transfers between devices, on_device(): c_got = lax.ppermute(jnp.concatenate([y_msg, y_got], 0), 'rows', pair_c)  4.5 us
    ppermute x2, starting transfers between devices, on_device(): lax.ppermute(lefts[:, half:], 'rows', pairs)  3.92 us
    ppermute x2, starting transfers between devices, on_device(): y_msg = jnp.concatenate([y_msg, lax.ppermute(y_msg, 'rows', pairs)], 0)  3.81 us
    ppermute x2, waiting for transfers between devices, on_device(): lax.ppermute(lefts[:, half:], 'rows', pairs)  3.76 us
    all_to_all x1, starting transfers between devices, on_device(): lax.all_to_all(product, ('rows', 'cols'), split_axis=0, concat_axis=0, ti...  3.76 us
  transfers between devices with their start and end apart: 10, of which 5 were waited for; matrix products, arithmetic and copies ran while one was open for 1% of the time, Pallas kernels for 2%

profile of v5, /device:TPU:1, one launch (start us, length us, event | category | flops | bytes accessed | tf_op | source)
XLA Modules:
  0.0 87.4 jit_solution(15866018795539249918)
XLA Ops:
  0.0 2.9 %shard_map.127 = (bf16[272,128]{1,0:T(8,128)(2,1)S(1)}, bf16[2,2,2,48,128]{4,3,2,1,0:T(8,128)(2,1)S(1)}) custom-call(f32[8,128,256]{2,1,0:T(8,128)} %fam_ref.1, s32[8,128]{1,0:T(8,128)} %keep_ref.1, s32[2,128]{1,0:T(2,128)} %bitcast.29, bf16[32,256]{1,0:T(8,128)(2,1)} %bitcast.27, bf16[32,256]{1,0:T(8,128)(2,1)} %bitcast.28), custom_call_target="tpu_custom_call" | custom-call | tf_op jit(solution)/shard_map/pallas_call | solution.py:42
  2.9 2.1 %collective-permute-start.4 = (bf16[2,2,2,48,128]{4,3,2,1,0:T(8,128)(2,1)S(1)}, bf16[2,2,2,48,128]{4,3,2,1,0:T(8,128)(2,1)S(1)}, u32[]{:S(2)}, u32[]{:S(2)}) collective-permute-start(bf16[2,2,2,48,128]{4,3,2,1,0:T(8,128)(2,1)S(1)} %get-tuple-element.15), channel_id=1, source_target_pairs={{0,1},{1,0},{2,3},{3,2},{4,5},{5,4},{6,7},{7,6},{8,9},{9,8},{10,11... | collective-permute-start | bytes 294920 | tf_op jit(solution)/shard_map/ppermute | solution.py:319
  5.0 2.3 %collective-permute-start = (bf16[272,128]{1,0:T(8,128)(2,1)S(1)}, bf16[272,128]{1,0:T(8,128)(2,1)S(1)}, u32[]{:S(2)}, u32[]{:S(2)}) collective-permute-start(bf16[272,128]{1,0:T(8,128)(2,1)S(1)} %get-tuple-element.14), channel_id=1, source_target_pairs={{0,16},{2,18},{4,20},{6,22},{8,24},{10,26},{12,28},{14,30},{16,0},... | collective-permute-start | bytes 208904 | tf_op jit(solution)/shard_map/ppermute | solution.py:326
  7.4 1.7 %collective-permute-done = bf16[272,128]{1,0:T(8,128)(2,1)S(1)} collective-permute-done((bf16[272,128]{1,0:T(8,128)(2,1)S(1)}, bf16[272,128]{1,0:T(8,128)(2,1)S(1)}, u32[]{:S(2)}, u32[]{:S(2)}) %collective-permute-start) | collective-permute-done | bytes 69664 | tf_op jit(solution)/shard_map/ppermute | solution.py:326
  9.1 1.5 %collective-permute-start.1 = (bf16[544,128]{1,0:T(8,128)(2,1)S(1)}, bf16[544,128]{1,0:T(8,128)(2,1)S(1)}, u32[]{:S(2)}, u32[]{:S(2)}) collective-permute-start(bf16[544,128]{1,0:T(8,128)(2,1)S(1)} %pad_maximum_fusion.1), channel_id=1, source_target_pairs={{0,8},{2,10},{4,12},{6,14},{8,0},{10,2},{12,4},{14,6},{16,24},{18,... | collective-permute-start | bytes 417800 | tf_op jit(solution)/shard_map/ppermute | solution.py:326
  10.6 0.0 collective-permute-done.4
  10.7 2.9 %collective-permute-start.5 = (bf16[1,2,2,2,48,128]{5,4,0,3,2,1:T(8,128)(2,1)S(1)}, bf16[1,2,2,2,48,128]{5,4,0,3,2,1:T(8,128)(2,1)S(1)}, u32[]{:S(2)}, u32[]{:S(2)}) collective-permute-start(bf16[1,2,2,2,48,128]{5,4,0,3,2,1:T(8,128)(2,1)S(1)} %get-tuple-element.26), channel_id=1, source_target_pairs={{0,16},{2,18},{4,20},{6,22},{8,24},{10,26},{12,28},{14,30},{16,0},... | collective-permute-start | bytes 294920 | tf_op jit(solution)/shard_map/ppermute | solution.py:327
  13.6 2.6 %collective-permute-done.5 = bf16[1,2,2,2,48,128]{5,4,0,3,2,1:T(8,128)(2,1)S(1)} collective-permute-done((bf16[1,2,2,2,48,128]{5,4,0,3,2,1:T(8,128)(2,1)S(1)}, bf16[1,2,2,2,48,128]{5,4,0,3,2,1:T(8,128)(2,1)S(1)}, u32[]{:S(2)}, u32[]{:S(2)}) %collective-permute-start.5) | collective-permute-done | bytes 98336 | tf_op jit(solution)/shard_map/ppermute | solution.py:327
  16.2 1.0 %collective-permute-start.6 = (bf16[2,1,2,2,48,128]{5,4,0,3,2,1:T(8,128)(2,1)S(1)}, bf16[2,1,2,2,48,128]{5,4,0,3,2,1:T(8,128)(2,1)S(1)}, u32[]{:S(2)}, u32[]{:S(2)}) collective-permute-start(bf16[2,1,2,2,48,128]{5,4,0,3,2,1:T(8,128)(2,1)S(1)} %get-tuple-element.24), channel_id=1, source_target_pairs={{0,8},{2,10},{4,12},{6,14},{8,0},{10,2},{12,4},{14,6},{16,24},{18,... | collective-permute-start | bytes 294920 | tf_op jit(solution)/shard_map/ppermute | solution.py:327
  17.2 0.0 collective-permute-done.1
  17.2 1.3 %collective-permute-start.2 = (bf16[1088,128]{1,0:T(8,128)(2,1)S(1)}, bf16[1088,128]{1,0:T(8,128)(2,1)S(1)}, u32[]{:S(2)}, u32[]{:S(2)}) collective-permute-start(bf16[1088,128]{1,0:T(8,128)(2,1)S(1)} %constant_dynamic-update-slice_fusion.after_ref.z_ref), channel_id=1, source_target_pairs={{0,4},{2,6},{4,0},{6,2},{8,12},{10,14},{12,8},{14,10},{16,20},{18,... | collective-permute-start | bytes 835592 | tf_op jit(solution)/shard_map/ppermute | solution.py:330
  18.5 1.2 %collective-permute-done.6 = bf16[2,1,2,2,48,128]{5,4,0,3,2,1:T(8,128)(2,1)S(1)} collective-permute-done((bf16[2,1,2,2,48,128]{5,4,0,3,2,1:T(8,128)(2,1)S(1)}, bf16[2,1,2,2,48,128]{5,4,0,3,2,1:T(8,128)(2,1)S(1)}, u32[]{:S(2)}, u32[]{:S(2)}) %collective-permute-start.6) | collective-permute-done | bytes 98336 | tf_op jit(solution)/shard_map/ppermute | solution.py:327
  19.7 1.3 %collective-permute-start.7 = (bf16[4,2,48,128]{3,2,0,1:T(8,128)(2,1)S(1)}, bf16[4,2,48,128]{3,2,0,1:T(8,128)(2,1)S(1)}, u32[]{:S(2)}, u32[]{:S(2)}) collective-permute-start(bf16[4,2,48,128]{3,2,0,1:T(8,128)(2,1)S(1)} %slice_bitcast_fusion), channel_id=1, source_target_pairs={{0,4},{2,6},{4,0},{6,2},{8,12},{10,14},{12,8},{14,10},{16,20},{18,... | collective-permute-start | bytes 294920 | tf_op jit(solution)/shard_map/ppermute | solution.py:332
  21.1 1.9 %collective-permute-done.2.y_ref = bf16[1088,128]{1,0:T(8,128)(2,1)S(1)} collective-permute-done((bf16[1088,128]{1,0:T(8,128)(2,1)S(1)}, bf16[1088,128]{1,0:T(8,128)(2,1)S(1)}, u32[]{:S(2)}, u32[]{:S(2)}) %collective-permute-start.2) | collective-permute-done | bytes 278560 | tf_op jit(solution)/shard_map/ppermute | solution.py:330
  23.0 4.5 %collective-permute-start.3 = (bf16[2176,128]{1,0:T(8,128)(2,1)S(1)}, bf16[2176,128]{1,0:T(8,128)(2,1)S(1)}, u32[]{:S(2)}, u32[]{:S(2)}) collective-permute-start(bf16[2176,128]{1,0:T(8,128)(2,1)S(1)} %pad_maximum_fusion), channel_id=1, source_target_pairs={{0,2},{2,0},{4,6},{6,4},{8,10},{10,8},{12,14},{14,12},{16,18},{18,... | collective-permute-start | bytes 1671176 | tf_op jit(solution)/shard_map/ppermute | solution.py:331
  27.5 0.0 collective-permute-done.7
  27.6 1.0 %collective-permute-start.8 = (bf16[8,48,128]{2,1,0:T(8,128)(2,1)S(1)}, bf16[8,48,128]{2,1,0:T(8,128)(2,1)S(1)}, u32[]{:S(2)}, u32[]{:S(2)}) collective-permute-start(bf16[8,48,128]{2,1,0:T(8,128)(2,1)S(1)} %pad_maximum_fusion.3), channel_id=1, source_target_pairs={{0,2},{2,0},{4,6},{6,4},{8,10},{10,8},{12,14},{14,12},{16,18},{18,... | collective-permute-start | bytes 294920 | tf_op jit(solution)/shard_map/ppermute | solution.py:333
  28.6 2.0 %shard_map.128 = (f32[16,128,128]{2,1,0:T(8,128)S(1)}, bf16[128,1024]{1,0:T(8,128)(2,1)S(1)}, bf16[640,128]{1,0:T(8,128)(2,1)S(1)}, f32[16,128]{1,0:T(8,128)S(1)}) custom-call(f32[16,128,128]{2,1,0:T(8,128)} %contact_ref.1, bf16[1024,128]{1,0:T(8,128)(2,1)} %wo_ref.1, bf16[128,256]{1,0:T(8,128)(2,1)} %src_ref.1, bf16[128,256]{1,0:T(8,128)(2,1)} %tgt_ref.1, ...), custom_call_target="tpu_custom_call" | custom-call | tf_op jit(solution)/shard_map/pallas_call | solution.py:42
  30.6 0.0 collective-permute-done.8.left_c_ref
  30.7 0.0 collective-permute-done.3.c_ref
  30.7 2.8 %shard_map.129 = (f32[16,128,128]{2,1,0:T(8,128)S(1)}, f32[16,128,128]{2,1,0:T(8,128)S(1)}, bf16[128,2,16,128]{3,2,1,0:T(8,128)(2,1)S(1)}) custom-call(bf16[1088,128]{1,0:T(8,128)(2,1)S(1)} %constant_dynamic-update-slice_fusion.after_ref.z_ref, bf16[1088,128]{1,0:T(8,128)(2,1)S(1)} %collective-permute-done.2.y_ref, ...), custom_call_target="tpu_custom_call" | custom-call | tf_op jit(solution)/shard_map/pallas_call | solution.py:42
  33.4 30.4 %all_to_all.10.recv_ref = bf16[32,4,2,16,128]{4,3,2,1,0:T(8,128)(2,1)S(1)} all-to-all(bf16[32,4,2,16,128]{4,3,2,1,0:T(8,128)(2,1)S(1)} %bitcast.22), channel_id=1, replica_groups=mesh['crops'=1,'rows'=16,'cols'=2] {'rows','cols'}, dimensions={0} | all-to-all | bytes 2097152 | tf_op jit(solution)/shard_map/all_to_all | solution.py:363
  63.8 0.0 copy-start
  63.8 1.1 %shard_map.130 = bf16[32,4,16,128]{3,2,1,0:T(8,128)(2,1)} custom-call(bf16[32,4,2,16,128]{4,3,2,1,0:T(8,128)(2,1)S(1)} %all_to_all.10.recv_ref), custom_call_target="tpu_custom_call" | custom-call | tf_op jit(solution)/shard_map/pallas_call | solution.py:42
  64.9 0.0 copy-start.1
  64.9 0.0 copy-start.2
  64.9 3.8 %all-to-all-start.1 = ((bf16[32,4,16,128]{3,2,1,0:T(8,128)(2,1)}), bf16[32,4,16,128]{3,2,1,0:T(8,128)(2,1)S(1)}, u32[]{:S(2)}, u32[]{:S(2)}) async-start(bf16[32,4,16,128]{3,2,1,0:T(8,128)(2,1)} %shard_map.130), calls=%async_computation.1 | async-start | bytes 1048576 | tf_op jit(solution)/shard_map/all_to_all | solution.py:373
  68.7 0.0 copy-done
  68.7 0.1 copy.17
  68.8 0.0 copy-done.1
  68.8 0.1 copy.18
  69.0 0.0 copy-done.2
  69.0 0.1 copy.16
  69.1 15.5 %all-to-all-done.1 = bf16[32,4,16,128]{3,2,1,0:T(8,128)(2,1)S(1)} async-done(((bf16[32,4,16,128]{3,2,1,0:T(8,128)(2,1)}), bf16[32,4,16,128]{3,2,1,0:T(8,128)(2,1)S(1)}, u32[]{:S(2)}, u32[]{:S(2)}) %all-to-all-start.1) | async-done | bytes 524320 | tf_op jit(solution)/shard_map/all_to_all | solution.py:373
  84.5 2.8 %shard_map.131 = f32[16,128,128]{2,1,0:T(8,128)} custom-call(bf16[128,16,128]{2,1,0:T(8,128)(2,1)S(1)} %bitcast.21, f32[16,128,128]{2,1,0:T(8,128)S(1)} %get-tuple-element.21.first_ref, f32[16,128,128]{2,1,0:T(8,128)S(1)} %get-tuple-element.22.gate_ref, bf16[128,128]{1,0:T(8,128)(2,1)S(1)} %bitcast.25, bf16[512,128]{1,0:T(8,128)(2,1)S(1)} %bitcast.23, ...), custom_call_target="tpu_custom_call" | custom-call | tf_op jit(solution)/shard_map/pallas_call | solution.py:42
  (17 shorter events, 0.3 us)
Async XLA Ops:
  2.9 7.7 %collective-permute-start.4 = (bf16[2,2,2,48,128]{4,3,2,1,0:T(8,128)(2,1)S(1)}, bf16[2,2,2,48,128]{4,3,2,1,0:T(8,128)(2,1)S(1)}, u32[]{:S(2)}, u32[]{:S(2)}) collective-permute-start(bf16[2,2,2,48,128]{4,3,2,1,0:T(8,128)(2,1)S(1)} %get-tuple-element.15), channel_id=1, source_target_pairs={{0,1},{1,0},{2,3},{3,2},{4,5},{5,4},{6,7},{7,6},{8,9},{9,8},{10,11... | collective-permute-start | bytes 294920 | tf_op jit(solution)/shard_map/ppermute | solution.py:319
  5.0 4.1 %collective-permute-start = (bf16[272,128]{1,0:T(8,128)(2,1)S(1)}, bf16[272,128]{1,0:T(8,128)(2,1)S(1)}, u32[]{:S(2)}, u32[]{:S(2)}) collective-permute-start(bf16[272,128]{1,0:T(8,128)(2,1)S(1)} %get-tuple-element.14), channel_id=1, source_target_pairs={{0,16},{2,18},{4,20},{6,22},{8,24},{10,26},{12,28},{14,30},{16,0},... | collective-permute-start | bytes 208904 | tf_op jit(solution)/shard_map/ppermute | solution.py:326
  9.1 8.1 %collective-permute-start.1 = (bf16[544,128]{1,0:T(8,128)(2,1)S(1)}, bf16[544,128]{1,0:T(8,128)(2,1)S(1)}, u32[]{:S(2)}, u32[]{:S(2)}) collective-permute-start(bf16[544,128]{1,0:T(8,128)(2,1)S(1)} %pad_maximum_fusion.1), channel_id=1, source_target_pairs={{0,8},{2,10},{4,12},{6,14},{8,0},{10,2},{12,4},{14,6},{16,24},{18,... | collective-permute-start | bytes 417800 | tf_op jit(solution)/shard_map/ppermute | solution.py:326
  10.7 5.5 %collective-permute-start.5 = (bf16[1,2,2,2,48,128]{5,4,0,3,2,1:T(8,128)(2,1)S(1)}, bf16[1,2,2,2,48,128]{5,4,0,3,2,1:T(8,128)(2,1)S(1)}, u32[]{:S(2)}, u32[]{:S(2)}) collective-permute-start(bf16[1,2,2,2,48,128]{5,4,0,3,2,1:T(8,128)(2,1)S(1)} %get-tuple-element.26), channel_id=1, source_target_pairs={{0,16},{2,18},{4,20},{6,22},{8,24},{10,26},{12,28},{14,30},{16,0},... | collective-permute-start | bytes 294920 | tf_op jit(solution)/shard_map/ppermute | solution.py:327
  16.2 3.5 %collective-permute-start.6 = (bf16[2,1,2,2,48,128]{5,4,0,3,2,1:T(8,128)(2,1)S(1)}, bf16[2,1,2,2,48,128]{5,4,0,3,2,1:T(8,128)(2,1)S(1)}, u32[]{:S(2)}, u32[]{:S(2)}) collective-permute-start(bf16[2,1,2,2,48,128]{5,4,0,3,2,1:T(8,128)(2,1)S(1)} %get-tuple-element.24), channel_id=1, source_target_pairs={{0,8},{2,10},{4,12},{6,14},{8,0},{10,2},{12,4},{14,6},{16,24},{18,... | collective-permute-start | bytes 294920 | tf_op jit(solution)/shard_map/ppermute | solution.py:327
  17.2 5.8 %collective-permute-start.2 = (bf16[1088,128]{1,0:T(8,128)(2,1)S(1)}, bf16[1088,128]{1,0:T(8,128)(2,1)S(1)}, u32[]{:S(2)}, u32[]{:S(2)}) collective-permute-start(bf16[1088,128]{1,0:T(8,128)(2,1)S(1)} %constant_dynamic-update-slice_fusion.after_ref.z_ref), channel_id=1, source_target_pairs={{0,4},{2,6},{4,0},{6,2},{8,12},{10,14},{12,8},{14,10},{16,20},{18,... | collective-permute-start | bytes 835592 | tf_op jit(solution)/shard_map/ppermute | solution.py:330
  19.7 7.8 %collective-permute-start.7 = (bf16[4,2,48,128]{3,2,0,1:T(8,128)(2,1)S(1)}, bf16[4,2,48,128]{3,2,0,1:T(8,128)(2,1)S(1)}, u32[]{:S(2)}, u32[]{:S(2)}) collective-permute-start(bf16[4,2,48,128]{3,2,0,1:T(8,128)(2,1)S(1)} %slice_bitcast_fusion), channel_id=1, source_target_pairs={{0,4},{2,6},{4,0},{6,2},{8,12},{10,14},{12,8},{14,10},{16,20},{18,... | collective-permute-start | bytes 294920 | tf_op jit(solution)/shard_map/ppermute | solution.py:332
  23.0 7.6 %collective-permute-start.3 = (bf16[2176,128]{1,0:T(8,128)(2,1)S(1)}, bf16[2176,128]{1,0:T(8,128)(2,1)S(1)}, u32[]{:S(2)}, u32[]{:S(2)}) collective-permute-start(bf16[2176,128]{1,0:T(8,128)(2,1)S(1)} %pad_maximum_fusion), channel_id=1, source_target_pairs={{0,2},{2,0},{4,6},{6,4},{8,10},{10,8},{12,14},{14,12},{16,18},{18,... | collective-permute-start | bytes 1671176 | tf_op jit(solution)/shard_map/ppermute | solution.py:331
  27.6 3.1 %collective-permute-start.8 = (bf16[8,48,128]{2,1,0:T(8,128)(2,1)S(1)}, bf16[8,48,128]{2,1,0:T(8,128)(2,1)S(1)}, u32[]{:S(2)}, u32[]{:S(2)}) collective-permute-start(bf16[8,48,128]{2,1,0:T(8,128)(2,1)S(1)} %pad_maximum_fusion.3), channel_id=1, source_target_pairs={{0,2},{2,0},{4,6},{6,4},{8,10},{10,8},{12,14},{14,12},{16,18},{18,... | collective-permute-start | bytes 294920 | tf_op jit(solution)/shard_map/ppermute | solution.py:333
  63.8 4.9 %copy-start = (bf16[128,512]{1,0:T(8,128)(2,1)S(1)}, bf16[128,512]{1,0:T(8,128)(2,1)}, u32[]{:S(2)}) copy-start(bf16[128,512]{1,0:T(8,128)(2,1)} %param.24) | copy-start | bytes 393220
  64.9 3.9 %copy-start.1 = (bf16[512,128]{1,0:T(8,128)(2,1)S(1)}, bf16[512,128]{1,0:T(8,128)(2,1)}, u32[]{:S(2)}) copy-start(bf16[512,128]{1,0:T(8,128)(2,1)} %param.25) | copy-start | bytes 393220
  64.9 4.0 %copy-start.2 = (bf16[128,128]{1,0:T(8,128)(2,1)S(1)}, bf16[128,128]{1,0:T(8,128)(2,1)}, u32[]{:S(2)}) copy-start(bf16[128,128]{1,0:T(8,128)(2,1)} %param.23) | copy-start | bytes 98308
  64.9 19.6 %all-to-all-start.1 = ((bf16[32,4,16,128]{3,2,1,0:T(8,128)(2,1)}), bf16[32,4,16,128]{3,2,1,0:T(8,128)(2,1)S(1)}, u32[]{:S(2)}, u32[]{:S(2)}) async-start(bf16[32,4,16,128]{3,2,1,0:T(8,128)(2,1)} %shard_map.130), calls=%async_computation.1 | async-start | bytes 1048576 | tf_op jit(solution)/shard_map/all_to_all | solution.py:373

commit v6 on v5

--- a/solution.py
+++ b/solution.py
@@ -16,6 +16,7 @@
 VMEM_LIMIT = 32 * 2**20
 PAD = 8
 GROUP = 16
+SEND = 4
 VMEM = pl.BlockSpec(memory_space=pltpu.VMEM)
 
 
@@ -97,7 +98,7 @@
     for p in range(pieces):
         at = ((p // 4) ^ z, lax.rem((p // 2) % 2 + y, 2), lax.rem(p % 2 + c, 2))
         left_ref[at[0], at[1], at[2], 0:block, :] = acc[p * block : (p + 1) * block].astype(BF16)
-        left_ref[at[0], at[1], at[2], block : block + TILE, :] = live_tile
+        left_ref[at[0], at[1], at[2], block : block + seqs, :] = live_tile[:seqs]
 
 
 def prepare_kernel(
@@ -265,9 +266,11 @@
         out = dot(w_2, hidden)
         for k in range(GROUP):
             out_ref[i + k] = (seconds[k] + out[:, k * cols : (k + 1) * cols]).T
-        copy = pltpu.make_async_copy(out_ref.at[pl.ds(i, GROUP)], hbm_ref.at[pl.ds(i, GROUP)], sems.at[i // GROUP])
-        copy.start()
-        copies.append(copy)
+            if (k + 1) % SEND == 0:
+                part = pl.ds(i + k + 1 - SEND, SEND)
+                copy = pltpu.make_async_copy(out_ref.at[part], hbm_ref.at[part], sems.at[(i + k) // SEND])
+                copy.start()
+                copies.append(copy)
     for copy in copies:
         copy.wait()
 
@@ -302,7 +305,7 @@
     planes = pieces // 4
 
     right_rows = chans * seqs + TILE
-    left_rows = tile_rows * chans * seqs // LANES + TILE
+    left_rows = tile_rows * chans * seqs // LANES + seqs
     right, left = call(
         functools.partial(project_kernel, tile_rows=tile_rows),
         (shape((right_rows, cols), BF16), shape((pieces // 4, 2, 2, left_rows, LANES), BF16)),
@@ -377,7 +380,7 @@
         [
             pltpu.VMEM((width * (tile_rows + PAD), cols), F32),
             pltpu.VMEM((tile_rows, cols, pair_feats), F32),
-            pltpu.SemaphoreType.DMA((tile_rows // GROUP,)),
+            pltpu.SemaphoreType.DMA((tile_rows // SEND,)),
         ],
         ins=(0, 1, 2, 3, 4, 5),
         out_specs=pl.BlockSpec(memory_space=pl.ANY),

time: 87.6 us -> 86.8 us (level)
  no operation moved by 1% of the time
where the time goes in v6:
time: 86.8 us; the launch traced here: 86.6 us
  blocking collectives  30.4 us (35%)
  waiting for transfers between devices  22.5 us (26%)
  starting transfers between devices  21.3 us (25%)
  Pallas kernels  11.5 us (13%)
    all_to_all x1, blocking collectives, on_device(): lax.all_to_all(panels.reshape(devices, width // devices, 2, tile_rows, co...  30.4 us
    all_to_all x1, waiting for transfers between devices, on_device(): lax.all_to_all(product, ('rows', 'cols'), split_axis=0, concat_axis=0, ti...  15.5 us
    pallas_call x5, Pallas kernels, run(): pl.pallas_call(kernel, out_shape=out_shape, in_specs=[VMEM] * len(args),...  11.5 us
    ppermute x1, starting transfers between devices, on_device(): c_got = lax.ppermute(jnp.concatenate([y_msg, y_got], 0), 'rows', pair_c)  4.32 us
    ppermute x2, starting transfers between devices, on_device(): lax.ppermute(lefts[:, half:], 'rows', pairs)  3.92 us
    ppermute x2, starting transfers between devices, on_device(): y_msg = jnp.concatenate([y_msg, lax.ppermute(y_msg, 'rows', pairs)], 0)  3.81 us
    all_to_all x1, starting transfers between devices, on_device(): lax.all_to_all(product, ('rows', 'cols'), split_axis=0, concat_axis=0, ti...  3.76 us
    ppermute x2, waiting for transfers between devices, on_device(): lax.ppermute(lefts[:, half:], 'rows', pairs)  3.23 us
  transfers between devices with their start and end apart: 10, of which 5 were waited for; matrix products, arithmetic and copies ran while one was open for 1% of the time, Pallas kernels for 2%

profile of v6, /device:TPU:1, one launch (start us, length us, event | category | flops | bytes accessed | tf_op | source)
XLA Modules:
  0.0 86.6 jit_solution(13582140060427185494)
XLA Ops:
  0.0 2.9 %shard_map.127 = (bf16[272,128]{1,0:T(8,128)(2,1)S(1)}, bf16[2,2,2,40,128]{4,3,2,1,0:T(8,128)(2,1)S(1)}) custom-call(f32[8,128,256]{2,1,0:T(8,128)} %fam_ref.1, s32[8,128]{1,0:T(8,128)} %keep_ref.1, s32[2,128]{1,0:T(2,128)} %bitcast.29, bf16[32,256]{1,0:T(8,128)(2,1)} %bitcast.27, bf16[32,256]{1,0:T(8,128)(2,1)} %bitcast.28), custom_call_target="tpu_custom_call" | custom-call | tf_op jit(solution)/shard_map/pallas_call | solution.py:43
  2.9 2.1 %collective-permute-start.4 = (bf16[2,2,2,40,128]{4,3,2,1,0:T(8,128)(2,1)S(1)}, bf16[2,2,2,40,128]{4,3,2,1,0:T(8,128)(2,1)S(1)}, u32[]{:S(2)}, u32[]{:S(2)}) collective-permute-start(bf16[2,2,2,40,128]{4,3,2,1,0:T(8,128)(2,1)S(1)} %get-tuple-element.15), channel_id=1, source_target_pairs={{0,1},{1,0},{2,3},{3,2},{4,5},{5,4},{6,7},{7,6},{8,9},{9,8},{10,11... | collective-permute-start | bytes 245768 | tf_op jit(solution)/shard_map/ppermute | solution.py:322
  5.0 2.3 %collective-permute-start = (bf16[272,128]{1,0:T(8,128)(2,1)S(1)}, bf16[272,128]{1,0:T(8,128)(2,1)S(1)}, u32[]{:S(2)}, u32[]{:S(2)}) collective-permute-start(bf16[272,128]{1,0:T(8,128)(2,1)S(1)} %get-tuple-element.14), channel_id=1, source_target_pairs={{0,16},{2,18},{4,20},{6,22},{8,24},{10,26},{12,28},{14,30},{16,0},... | collective-permute-start | bytes 208904 | tf_op jit(solution)/shard_map/ppermute | solution.py:329
  7.4 1.7 %collective-permute-done = bf16[272,128]{1,0:T(8,128)(2,1)S(1)} collective-permute-done((bf16[272,128]{1,0:T(8,128)(2,1)S(1)}, bf16[272,128]{1,0:T(8,128)(2,1)S(1)}, u32[]{:S(2)}, u32[]{:S(2)}) %collective-permute-start) | collective-permute-done | bytes 69664 | tf_op jit(solution)/shard_map/ppermute | solution.py:329
  9.1 1.5 %collective-permute-start.1 = (bf16[544,128]{1,0:T(8,128)(2,1)S(1)}, bf16[544,128]{1,0:T(8,128)(2,1)S(1)}, u32[]{:S(2)}, u32[]{:S(2)}) collective-permute-start(bf16[544,128]{1,0:T(8,128)(2,1)S(1)} %pad_maximum_fusion.1), channel_id=1, source_target_pairs={{0,8},{2,10},{4,12},{6,14},{8,0},{10,2},{12,4},{14,6},{16,24},{18,... | collective-permute-start | bytes 417800 | tf_op jit(solution)/shard_map/ppermute | solution.py:329
  10.6 0.0 collective-permute-done.4
  10.7 2.9 %collective-permute-start.5 = (bf16[1,2,2,2,40,128]{5,4,0,3,2,1:T(8,128)(2,1)S(1)}, bf16[1,2,2,2,40,128]{5,4,0,3,2,1:T(8,128)(2,1)S(1)}, u32[]{:S(2)}, u32[]{:S(2)}) collective-permute-start(bf16[1,2,2,2,40,128]{5,4,0,3,2,1:T(8,128)(2,1)S(1)} %get-tuple-element.26), channel_id=1, source_target_pairs={{0,16},{2,18},{4,20},{6,22},{8,24},{10,26},{12,28},{14,30},{16,0},... | collective-permute-start | bytes 245768 | tf_op jit(solution)/shard_map/ppermute | solution.py:330
  13.6 2.2 %collective-permute-done.5 = bf16[1,2,2,2,40,128]{5,4,0,3,2,1:T(8,128)(2,1)S(1)} collective-permute-done((bf16[1,2,2,2,40,128]{5,4,0,3,2,1:T(8,128)(2,1)S(1)}, bf16[1,2,2,2,40,128]{5,4,0,3,2,1:T(8,128)(2,1)S(1)}, u32[]{:S(2)}, u32[]{:S(2)}) %collective-permute-start.5) | collective-permute-done | bytes 81952 | tf_op jit(solution)/shard_map/ppermute | solution.py:330
  15.8 1.0 %collective-permute-start.6 = (bf16[2,1,2,2,40,128]{5,4,0,3,2,1:T(8,128)(2,1)S(1)}, bf16[2,1,2,2,40,128]{5,4,0,3,2,1:T(8,128)(2,1)S(1)}, u32[]{:S(2)}, u32[]{:S(2)}) collective-permute-start(bf16[2,1,2,2,40,128]{5,4,0,3,2,1:T(8,128)(2,1)S(1)} %get-tuple-element.24), channel_id=1, source_target_pairs={{0,8},{2,10},{4,12},{6,14},{8,0},{10,2},{12,4},{14,6},{16,24},{18,... | collective-permute-start | bytes 245768 | tf_op jit(solution)/shard_map/ppermute | solution.py:330
  16.9 0.0 collective-permute-done.1
  16.9 1.3 %collective-permute-start.2 = (bf16[1088,128]{1,0:T(8,128)(2,1)S(1)}, bf16[1088,128]{1,0:T(8,128)(2,1)S(1)}, u32[]{:S(2)}, u32[]{:S(2)}) collective-permute-start(bf16[1088,128]{1,0:T(8,128)(2,1)S(1)} %constant_dynamic-update-slice_fusion.after_ref.z_ref), channel_id=1, source_target_pairs={{0,4},{2,6},{4,0},{6,2},{8,12},{10,14},{12,8},{14,10},{16,20},{18,... | collective-permute-start | bytes 835592 | tf_op jit(solution)/shard_map/ppermute | solution.py:333
  18.2 1.0 %collective-permute-done.6 = bf16[2,1,2,2,40,128]{5,4,0,3,2,1:T(8,128)(2,1)S(1)} collective-permute-done((bf16[2,1,2,2,40,128]{5,4,0,3,2,1:T(8,128)(2,1)S(1)}, bf16[2,1,2,2,40,128]{5,4,0,3,2,1:T(8,128)(2,1)S(1)}, u32[]{:S(2)}, u32[]{:S(2)}) %collective-permute-start.6) | collective-permute-done | bytes 81952 | tf_op jit(solution)/shard_map/ppermute | solution.py:330
  19.2 1.3 %collective-permute-start.7 = (bf16[4,2,40,128]{3,2,0,1:T(8,128)(2,1)S(1)}, bf16[4,2,40,128]{3,2,0,1:T(8,128)(2,1)S(1)}, u32[]{:S(2)}, u32[]{:S(2)}) collective-permute-start(bf16[4,2,40,128]{3,2,0,1:T(8,128)(2,1)S(1)} %slice_bitcast_fusion), channel_id=1, source_target_pairs={{0,4},{2,6},{4,0},{6,2},{8,12},{10,14},{12,8},{14,10},{16,20},{18,... | collective-permute-start | bytes 245768 | tf_op jit(solution)/shard_map/ppermute | solution.py:335
  20.5 2.1 %collective-permute-done.2.y_ref = bf16[1088,128]{1,0:T(8,128)(2,1)S(1)} collective-permute-done((bf16[1088,128]{1,0:T(8,128)(2,1)S(1)}, bf16[1088,128]{1,0:T(8,128)(2,1)S(1)}, u32[]{:S(2)}, u32[]{:S(2)}) %collective-permute-start.2) | collective-permute-done | bytes 278560 | tf_op jit(solution)/shard_map/ppermute | solution.py:333
  22.7 4.3 %collective-permute-start.3 = (bf16[2176,128]{1,0:T(8,128)(2,1)S(1)}, bf16[2176,128]{1,0:T(8,128)(2,1)S(1)}, u32[]{:S(2)}, u32[]{:S(2)}) collective-permute-start(bf16[2176,128]{1,0:T(8,128)(2,1)S(1)} %pad_maximum_fusion), channel_id=1, source_target_pairs={{0,2},{2,0},{4,6},{6,4},{8,10},{10,8},{12,14},{14,12},{16,18},{18,... | collective-permute-start | bytes 1671176 | tf_op jit(solution)/shard_map/ppermute | solution.py:334
  27.0 0.0 collective-permute-done.7
  27.0 0.8 collective-permute-start.8
  27.9 2.0 %shard_map.128 = (f32[16,128,128]{2,1,0:T(8,128)S(1)}, bf16[128,1024]{1,0:T(8,128)(2,1)S(1)}, bf16[640,128]{1,0:T(8,128)(2,1)S(1)}, f32[16,128]{1,0:T(8,128)S(1)}) custom-call(f32[16,128,128]{2,1,0:T(8,128)} %contact_ref.1, bf16[1024,128]{1,0:T(8,128)(2,1)} %wo_ref.1, bf16[128,256]{1,0:T(8,128)(2,1)} %src_ref.1, bf16[128,256]{1,0:T(8,128)(2,1)} %tgt_ref.1, ...), custom_call_target="tpu_custom_call" | custom-call | tf_op jit(solution)/shard_map/pallas_call | solution.py:43
  29.9 0.0 collective-permute-done.8.left_c_ref
  29.9 0.0 collective-permute-done.3.c_ref
  30.0 2.8 %shard_map.129 = (f32[16,128,128]{2,1,0:T(8,128)S(1)}, f32[16,128,128]{2,1,0:T(8,128)S(1)}, bf16[128,2,16,128]{3,2,1,0:T(8,128)(2,1)S(1)}) custom-call(bf16[1088,128]{1,0:T(8,128)(2,1)S(1)} %constant_dynamic-update-slice_fusion.after_ref.z_ref, bf16[1088,128]{1,0:T(8,128)(2,1)S(1)} %collective-permute-done.2.y_ref, ...), custom_call_target="tpu_custom_call" | custom-call | tf_op jit(solution)/shard_map/pallas_call | solution.py:43
  32.7 30.4 %all_to_all.10.recv_ref = bf16[32,4,2,16,128]{4,3,2,1,0:T(8,128)(2,1)S(1)} all-to-all(bf16[32,4,2,16,128]{4,3,2,1,0:T(8,128)(2,1)S(1)} %bitcast.22), channel_id=1, replica_groups=mesh['crops'=1,'rows'=16,'cols'=2] {'rows','cols'}, dimensions={0} | all-to-all | bytes 2097152 | tf_op jit(solution)/shard_map/all_to_all | solution.py:366
  63.2 0.0 copy-start
  63.2 1.1 %shard_map.130 = bf16[32,4,16,128]{3,2,1,0:T(8,128)(2,1)} custom-call(bf16[32,4,2,16,128]{4,3,2,1,0:T(8,128)(2,1)S(1)} %all_to_all.10.recv_ref), custom_call_target="tpu_custom_call" | custom-call | tf_op jit(solution)/shard_map/pallas_call | solution.py:43
  64.3 0.0 copy-start.1
  64.3 0.0 copy-start.2
  64.3 3.8 %all-to-all-start.1 = ((bf16[32,4,16,128]{3,2,1,0:T(8,128)(2,1)}), bf16[32,4,16,128]{3,2,1,0:T(8,128)(2,1)S(1)}, u32[]{:S(2)}, u32[]{:S(2)}) async-start(bf16[32,4,16,128]{3,2,1,0:T(8,128)(2,1)} %shard_map.130), calls=%async_computation.1 | async-start | bytes 1048576 | tf_op jit(solution)/shard_map/all_to_all | solution.py:376
  68.1 0.0 copy-done
  68.1 0.1 copy.17
  68.2 0.0 copy-done.1
  68.2 0.1 copy.18
  68.3 0.0 copy-done.2
  68.3 0.1 copy.16
  68.5 15.5 %all-to-all-done.1 = bf16[32,4,16,128]{3,2,1,0:T(8,128)(2,1)S(1)} async-done(((bf16[32,4,16,128]{3,2,1,0:T(8,128)(2,1)}), bf16[32,4,16,128]{3,2,1,0:T(8,128)(2,1)S(1)}, u32[]{:S(2)}, u32[]{:S(2)}) %all-to-all-start.1) | async-done | bytes 524320 | tf_op jit(solution)/shard_map/all_to_all | solution.py:376
  83.9 2.6 %shard_map.131 = f32[16,128,128]{2,1,0:T(8,128)} custom-call(bf16[128,16,128]{2,1,0:T(8,128)(2,1)S(1)} %bitcast.21, f32[16,128,128]{2,1,0:T(8,128)S(1)} %get-tuple-element.21.first_ref, f32[16,128,128]{2,1,0:T(8,128)S(1)} %get-tuple-element.22.gate_ref, bf16[128,128]{1,0:T(8,128)(2,1)S(1)} %bitcast.25, bf16[512,128]{1,0:T(8,128)(2,1)S(1)} %bitcast.23, ...), custom_call_target="tpu_custom_call" | custom-call | tf_op jit(solution)/shard_map/pallas_call | solution.py:43
  (17 shorter events, 0.2 us)
Async XLA Ops:
  2.9 7.7 %collective-permute-start.4 = (bf16[2,2,2,40,128]{4,3,2,1,0:T(8,128)(2,1)S(1)}, bf16[2,2,2,40,128]{4,3,2,1,0:T(8,128)(2,1)S(1)}, u32[]{:S(2)}, u32[]{:S(2)}) collective-permute-start(bf16[2,2,2,40,128]{4,3,2,1,0:T(8,128)(2,1)S(1)} %get-tuple-element.15), channel_id=1, source_target_pairs={{0,1},{1,0},{2,3},{3,2},{4,5},{5,4},{6,7},{7,6},{8,9},{9,8},{10,11... | collective-permute-start | bytes 245768 | tf_op jit(solution)/shard_map/ppermute | solution.py:322
  5.0 4.1 %collective-permute-start = (bf16[272,128]{1,0:T(8,128)(2,1)S(1)}, bf16[272,128]{1,0:T(8,128)(2,1)S(1)}, u32[]{:S(2)}, u32[]{:S(2)}) collective-permute-start(bf16[272,128]{1,0:T(8,128)(2,1)S(1)} %get-tuple-element.14), channel_id=1, source_target_pairs={{0,16},{2,18},{4,20},{6,22},{8,24},{10,26},{12,28},{14,30},{16,0},... | collective-permute-start | bytes 208904 | tf_op jit(solution)/shard_map/ppermute | solution.py:329
  9.1 7.7 %collective-permute-start.1 = (bf16[544,128]{1,0:T(8,128)(2,1)S(1)}, bf16[544,128]{1,0:T(8,128)(2,1)S(1)}, u32[]{:S(2)}, u32[]{:S(2)}) collective-permute-start(bf16[544,128]{1,0:T(8,128)(2,1)S(1)} %pad_maximum_fusion.1), channel_id=1, source_target_pairs={{0,8},{2,10},{4,12},{6,14},{8,0},{10,2},{12,4},{14,6},{16,24},{18,... | collective-permute-start | bytes 417800 | tf_op jit(solution)/shard_map/ppermute | solution.py:329
  10.7 5.1 %collective-permute-start.5 = (bf16[1,2,2,2,40,128]{5,4,0,3,2,1:T(8,128)(2,1)S(1)}, bf16[1,2,2,2,40,128]{5,4,0,3,2,1:T(8,128)(2,1)S(1)}, u32[]{:S(2)}, u32[]{:S(2)}) collective-permute-start(bf16[1,2,2,2,40,128]{5,4,0,3,2,1:T(8,128)(2,1)S(1)} %get-tuple-element.26), channel_id=1, source_target_pairs={{0,16},{2,18},{4,20},{6,22},{8,24},{10,26},{12,28},{14,30},{16,0},... | collective-permute-start | bytes 245768 | tf_op jit(solution)/shard_map/ppermute | solution.py:330
  15.8 3.4 %collective-permute-start.6 = (bf16[2,1,2,2,40,128]{5,4,0,3,2,1:T(8,128)(2,1)S(1)}, bf16[2,1,2,2,40,128]{5,4,0,3,2,1:T(8,128)(2,1)S(1)}, u32[]{:S(2)}, u32[]{:S(2)}) collective-permute-start(bf16[2,1,2,2,40,128]{5,4,0,3,2,1:T(8,128)(2,1)S(1)} %get-tuple-element.24), channel_id=1, source_target_pairs={{0,8},{2,10},{4,12},{6,14},{8,0},{10,2},{12,4},{14,6},{16,24},{18,... | collective-permute-start | bytes 245768 | tf_op jit(solution)/shard_map/ppermute | solution.py:330
  16.9 5.8 %collective-permute-start.2 = (bf16[1088,128]{1,0:T(8,128)(2,1)S(1)}, bf16[1088,128]{1,0:T(8,128)(2,1)S(1)}, u32[]{:S(2)}, u32[]{:S(2)}) collective-permute-start(bf16[1088,128]{1,0:T(8,128)(2,1)S(1)} %constant_dynamic-update-slice_fusion.after_ref.z_ref), channel_id=1, source_target_pairs={{0,4},{2,6},{4,0},{6,2},{8,12},{10,14},{12,8},{14,10},{16,20},{18,... | collective-permute-start | bytes 835592 | tf_op jit(solution)/shard_map/ppermute | solution.py:333
  19.2 7.8 %collective-permute-start.7 = (bf16[4,2,40,128]{3,2,0,1:T(8,128)(2,1)S(1)}, bf16[4,2,40,128]{3,2,0,1:T(8,128)(2,1)S(1)}, u32[]{:S(2)}, u32[]{:S(2)}) collective-permute-start(bf16[4,2,40,128]{3,2,0,1:T(8,128)(2,1)S(1)} %slice_bitcast_fusion), channel_id=1, source_target_pairs={{0,4},{2,6},{4,0},{6,2},{8,12},{10,14},{12,8},{14,10},{16,20},{18,... | collective-permute-start | bytes 245768 | tf_op jit(solution)/shard_map/ppermute | solution.py:335
  22.7 7.3 %collective-permute-start.3 = (bf16[2176,128]{1,0:T(8,128)(2,1)S(1)}, bf16[2176,128]{1,0:T(8,128)(2,1)S(1)}, u32[]{:S(2)}, u32[]{:S(2)}) collective-permute-start(bf16[2176,128]{1,0:T(8,128)(2,1)S(1)} %pad_maximum_fusion), channel_id=1, source_target_pairs={{0,2},{2,0},{4,6},{6,4},{8,10},{10,8},{12,14},{14,12},{16,18},{18,... | collective-permute-start | bytes 1671176 | tf_op jit(solution)/shard_map/ppermute | solution.py:334
  27.0 2.9 %collective-permute-start.8 = (bf16[8,40,128]{2,1,0:T(8,128)(2,1)S(1)}, bf16[8,40,128]{2,1,0:T(8,128)(2,1)S(1)}, u32[]{:S(2)}, u32[]{:S(2)}) collective-permute-start(bf16[8,40,128]{2,1,0:T(8,128)(2,1)S(1)} %pad_maximum_fusion.3), channel_id=1, source_target_pairs={{0,2},{2,0},{4,6},{6,4},{8,10},{10,8},{12,14},{14,12},{16,18},{18,... | collective-permute-start | bytes 245768 | tf_op jit(solution)/shard_map/ppermute | solution.py:336
  63.2 4.9 %copy-start = (bf16[128,512]{1,0:T(8,128)(2,1)S(1)}, bf16[128,512]{1,0:T(8,128)(2,1)}, u32[]{:S(2)}) copy-start(bf16[128,512]{1,0:T(8,128)(2,1)} %param.24) | copy-start | bytes 393220
  64.3 3.9 %copy-start.1 = (bf16[512,128]{1,0:T(8,128)(2,1)S(1)}, bf16[512,128]{1,0:T(8,128)(2,1)}, u32[]{:S(2)}) copy-start(bf16[512,128]{1,0:T(8,128)(2,1)} %param.25) | copy-start | bytes 393220
  64.3 4.0 %copy-start.2 = (bf16[128,128]{1,0:T(8,128)(2,1)S(1)}, bf16[128,128]{1,0:T(8,128)(2,1)}, u32[]{:S(2)}) copy-start(bf16[128,128]{1,0:T(8,128)(2,1)} %param.23) | copy-start | bytes 98308
  64.3 19.6 %all-to-all-start.1 = ((bf16[32,4,16,128]{3,2,1,0:T(8,128)(2,1)}), bf16[32,4,16,128]{3,2,1,0:T(8,128)(2,1)S(1)}, u32[]{:S(2)}, u32[]{:S(2)}) async-start(bf16[32,4,16,128]{3,2,1,0:T(8,128)(2,1)} %shard_map.130), calls=%async_computation.1 | async-start | bytes 1048576 | tf_op jit(solution)/shard_map/all_to_all | solution.py:376

commit v7 on v6

--- a/solution.py
+++ b/solution.py
@@ -130,7 +130,7 @@
 
 
 def pair_kernel(
-    z_ref, y_ref, c_ref, left_z_ref, left_y_ref, left_c_ref, contact_ref, live_ref, wo_ref, wp_ref,
+    z_ref, y_ref, c_first_ref, c_last_ref, left_z_ref, left_y_ref, left_c_ref, contact_ref, live_ref, wo_ref, wp_ref,
     first_ref, gate_ref, panel_ref,
     o_scr, cnt_scr, pan_scr,
     *, seqs, radix, tile_rows, chans,
@@ -148,8 +148,8 @@
 
     def right(b, t):
         core, pair, k = b // (2 * radix), b // radix % 2, b % radix
-        ref, at = (c_ref, pair * radix + k) if core else (y_ref if pair else z_ref, k)
-        return ref[at * right_rows + t * TILE : at * right_rows + (t + 1) * TILE, :]
+        ref = ((z_ref, y_ref), (c_first_ref, c_last_ref))[core][pair]
+        return ref[k * right_rows + t * TILE : k * right_rows + (t + 1) * TILE, :]
 
     def left(b):
         core, pair, k = b // (2 * radix), b // radix % 2, b % radix
@@ -331,7 +331,8 @@
         half //= 2
     lefts = lefts[:, 0]
     y_got = lax.ppermute(y_msg, "rows", pair_y)
-    c_got = lax.ppermute(jnp.concatenate([y_msg, y_got], 0), "rows", pair_c)
+    c_first = lax.ppermute(y_msg, "rows", pair_c)
+    c_last = lax.ppermute(y_got, "rows", pair_c)
     left_y = lax.ppermute(lefts[:, 1], "rows", pair_y)
     left_c = lax.ppermute(jnp.concatenate([lefts[:, 0, 1], left_y[:, 1]], 0), "rows", pair_c)
 
@@ -351,7 +352,7 @@
         contact_embedding, pairwise_final_matrix, edge_source_matrix, edge_target_matrix,
         edge_final_sigmoid_matrix, presence, y_msg,
     )
-    args = [y_msg, y_got, c_got, lefts, left_y, left_c, contact_t, live, w_o, w_p]
+    args = [y_msg, y_got, c_first, c_last, lefts, left_y, left_c, contact_t, live, w_o, w_p]
     first, gate, panels = call(
         functools.partial(pair_kernel, seqs=seqs, radix=radix, tile_rows=tile_rows, chans=chans),
         (pair, pair, shape((width, 2, tile_rows, cols), BF16)),

time: 86.8 us -> 87.8 us (1.012)
  waiting for transfers between devices: 22.5 us -> 18.5 us
  starting transfers between devices: 21.3 us -> 24.9 us
  local copies, waits for them, and re-layouts: 0.51 us -> 1.91 us
    ppermute x1 -> x2, starting transfers between devices: 4.32 us -> 8.74 us  [the longest x1 5.1 us: on_device(): c_last = lax.ppermute(y_got, 'rows', pair_c)]
    ppermute x1, waiting for transfers between devices: 2.12 us -> 0.47 us  [on_device(): y_got = lax.ppermute(y_msg, 'rows', pair_y)]
    unnamed x11, local copies, waits for them, and re-layouts: 0.37 us -> 1.78 us
    all_to_all x1, waiting for transfers between devices: 15.5 us -> 14.1 us  [on_device(): lax.all_to_all(product, ('rows', 'cols'), split_axis=0, concat_axis=0, ti...]
    ppermute x1, starting transfers between devices: 1.31 us -> 0.29 us  [on_device(): left_y = lax.ppermute(lefts[:, 1], 'rows', pair_y)]
    ppermute x2, waiting for transfers between devices: 3.23 us -> 2.25 us  [on_device(): lax.ppermute(lefts[:, half:], 'rows', pairs)]
  transfers between devices with their start and end apart: 10 -> 11, of which waited for: 5 -> 4; matrix products, arithmetic and copies ran while one was open for 1% -> 1% of each run, Pallas kernels for 2% -> 2%
where the time goes in v7:
time: 87.8 us; the launch traced here: 87.4 us
  blocking collectives  30.5 us (35%)
  starting transfers between devices  24.9 us (28%)
  waiting for transfers between devices  18.5 us (21%)
  Pallas kernels  11.5 us (13%)
  local copies, waits for them, and re-layouts  1.91 us (2%)
    all_to_all x1, blocking collectives, on_device(): lax.all_to_all(panels.reshape(devices, width // devices, 2, tile_rows, co...  30.5 us
    all_to_all x1, waiting for transfers between devices, on_device(): lax.all_to_all(product, ('rows', 'cols'), split_axis=0, concat_axis=0, ti...  14.1 us
    pallas_call x5, Pallas kernels, run(): pl.pallas_call(kernel, out_shape=out_shape, in_specs=[VMEM] * len(args),...  11.5 us
    ppermute x1, starting transfers between devices, on_device(): c_last = lax.ppermute(y_got, 'rows', pair_c)  5.1 us
    ppermute x2, starting transfers between devices, on_device(): lax.ppermute(lefts[:, half:], 'rows', pairs)  3.92 us
    ppermute x2, starting transfers between devices, on_device(): y_msg = jnp.concatenate([y_msg, lax.ppermute(y_msg, 'rows', pairs)], 0)  3.81 us
    all_to_all x1, starting transfers between devices, on_device(): lax.all_to_all(product, ('rows', 'cols'), split_axis=0, concat_axis=0, ti...  3.76 us
    ppermute x1, starting transfers between devices, on_device(): c_first = lax.ppermute(y_msg, 'rows', pair_c)  3.64 us
  transfers between devices with their start and end apart: 11, of which 4 were waited for; matrix products, arithmetic and copies ran while one was open for 1% of the time, Pallas kernels for 2%

profile of v7, /device:TPU:1, one launch (start us, length us, event | category | flops | bytes accessed | tf_op | source)
XLA Modules:
  0.0 87.4 jit_solution(9690786374922411034)
XLA Ops:
  0.0 2.9 %shard_map.127 = (bf16[272,128]{1,0:T(8,128)(2,1)S(1)}, bf16[2,2,2,40,128]{4,3,2,1,0:T(8,128)(2,1)S(1)}) custom-call(f32[8,128,256]{2,1,0:T(8,128)} %fam_ref.1, s32[8,128]{1,0:T(8,128)} %keep_ref.1, s32[2,128]{1,0:T(2,128)} %bitcast.29, bf16[32,256]{1,0:T(8,128)(2,1)} %bitcast.27, bf16[32,256]{1,0:T(8,128)(2,1)} %bitcast.28), custom_call_target="tpu_custom_call" | custom-call | tf_op jit(solution)/shard_map/pallas_call | solution.py:43
  2.9 2.1 %collective-permute-start.5 = (bf16[2,2,2,40,128]{4,3,2,1,0:T(8,128)(2,1)S(1)}, bf16[2,2,2,40,128]{4,3,2,1,0:T(8,128)(2,1)S(1)}, u32[]{:S(2)}, u32[]{:S(2)}) collective-permute-start(bf16[2,2,2,40,128]{4,3,2,1,0:T(8,128)(2,1)S(1)} %get-tuple-element.15), channel_id=1, source_target_pairs={{0,1},{1,0},{2,3},{3,2},{4,5},{5,4},{6,7},{7,6},{8,9},{9,8},{10,11... | collective-permute-start | bytes 245768 | tf_op jit(solution)/shard_map/ppermute | solution.py:322
  5.0 2.3 %collective-permute-start = (bf16[272,128]{1,0:T(8,128)(2,1)S(1)}, bf16[272,128]{1,0:T(8,128)(2,1)S(1)}, u32[]{:S(2)}, u32[]{:S(2)}) collective-permute-start(bf16[272,128]{1,0:T(8,128)(2,1)S(1)} %get-tuple-element.14), channel_id=1, source_target_pairs={{0,16},{2,18},{4,20},{6,22},{8,24},{10,26},{12,28},{14,30},{16,0},... | collective-permute-start | bytes 208904 | tf_op jit(solution)/shard_map/ppermute | solution.py:329
  7.4 1.7 %collective-permute-done = bf16[272,128]{1,0:T(8,128)(2,1)S(1)} collective-permute-done((bf16[272,128]{1,0:T(8,128)(2,1)S(1)}, bf16[272,128]{1,0:T(8,128)(2,1)S(1)}, u32[]{:S(2)}, u32[]{:S(2)}) %collective-permute-start) | collective-permute-done | bytes 69664 | tf_op jit(solution)/shard_map/ppermute | solution.py:329
  9.1 1.5 %collective-permute-start.1 = (bf16[544,128]{1,0:T(8,128)(2,1)S(1)}, bf16[544,128]{1,0:T(8,128)(2,1)S(1)}, u32[]{:S(2)}, u32[]{:S(2)}) collective-permute-start(bf16[544,128]{1,0:T(8,128)(2,1)S(1)} %pad_maximum_fusion), channel_id=1, source_target_pairs={{0,8},{2,10},{4,12},{6,14},{8,0},{10,2},{12,4},{14,6},{16,24},{18,... | collective-permute-start | bytes 417800 | tf_op jit(solution)/shard_map/ppermute | solution.py:329
  10.6 0.0 collective-permute-done.5
  10.7 2.9 %collective-permute-start.6 = (bf16[1,2,2,2,40,128]{5,4,0,3,2,1:T(8,128)(2,1)S(1)}, bf16[1,2,2,2,40,128]{5,4,0,3,2,1:T(8,128)(2,1)S(1)}, u32[]{:S(2)}, u32[]{:S(2)}) collective-permute-start(bf16[1,2,2,2,40,128]{5,4,0,3,2,1:T(8,128)(2,1)S(1)} %get-tuple-element.26), channel_id=1, source_target_pairs={{0,16},{2,18},{4,20},{6,22},{8,24},{10,26},{12,28},{14,30},{16,0},... | collective-permute-start | bytes 245768 | tf_op jit(solution)/shard_map/ppermute | solution.py:330
  13.6 2.2 %collective-permute-done.6 = bf16[1,2,2,2,40,128]{5,4,0,3,2,1:T(8,128)(2,1)S(1)} collective-permute-done((bf16[1,2,2,2,40,128]{5,4,0,3,2,1:T(8,128)(2,1)S(1)}, bf16[1,2,2,2,40,128]{5,4,0,3,2,1:T(8,128)(2,1)S(1)}, u32[]{:S(2)}, u32[]{:S(2)}) %collective-permute-start.6) | collective-permute-done | bytes 81952 | tf_op jit(solution)/shard_map/ppermute | solution.py:330
  15.8 1.0 %collective-permute-start.7 = (bf16[2,1,2,2,40,128]{5,4,0,3,2,1:T(8,128)(2,1)S(1)}, bf16[2,1,2,2,40,128]{5,4,0,3,2,1:T(8,128)(2,1)S(1)}, u32[]{:S(2)}, u32[]{:S(2)}) collective-permute-start(bf16[2,1,2,2,40,128]{5,4,0,3,2,1:T(8,128)(2,1)S(1)} %get-tuple-element.24), channel_id=1, source_target_pairs={{0,8},{2,10},{4,12},{6,14},{8,0},{10,2},{12,4},{14,6},{16,24},{18,... | collective-permute-start | bytes 245768 | tf_op jit(solution)/shard_map/ppermute | solution.py:330
  16.9 0.0 collective-permute-done.1
  16.9 1.3 %collective-permute-start.2 = (bf16[1088,128]{1,0:T(8,128)(2,1)S(1)}, bf16[1088,128]{1,0:T(8,128)(2,1)S(1)}, u32[]{:S(2)}, u32[]{:S(2)}) collective-permute-start(bf16[1088,128]{1,0:T(8,128)(2,1)S(1)} %constant_dynamic-update-slice_fusion.after_ref.z_ref), channel_id=1, source_target_pairs={{0,4},{2,6},{4,0},{6,2},{8,12},{10,14},{12,8},{14,10},{16,20},{18,... | collective-permute-start | bytes 835592 | tf_op jit(solution)/shard_map/ppermute | solution.py:333
  18.2 3.6 %collective-permute-start.3 = (bf16[1088,128]{1,0:T(8,128)(2,1)S(1)}, bf16[1088,128]{1,0:T(8,128)(2,1)S(1)}, u32[]{:S(2)}, u32[]{:S(2)}) collective-permute-start(bf16[1088,128]{1,0:T(8,128)(2,1)S(1)} %constant_dynamic-update-slice_fusion.after_ref.z_ref), channel_id=1, source_target_pairs={{0,2},{2,0},{4,6},{6,4},{8,10},{10,8},{12,14},{14,12},{16,18},{18,... | collective-permute-start | bytes 835592 | tf_op jit(solution)/shard_map/ppermute | solution.py:334
  21.8 0.0 collective-permute-done.7
  21.9 0.3 collective-permute-start.8
  22.2 0.5 collective-permute-done.2.y_ref
  22.6 5.1 %collective-permute-start.4 = (bf16[1088,128]{1,0:T(8,128)(2,1)S(1)}, bf16[1088,128]{1,0:T(8,128)(2,1)S(1)}, u32[]{:S(2)}, u32[]{:S(2)}) collective-permute-start(bf16[1088,128]{1,0:T(8,128)(2,1)S(1)} %collective-permute-done.2.y_ref), channel_id=1, source_target_pairs={{0,2},{2,0},{4,6},{6,4},{8,10},{10,8},{12,14},{14,12},{16,18},{18,... | collective-permute-start | bytes 835592 | tf_op jit(solution)/shard_map/ppermute | solution.py:335
  27.7 0.0 collective-permute-done.8
  27.8 0.9 %collective-permute-start.9 = (bf16[8,40,128]{2,1,0:T(8,128)(2,1)S(1)}, bf16[8,40,128]{2,1,0:T(8,128)(2,1)S(1)}, u32[]{:S(2)}, u32[]{:S(2)}) collective-permute-start(bf16[8,40,128]{2,1,0:T(8,128)(2,1)S(1)} %pad_maximum_fusion.2), channel_id=1, source_target_pairs={{0,2},{2,0},{4,6},{6,4},{8,10},{10,8},{12,14},{14,12},{16,18},{18,... | collective-permute-start | bytes 245768 | tf_op jit(solution)/shard_map/ppermute | solution.py:337
  28.7 2.0 %shard_map.128 = (f32[16,128,128]{2,1,0:T(8,128)S(1)}, bf16[128,1024]{1,0:T(8,128)(2,1)S(1)}, bf16[640,128]{1,0:T(8,128)(2,1)S(1)}, f32[16,128]{1,0:T(8,128)S(1)}) custom-call(f32[16,128,128]{2,1,0:T(8,128)} %contact_ref.1, bf16[1024,128]{1,0:T(8,128)(2,1)} %wo_ref.1, bf16[128,256]{1,0:T(8,128)(2,1)} %src_ref.1, bf16[128,256]{1,0:T(8,128)(2,1)} %tgt_ref.1, ...), custom_call_target="tpu_custom_call" | custom-call | tf_op jit(solution)/shard_map/pallas_call | solution.py:43
  30.8 0.0 collective-permute-done.9.left_c_ref
  30.8 0.0 collective-permute-done.3.c_first_ref
  30.8 0.0 collective-permute-done.4.c_last_ref
  30.8 2.8 %shard_map.129 = (f32[16,128,128]{2,1,0:T(8,128)S(1)}, f32[16,128,128]{2,1,0:T(8,128)S(1)}, bf16[128,2,16,128]{3,2,1,0:T(8,128)(2,1)S(1)}) custom-call(bf16[1088,128]{1,0:T(8,128)(2,1)S(1)} %constant_dynamic-update-slice_fusion.after_ref.z_ref, bf16[1088,128]{1,0:T(8,128)(2,1)S(1)} %collective-permute-done.2.y_ref, ...), custom_call_target="tpu_custom_call" | custom-call | tf_op jit(solution)/shard_map/pallas_call | solution.py:43
  33.6 30.5 %all_to_all.10.recv_ref = bf16[32,4,2,16,128]{4,3,2,1,0:T(8,128)(2,1)S(1)} all-to-all(bf16[32,4,2,16,128]{4,3,2,1,0:T(8,128)(2,1)S(1)} %bitcast.22), channel_id=1, replica_groups=mesh['crops'=1,'rows'=16,'cols'=2] {'rows','cols'}, dimensions={0} | all-to-all | bytes 2097152 | tf_op jit(solution)/shard_map/all_to_all | solution.py:367
  64.1 1.1 %shard_map.130 = bf16[32,4,16,128]{3,2,1,0:T(8,128)(2,1)} custom-call(bf16[32,4,2,16,128]{4,3,2,1,0:T(8,128)(2,1)S(1)} %all_to_all.10.recv_ref), custom_call_target="tpu_custom_call" | custom-call | tf_op jit(solution)/shard_map/pallas_call | solution.py:43
  65.2 0.0 copy-start
  65.2 3.8 %all-to-all-start.1 = ((bf16[32,4,16,128]{3,2,1,0:T(8,128)(2,1)}), bf16[32,4,16,128]{3,2,1,0:T(8,128)(2,1)S(1)}, u32[]{:S(2)}, u32[]{:S(2)}) async-start(bf16[32,4,16,128]{3,2,1,0:T(8,128)(2,1)} %shard_map.130), calls=%async_computation.1 | async-start | bytes 1048576 | tf_op jit(solution)/shard_map/all_to_all | solution.py:377
  69.0 0.0 copy-done
  69.0 0.0 copy-start.1
  69.0 0.1 copy.17
  69.1 0.8 copy-done.1
  69.9 0.0 copy-start.2
  69.9 0.1 copy.18
  70.0 0.6 copy-done.2
  70.6 0.1 copy.16
  70.7 14.1 %all-to-all-done.1 = bf16[32,4,16,128]{3,2,1,0:T(8,128)(2,1)S(1)} async-done(((bf16[32,4,16,128]{3,2,1,0:T(8,128)(2,1)}), bf16[32,4,16,128]{3,2,1,0:T(8,128)(2,1)S(1)}, u32[]{:S(2)}, u32[]{:S(2)}) %all-to-all-start.1) | async-done | bytes 524320 | tf_op jit(solution)/shard_map/all_to_all | solution.py:377
  84.8 2.6 %shard_map.131 = f32[16,128,128]{2,1,0:T(8,128)} custom-call(bf16[128,16,128]{2,1,0:T(8,128)(2,1)S(1)} %bitcast.21, f32[16,128,128]{2,1,0:T(8,128)S(1)} %get-tuple-element.21.first_ref, f32[16,128,128]{2,1,0:T(8,128)S(1)} %get-tuple-element.22.gate_ref, bf16[128,128]{1,0:T(8,128)(2,1)S(1)} %bitcast.25, bf16[512,128]{1,0:T(8,128)(2,1)S(1)} %bitcast.23, ...), custom_call_target="tpu_custom_call" | custom-call | tf_op jit(solution)/shard_map/pallas_call | solution.py:43
  (16 shorter events, 0.2 us)
Async XLA Ops:
  2.9 7.7 %collective-permute-start.5 = (bf16[2,2,2,40,128]{4,3,2,1,0:T(8,128)(2,1)S(1)}, bf16[2,2,2,40,128]{4,3,2,1,0:T(8,128)(2,1)S(1)}, u32[]{:S(2)}, u32[]{:S(2)}) collective-permute-start(bf16[2,2,2,40,128]{4,3,2,1,0:T(8,128)(2,1)S(1)} %get-tuple-element.15), channel_id=1, source_target_pairs={{0,1},{1,0},{2,3},{3,2},{4,5},{5,4},{6,7},{7,6},{8,9},{9,8},{10,11... | collective-permute-start | bytes 245768 | tf_op jit(solution)/shard_map/ppermute | solution.py:322
  5.0 4.1 %collective-permute-start = (bf16[272,128]{1,0:T(8,128)(2,1)S(1)}, bf16[272,128]{1,0:T(8,128)(2,1)S(1)}, u32[]{:S(2)}, u32[]{:S(2)}) collective-permute-start(bf16[272,128]{1,0:T(8,128)(2,1)S(1)} %get-tuple-element.14), channel_id=1, source_target_pairs={{0,16},{2,18},{4,20},{6,22},{8,24},{10,26},{12,28},{14,30},{16,0},... | collective-permute-start | bytes 208904 | tf_op jit(solution)/shard_map/ppermute | solution.py:329
  9.1 7.7 %collective-permute-start.1 = (bf16[544,128]{1,0:T(8,128)(2,1)S(1)}, bf16[544,128]{1,0:T(8,128)(2,1)S(1)}, u32[]{:S(2)}, u32[]{:S(2)}) collective-permute-start(bf16[544,128]{1,0:T(8,128)(2,1)S(1)} %pad_maximum_fusion), channel_id=1, source_target_pairs={{0,8},{2,10},{4,12},{6,14},{8,0},{10,2},{12,4},{14,6},{16,24},{18,... | collective-permute-start | bytes 417800 | tf_op jit(solution)/shard_map/ppermute | solution.py:329
  10.7 5.1 %collective-permute-start.6 = (bf16[1,2,2,2,40,128]{5,4,0,3,2,1:T(8,128)(2,1)S(1)}, bf16[1,2,2,2,40,128]{5,4,0,3,2,1:T(8,128)(2,1)S(1)}, u32[]{:S(2)}, u32[]{:S(2)}) collective-permute-start(bf16[1,2,2,2,40,128]{5,4,0,3,2,1:T(8,128)(2,1)S(1)} %get-tuple-element.26), channel_id=1, source_target_pairs={{0,16},{2,18},{4,20},{6,22},{8,24},{10,26},{12,28},{14,30},{16,0},... | collective-permute-start | bytes 245768 | tf_op jit(solution)/shard_map/ppermute | solution.py:330
  15.8 6.0 %collective-permute-start.7 = (bf16[2,1,2,2,40,128]{5,4,0,3,2,1:T(8,128)(2,1)S(1)}, bf16[2,1,2,2,40,128]{5,4,0,3,2,1:T(8,128)(2,1)S(1)}, u32[]{:S(2)}, u32[]{:S(2)}) collective-permute-start(bf16[2,1,2,2,40,128]{5,4,0,3,2,1:T(8,128)(2,1)S(1)} %get-tuple-element.24), channel_id=1, source_target_pairs={{0,8},{2,10},{4,12},{6,14},{8,0},{10,2},{12,4},{14,6},{16,24},{18,... | collective-permute-start | bytes 245768 | tf_op jit(solution)/shard_map/ppermute | solution.py:330
  16.9 5.8 %collective-permute-start.2 = (bf16[1088,128]{1,0:T(8,128)(2,1)S(1)}, bf16[1088,128]{1,0:T(8,128)(2,1)S(1)}, u32[]{:S(2)}, u32[]{:S(2)}) collective-permute-start(bf16[1088,128]{1,0:T(8,128)(2,1)S(1)} %constant_dynamic-update-slice_fusion.after_ref.z_ref), channel_id=1, source_target_pairs={{0,4},{2,6},{4,0},{6,2},{8,12},{10,14},{12,8},{14,10},{16,20},{18,... | collective-permute-start | bytes 835592 | tf_op jit(solution)/shard_map/ppermute | solution.py:333
  18.2 12.6 %collective-permute-start.3 = (bf16[1088,128]{1,0:T(8,128)(2,1)S(1)}, bf16[1088,128]{1,0:T(8,128)(2,1)S(1)}, u32[]{:S(2)}, u32[]{:S(2)}) collective-permute-start(bf16[1088,128]{1,0:T(8,128)(2,1)S(1)} %constant_dynamic-update-slice_fusion.after_ref.z_ref), channel_id=1, source_target_pairs={{0,2},{2,0},{4,6},{6,4},{8,10},{10,8},{12,14},{14,12},{16,18},{18,... | collective-permute-start | bytes 835592 | tf_op jit(solution)/shard_map/ppermute | solution.py:334
  21.9 5.9 %collective-permute-start.8 = (bf16[4,2,40,128]{3,2,0,1:T(8,128)(2,1)S(1)}, bf16[4,2,40,128]{3,2,0,1:T(8,128)(2,1)S(1)}, u32[]{:S(2)}, u32[]{:S(2)}) collective-permute-start(bf16[4,2,40,128]{3,2,0,1:T(8,128)(2,1)S(1)} %slice_bitcast_fusion), channel_id=1, source_target_pairs={{0,4},{2,6},{4,0},{6,2},{8,12},{10,14},{12,8},{14,10},{16,20},{18,... | collective-permute-start | bytes 245768 | tf_op jit(solution)/shard_map/ppermute | solution.py:336
  22.6 8.2 %collective-permute-start.4 = (bf16[1088,128]{1,0:T(8,128)(2,1)S(1)}, bf16[1088,128]{1,0:T(8,128)(2,1)S(1)}, u32[]{:S(2)}, u32[]{:S(2)}) collective-permute-start(bf16[1088,128]{1,0:T(8,128)(2,1)S(1)} %collective-permute-done.2.y_ref), channel_id=1, source_target_pairs={{0,2},{2,0},{4,6},{6,4},{8,10},{10,8},{12,14},{14,12},{16,18},{18,... | collective-permute-start | bytes 835592 | tf_op jit(solution)/shard_map/ppermute | solution.py:335
  27.8 3.0 %collective-permute-start.9 = (bf16[8,40,128]{2,1,0:T(8,128)(2,1)S(1)}, bf16[8,40,128]{2,1,0:T(8,128)(2,1)S(1)}, u32[]{:S(2)}, u32[]{:S(2)}) collective-permute-start(bf16[8,40,128]{2,1,0:T(8,128)(2,1)S(1)} %pad_maximum_fusion.2), channel_id=1, source_target_pairs={{0,2},{2,0},{4,6},{6,4},{8,10},{10,8},{12,14},{14,12},{16,18},{18,... | collective-permute-start | bytes 245768 | tf_op jit(solution)/shard_map/ppermute | solution.py:337
  65.2 3.8 %copy-start = (bf16[128,512]{1,0:T(8,128)(2,1)S(1)}, bf16[128,512]{1,0:T(8,128)(2,1)}, u32[]{:S(2)}) copy-start(bf16[128,512]{1,0:T(8,128)(2,1)} %param.24) | copy-start | bytes 393220
  65.2 19.6 %all-to-all-start.1 = ((bf16[32,4,16,128]{3,2,1,0:T(8,128)(2,1)}), bf16[32,4,16,128]{3,2,1,0:T(8,128)(2,1)S(1)}, u32[]{:S(2)}, u32[]{:S(2)}) async-start(bf16[32,4,16,128]{3,2,1,0:T(8,128)(2,1)} %shard_map.130), calls=%async_computation.1 | async-start | bytes 1048576 | tf_op jit(solution)/shard_map/all_to_all | solution.py:377
  69.0 0.9 %copy-start.1 = (bf16[512,128]{1,0:T(8,128)(2,1)S(1)}, bf16[512,128]{1,0:T(8,128)(2,1)}, u32[]{:S(2)}) copy-start(bf16[512,128]{1,0:T(8,128)(2,1)} %param.25) | copy-start | bytes 393220
  69.9 0.8 copy-start.2
